TPU v7x, 32 devices: a whole 2x2x4 slice. The times are simulated.
32 devices in a mesh: lat: 8 (over z, y), ch: 4 (over x, core).
Axes of the slice: x: 2, y: 2, z: 4, core: 2. Of those that a mesh axis runs over, the one named last changes fastest.
Arguments:
- state: float32 [1, 24, 180, 768], P(None, 'lat', None, 'ch'), may hold values from -30 to 30
- norm_gains: bfloat16 [2, 768], P(None, 'ch'), may hold values from 0.099609375 to 1.8984375
- channel_biases: bfloat16 [3, 768], P(None, 'ch'), may hold values from -2 to 2
- filter_in: float32 [2, 8, 96, 96], P(None, 'ch'), may hold values from -0.4375 to 0.4375
- filter_in_bias: float32 [2, 8, 96], P(None, 'ch'), may hold values from -2 to 2
- filter_out: float32 [2, 8, 96, 96], P(None, 'ch'), may hold values from -0.4375 to 0.4375
- filter_out_bias: float32 [2, 8, 96], P(None, 'ch'), may hold values from -2 to 2
- up_weight: bfloat16 [768, 3072], P(None, 'ch'), may hold values from -0.21875 to 0.21875
- up_bias: bfloat16 [3072], P('ch'), may hold values from -2 to 2
- down_weight: bfloat16 [3072, 768], P('ch'), may hold values from -0.109375 to 0.109375
Outputs:
- final_state: float32 [1, 24, 180, 768], P(None, 'lat', None, 'ch')
All inputs are finite; a program needn't handle non-finite values.
Results may differ from a plain program's by a relative error of at most 0.0012.
Values may be sent and summed in bfloat16 or wider, within the bound.
No kernel may reach another device: no remote copies, remote signals or barrier semaphores. Data moves between devices by JAX's collectives and lax.ppermute only.
A program may use at most 128 MiB of HBM per device.

v0:
```python
import math

import jax
import jax.numpy as jnp
from jax import lax
from jax.sharding import PartitionSpec as P

D = 768
M = 64
STEPS = 4


EPS = 1e-05
SHRINK = 0.01
HIGH = lax.Precision.HIGHEST


def longitude_tables(width, modes):
    column = jnp.arange(width, dtype=jnp.int32)[:, None]
    order = jnp.arange(modes, dtype=jnp.int32)[None, :]
    angle = 2.0 * math.pi / width * (column * order % width).astype(jnp.float32)
    doubled = jnp.where(order == 0, 1.0, 2.0).astype(jnp.float32)
    return (jnp.cos(angle), jnp.sin(angle), jnp.cos(angle) * doubled, jnp.sin(angle) * doubled)


def latitude_tables(height):
    column = jnp.arange(height, dtype=jnp.int32)[:, None]
    order = jnp.arange(height, dtype=jnp.int32)[None, :]
    angle = 2.0 * math.pi / height * (column * order % height).astype(jnp.float32)
    return (jnp.cos(angle), jnp.sin(angle))


def layer_norm(values, gain, shift):
    mean = jnp.sum(values, -1, keepdims=True) / values.shape[-1]
    spread = jnp.sum(values * values, -1, keepdims=True) / values.shape[-1] - mean * mean
    return (values - mean) * lax.rsqrt(spread + EPS) * gain + shift


def soft_shrink(values):
    return jnp.where(
        values > SHRINK, values - SHRINK, jnp.where(values < -SHRINK, values + SHRINK, 0.0)
    )


def block_apply(left, matrix):
    return jnp.einsum("bkmnj,nji->bkmni", left, matrix, precision=HIGH)


def spectral_mlp(real_part, imag_part, filter_in, filter_in_bias, filter_out, filter_out_bias):
    shape = real_part.shape
    blocks = filter_in.shape[1]
    size = filter_in.shape[2]
    real_blocks = real_part.reshape(shape[:-1] + (blocks, size))
    imag_blocks = imag_part.reshape(shape[:-1] + (blocks, size))
    first_real = jax.nn.relu(
        block_apply(real_blocks, filter_in[0])
        - block_apply(imag_blocks, filter_in[1])
        + filter_in_bias[0]
    )
    first_imag = jax.nn.relu(
        block_apply(imag_blocks, filter_in[0])
        + block_apply(real_blocks, filter_in[1])
        + filter_in_bias[1]
    )
    second_real = (
        block_apply(first_real, filter_out[0])
        - block_apply(first_imag, filter_out[1])
        + filter_out_bias[0]
    )
    second_imag = (
        block_apply(first_imag, filter_out[0])
        + block_apply(first_real, filter_out[1])
        + filter_out_bias[1]
    )
    return (soft_shrink(second_real).reshape(shape), soft_shrink(second_imag).reshape(shape))


def local(
    state,
    norm_gains,
    channel_biases,
    filter_in,
    filter_in_bias,
    filter_out,
    filter_out_bias,
    up_weight,
    up_bias,
    down_weight,
):
    width = state.shape[2]
    height = state.shape[1] * lax.axis_size("lat")
    scale = 1.0 / math.sqrt(height * width)
    lon_cos, lon_sin, back_cos, back_sin = longitude_tables(width, M)
    lat_cos, lat_sin = latitude_tables(height)
    gains = norm_gains.astype(jnp.float32)
    shifts = channel_biases.astype(jnp.float32)
    full_up, full_gains, full_biases = (
        lax.all_gather(up_weight, "ch", axis=1, tiled=True),
        lax.all_gather(norm_gains, "ch", axis=1, tiled=True),
        lax.all_gather(channel_biases, "ch", axis=1, tiled=True),
    )
    full_down, full_up_bias = (
        lax.all_gather(down_weight, "ch", axis=0, tiled=True),
        lax.all_gather(up_bias, "ch", axis=0, tiled=True),
    )
    wide_gains = full_gains.astype(jnp.float32)
    wide_biases = full_biases.astype(jnp.float32)
    wide_up_bias = full_up_bias.astype(jnp.float32)
    values = state
    for step_index in range(STEPS):
        total, squares = lax.psum(
            (jnp.sum(values, -1, keepdims=True), jnp.sum(values * values, -1, keepdims=True)), "ch"
        )
        mean = total / D
        mean, spread = (mean, squares / D - mean * mean)
        normed = (values - mean) * lax.rsqrt(spread + EPS) * gains[0] + shifts[0]
        real_lon = jnp.einsum("bhwd,wm->bhmd", normed, lon_cos, precision=HIGH)
        imag_lon = -jnp.einsum("bhwd,wm->bhmd", normed, lon_sin, precision=HIGH)
        stacked = lax.all_to_all(
            jnp.stack((real_lon, imag_lon)), "lat", split_axis=3, concat_axis=2, tiled=True
        )
        spectral_real_lon = stacked[0]
        spectral_imag_lon = stacked[1]
        real_spec = (
            jnp.einsum("kh,bhmd->bkmd", lat_cos, spectral_real_lon, precision=HIGH)
            + jnp.einsum("kh,bhmd->bkmd", lat_sin, spectral_imag_lon, precision=HIGH)
        ) * scale
        imag_spec = (
            jnp.einsum("kh,bhmd->bkmd", lat_cos, spectral_imag_lon, precision=HIGH)
            - jnp.einsum("kh,bhmd->bkmd", lat_sin, spectral_real_lon, precision=HIGH)
        ) * scale
        out_real, out_imag = spectral_mlp(
            real_spec, imag_spec, filter_in, filter_in_bias, filter_out, filter_out_bias
        )
        real_rows = jnp.einsum("kh,bkmd->bhmd", lat_cos, out_real, precision=HIGH) - jnp.einsum(
            "kh,bkmd->bhmd", lat_sin, out_imag, precision=HIGH
        )
        imag_rows = jnp.einsum("kh,bkmd->bhmd", lat_cos, out_imag, precision=HIGH) + jnp.einsum(
            "kh,bkmd->bhmd", lat_sin, out_real, precision=HIGH
        )
        rows = lax.all_to_all(
            jnp.stack((real_rows, imag_rows)), "lat", split_axis=2, concat_axis=3, tiled=True
        )
        back = jnp.einsum("bhmd,wm->bhwd", rows[0], back_cos, precision=HIGH) - jnp.einsum(
            "bhmd,wm->bhwd", rows[1], back_sin, precision=HIGH
        )
        values = values + back * scale + normed
        owned = lax.all_to_all(values, "ch", split_axis=2, concat_axis=3, tiled=True)
        normed_two = layer_norm(owned, wide_gains[1], wide_biases[1]).astype(jnp.bfloat16)
        flat = normed_two.reshape(-1, normed_two.shape[-1])
        pre = jnp.dot(flat, full_up, preferred_element_type=jnp.float32) + wide_up_bias
        hidden = jax.nn.gelu(pre, approximate=False).astype(jnp.bfloat16)
        mixed = jnp.dot(hidden, full_down, preferred_element_type=jnp.float32) + wide_biases[2]
        values = values + lax.all_to_all(
            mixed.reshape(owned.shape), "ch", split_axis=3, concat_axis=2, tiled=True
        )
    return values


def solution(mesh):
    placed = (
        P(None, "lat", None, "ch"),
        P(None, "ch"),
        P(None, "ch"),
        P(None, "ch", None, None),
        P(None, "ch", None),
        P(None, "ch", None, None),
        P(None, "ch", None),
        P(None, "ch"),
        P("ch"),
        P("ch", None),
    )
    return jax.shard_map(
        local, mesh=mesh, in_specs=placed, out_specs=P(None, "lat", None, "ch"), check_vma=False
    )
```

profile of v0, /device:TPU:0, one launch (start us, length us, event | category | flops | bytes accessed | tf_op | source)
XLA Modules:
  0.0 448.4 jit_solution(3237822838711945097)
XLA Ops:
  10.7 8.5 %all-reduce.3 = (f32[1,3,180,1]{2,1,3,0:T(4,128)S(1)}, f32[1,3,180,1]{2,1,3,0:T(4,128)S(1)}) all-reduce(f32[1,3,180,1]{2,1,3,0:T(4,128)S(1)} %bitcast.885, f32[1,3,180,1]{2,1,3,0:T(4,128)S(1)} %bitcast.884), channel_id=1, replica_groups=mesh['lat'=8,'ch'=4] {'ch'}, use_global_device_ids=true, to_apply=%region_3.4 | all-reduce | flops 1080 | bytes 8640 | tf_op jit(solution)/shard_map/psum | solution.py:111
  22.0 5.8 %all-to-all-start = ((f32[2,1,3,64,192]{4,0,2,1,3:T(2,128)}), f32[2,1,3,64,192]{4,0,2,1,3:T(2,128)S(1)}, u32[]{:S(2)}, u32[]{:S(2)}) async-start(f32[2,1,3,64,192]{4,0,2,1,3:T(2,128)} %copy.567), calls=%async_computation | async-start | bytes 786432 | tf_op jit(solution)/shard_map/all_to_all | solution.py:119
  27.9 10.4 %all-to-all-done = f32[2,1,3,64,192]{4,0,2,1,3:T(2,128)S(1)} async-done(((f32[2,1,3,64,192]{4,0,2,1,3:T(2,128)}), f32[2,1,3,64,192]{4,0,2,1,3:T(2,128)S(1)}, u32[]{:S(2)}, u32[]{:S(2)}) %all-to-all-start) | async-done | bytes 294944 | tf_op jit(solution)/shard_map/all_to_all | solution.py:119
  50.0 5.1 %all-gather = bf16[4,192,2]{1,2,0:T(2,128)(2,1)S(1)} all-gather(bf16[1,192,2]{1,2,0:T(2,128)(2,1)S(1)} %bitcast.892), channel_id=1, replica_groups=mesh['lat'=8,'ch'=4] {'ch'}, dimensions={0}, use_global_device_ids=true | all-gather | bytes 3840 | tf_op jit(solution)/shard_map/all_gather | solution.py:99
  55.2 5.4 %all-gather.1 = bf16[4,192,3]{1,2,0:T(4,128)(2,1)S(1)} all-gather(bf16[1,192,3]{1,2,0:T(4,128)(2,1)S(1)} %bitcast.891), channel_id=1, replica_groups=mesh['lat'=8,'ch'=4] {'ch'}, dimensions={0}, use_global_device_ids=true | all-gather | bytes 5760 | tf_op jit(solution)/shard_map/all_gather | solution.py:100
  67.9 16.5 %all-gather.2 = bf16[4,1,768]{2,1,0:T(2,128)(2,1)S(1)} all-gather(bf16[1,1,768]{2,1,0:T(2,128)(2,1)S(1)} %reshape.758), channel_id=1, replica_groups=mesh['lat'=8,'ch'=4] {'ch'}, dimensions={0}, use_global_device_ids=true | all-gather | bytes 7680 | tf_op jit(solution)/shard_map/all_gather | solution.py:104
  86.8 7.3 %all-gather.8.cloned.1.call-done = bf16[3072,768]{1,0:T(8,128)(2,1)} async-done(((bf16[768,768]{1,0:T(8,128)(2,1)}), bf16[3072,768]{1,0:T(8,128)(2,1)}) %all-gather.8.cloned.1.call-update) | async-done | bytes 4718608 | tf_op jit(solution)/shard_map/all_gather | solution.py:103
  94.1 8.7 %convolution_add_fusion.7 = f32[135,768]{1,0:T(8,128)S(1)} fusion(bf16[3072,768]{1,0:T(8,128)(2,1)} %all-gather.8.cloned.1.call-done, bf16[768,3072]{1,0:T(8,128)(2,1)} %all-gather.6.cloned.1.call-done, f32[3072]{0:T(1024)S(1)} %bitcast.886, f32[135,768]{1,0:T(8,128)S(1)} %all_to_all.201, f32[768]{0:T(1024)S(1)} %get-tuple-element.22, ...), kind=kOutput, calls=%fused_computation.103 | convolution fusion | flops 1302013440 | bytes 10289208 | tf_op jit(solution)/shard_map/dot_general | solution.py:153
  106.0 5.2 %reduce.38 = f32[768,3,45]{2,1,0:T(4,128)S(1)} reduce(f32[768,3,1,45]{3,2,1,0:T(1,128)} %bitcast.817, f32[]{:T(128)} %broadcast.994), dimensions={2}, to_apply=%bitcast.749.reduce_sub_computation | reduce | bytes 829444
  112.8 10.4 %all_to_all.264 = f32[4,1,25920]{2,1,0:T(1,128)S(1)} all-to-all(f32[4,1,25920]{2,1,0:T(1,128)S(1)} %reshape.803), channel_id=1, replica_groups=mesh['lat'=8,'ch'=4] {'ch'}, dimensions={0} | all-to-all | bytes 829440 | tf_op jit(solution)/shard_map/all_to_all | solution.py:154
  128.4 4.9 %bitcast_reduce_fusion.3 = f32[3,45,768]{1,0,2:T(4,128)S(1)} fusion(f32[768,3,1,45]{3,2,1,0:T(1,128)} %reshape.804), kind=kLoop, calls=%fused_computation.1077 | loop fusion | bytes 829440 | tf_op jit(solution)/shard_map/all_to_all | solution.py:154
  135.1 5.9 %all-reduce.2 = (f32[1,3,180,1]{2,1,3,0:T(4,128)S(1)}, f32[1,3,180,1]{2,1,3,0:T(4,128)S(1)}) all-reduce(f32[1,3,180,1]{2,1,3,0:T(4,128)S(1)} %bitcast.879, f32[1,3,180,1]{2,1,3,0:T(4,128)S(1)} %bitcast.878), channel_id=1, replica_groups=mesh['lat'=8,'ch'=4] {'ch'}, use_global_device_ids=true, to_apply=%region_9.10 | all-reduce | flops 1080 | bytes 8640 | tf_op jit(solution)/shard_map/psum | solution.py:111
  143.1 17.5 %all_to_all.265 = f32[2,1,3,64,192]{4,0,2,1,3:T(2,128)S(1)} all-to-all(f32[2,1,3,64,192]{4,0,2,1,3:T(2,128)S(1)} %copy.603), channel_id=1, replica_groups=mesh['lat'=8,'ch'=4] {'lat'}, dimensions={3} | all-to-all | bytes 589824 | tf_op jit(solution)/shard_map/all_to_all | solution.py:119
  167.8 14.9 %all_to_all.266 = f32[2,1,24,8,192]{4,3,1,0,2:T(8,128)S(1)} all-to-all(f32[2,1,24,8,192]{4,3,1,0,2:T(8,128)S(1)} %copy.625), channel_id=1, replica_groups=mesh['lat'=8,'ch'=4] {'lat'}, dimensions={2} | all-to-all | bytes 589824 | tf_op jit(solution)/shard_map/all_to_all | solution.py:141
  185.3 11.7 %all_to_all.267 = f32[1,3,180,192]{3,0,1,2:T(1,128)S(1)} all-to-all(f32[1,3,180,192]{3,0,1,2:T(1,128)S(1)} %copy.629), channel_id=1, replica_groups=mesh['lat'=8,'ch'=4] {'ch'}, dimensions={2} | all-to-all | bytes 829440 | tf_op jit(solution)/shard_map/all_to_all | solution.py:148
  199.2 8.7 %convolution_add_fusion.6 = f32[135,768]{1,0:T(8,128)S(1)} fusion(bf16[3072,768]{1,0:T(8,128)(2,1)} %all-gather.8.cloned.1.call-done, bf16[768,3072]{1,0:T(8,128)(2,1)} %all-gather.6.cloned.1.call-done, f32[3072]{0:T(1024)S(1)} %bitcast.887, f32[135,768]{1,0:T(8,128)S(1)} %all_to_all.215, f32[135]{0:T(256)S(1)} %add_rsqrt_fusion.2, f32[135]{0:T(256)S(1)} %div.73, ...), kind=kOutput, calls=%fused_computation.102 | convolution fusion | flops 1302013440 | bytes 10289208 | tf_op jit(solution)/shard_map/dot_general | solution.py:153
  210.6 5.2 %reduce.40 = f32[768,3,45]{2,1,0:T(4,128)S(1)} reduce(f32[768,3,1,45]{3,2,1,0:T(1,128)} %bitcast.818, f32[]{:T(128)} %broadcast.994), dimensions={2}, to_apply=%bitcast.751.reduce_sub_computation | reduce | bytes 829444
  217.5 10.4 %all_to_all.268 = f32[4,1,25920]{2,1,0:T(1,128)S(1)} all-to-all(f32[4,1,25920]{2,1,0:T(1,128)S(1)} %reshape.805), channel_id=1, replica_groups=mesh['lat'=8,'ch'=4] {'ch'}, dimensions={0} | all-to-all | bytes 829440 | tf_op jit(solution)/shard_map/all_to_all | solution.py:154
  233.0 4.9 %bitcast_reduce_fusion.2 = f32[3,45,768]{1,0,2:T(4,128)S(1)} fusion(f32[768,3,1,45]{3,2,1,0:T(1,128)} %reshape.806), kind=kLoop, calls=%fused_computation.1076 | loop fusion | bytes 829440 | tf_op jit(solution)/shard_map/all_to_all | solution.py:154
  239.8 5.9 %all-reduce.1 = (f32[1,3,180,1]{2,1,3,0:T(4,128)S(1)}, f32[1,3,180,1]{2,1,3,0:T(4,128)S(1)}) all-reduce(f32[1,3,180,1]{2,1,3,0:T(4,128)S(1)} %bitcast.881, f32[1,3,180,1]{2,1,3,0:T(4,128)S(1)} %bitcast.880), channel_id=1, replica_groups=mesh['lat'=8,'ch'=4] {'ch'}, use_global_device_ids=true, to_apply=%region_15.16 | all-reduce | flops 1080 | bytes 8640 | tf_op jit(solution)/shard_map/psum | solution.py:111
  247.7 15.2 %all_to_all.269 = f32[2,1,3,64,192]{4,0,2,1,3:T(2,128)S(1)} all-to-all(f32[2,1,3,64,192]{4,0,2,1,3:T(2,128)S(1)} %copy.636), channel_id=1, replica_groups=mesh['lat'=8,'ch'=4] {'lat'}, dimensions={3} | all-to-all | bytes 589824 | tf_op jit(solution)/shard_map/all_to_all | solution.py:119
  270.1 14.9 %all_to_all.270 = f32[2,1,24,8,192]{4,3,1,0,2:T(8,128)S(1)} all-to-all(f32[2,1,24,8,192]{4,3,1,0,2:T(8,128)S(1)} %copy.658), channel_id=1, replica_groups=mesh['lat'=8,'ch'=4] {'lat'}, dimensions={2} | all-to-all | bytes 589824 | tf_op jit(solution)/shard_map/all_to_all | solution.py:141
  287.6 11.7 %all_to_all.271 = f32[1,3,180,192]{3,0,1,2:T(1,128)S(1)} all-to-all(f32[1,3,180,192]{3,0,1,2:T(1,128)S(1)} %copy.662), channel_id=1, replica_groups=mesh['lat'=8,'ch'=4] {'ch'}, dimensions={2} | all-to-all | bytes 829440 | tf_op jit(solution)/shard_map/all_to_all | solution.py:148
  301.6 8.7 %convolution_add_fusion.5 = f32[135,768]{1,0:T(8,128)S(1)} fusion(bf16[3072,768]{1,0:T(8,128)(2,1)} %all-gather.8.cloned.1.call-done, bf16[768,3072]{1,0:T(8,128)(2,1)} %all-gather.6.cloned.1.call-done, f32[3072]{0:T(1024)S(1)} %bitcast.888, f32[135,768]{1,0:T(8,128)S(1)} %all_to_all.229, f32[135]{0:T(256)S(1)} %add_rsqrt_fusion.1, f32[135]{0:T(256)S(1)} %div.79, ...), kind=kOutput, calls=%fused_computation.101 | convolution fusion | flops 1302013440 | bytes 10289208 | tf_op jit(solution)/shard_map/dot_general | solution.py:153
  313.0 5.2 %reduce.42 = f32[768,3,45]{2,1,0:T(4,128)S(1)} reduce(f32[768,3,1,45]{3,2,1,0:T(1,128)} %bitcast.819, f32[]{:T(128)} %broadcast.994), dimensions={2}, to_apply=%bitcast.753.reduce_sub_computation | reduce | bytes 829444
  319.8 10.4 %all_to_all.272 = f32[4,1,25920]{2,1,0:T(1,128)S(1)} all-to-all(f32[4,1,25920]{2,1,0:T(1,128)S(1)} %reshape.807), channel_id=1, replica_groups=mesh['lat'=8,'ch'=4] {'ch'}, dimensions={0} | all-to-all | bytes 829440 | tf_op jit(solution)/shard_map/all_to_all | solution.py:154
  342.1 5.9 %all-reduce = (f32[1,3,180,1]{2,1,3,0:T(4,128)S(1)}, f32[1,3,180,1]{2,1,3,0:T(4,128)S(1)}) all-reduce(f32[1,3,180,1]{2,1,3,0:T(4,128)S(1)} %bitcast.883, f32[1,3,180,1]{2,1,3,0:T(4,128)S(1)} %bitcast.882), channel_id=1, replica_groups=mesh['lat'=8,'ch'=4] {'ch'}, use_global_device_ids=true, to_apply=%region_21.22 | all-reduce | flops 1080 | bytes 8640 | tf_op jit(solution)/shard_map/psum | solution.py:111
  350.0 15.2 %all_to_all.273 = f32[2,1,3,64,192]{4,0,2,1,3:T(2,128)S(1)} all-to-all(f32[2,1,3,64,192]{4,0,2,1,3:T(2,128)S(1)} %copy.669), channel_id=1, replica_groups=mesh['lat'=8,'ch'=4] {'lat'}, dimensions={3} | all-to-all | bytes 589824 | tf_op jit(solution)/shard_map/all_to_all | solution.py:119
  372.5 14.9 %all_to_all.274 = f32[2,1,24,8,192]{4,3,1,0,2:T(8,128)S(1)} all-to-all(f32[2,1,24,8,192]{4,3,1,0,2:T(8,128)S(1)} %copy.691), channel_id=1, replica_groups=mesh['lat'=8,'ch'=4] {'lat'}, dimensions={2} | all-to-all | bytes 589824 | tf_op jit(solution)/shard_map/all_to_all | solution.py:141
  390.0 11.7 %all_to_all.275 = f32[1,3,180,192]{3,0,1,2:T(1,128)S(1)} all-to-all(f32[1,3,180,192]{3,0,1,2:T(1,128)S(1)} %copy.695), channel_id=1, replica_groups=mesh['lat'=8,'ch'=4] {'ch'}, dimensions={2} | all-to-all | bytes 829440 | tf_op jit(solution)/shard_map/all_to_all | solution.py:148
  404.0 8.7 %convolution_add_fusion.4 = f32[135,768]{1,0:T(8,128)S(1)} fusion(bf16[3072,768]{1,0:T(8,128)(2,1)} %all-gather.8.cloned.1.call-done, bf16[768,3072]{1,0:T(8,128)(2,1)} %all-gather.6.cloned.1.call-done, f32[3072]{0:T(1024)S(1)} %bitcast.889, f32[135,768]{1,0:T(8,128)S(1)} %all_to_all.243, f32[135]{0:T(256)S(1)} %add_rsqrt_fusion, f32[135]{0:T(256)S(1)} %div.85, ...), kind=kOutput, calls=%fused_computation.100 | convolution fusion | flops 1302013440 | bytes 10289208 | tf_op jit(solution)/shard_map/dot_general | solution.py:153
  420.3 10.0 %all_to_all.276 = f32[4,1,25920]{2,1,0:T(1,128)S(1)} all-to-all(f32[4,1,25920]{2,1,0:T(1,128)S(1)} %reshape.809), channel_id=1, replica_groups=mesh['lat'=8,'ch'=4] {'ch'}, dimensions={0} | all-to-all | bytes 829440 | tf_op jit(solution)/shard_map/all_to_all | solution.py:154
  (263 shorter events, 127.3 us)
Async XLA Ops:
  6.5 1.5 copy-start.3
  6.5 1.5 copy-start.2
  6.5 12.7 %copy-start.4 = (bf16[2,192]{1,0:T(2,128)(2,1)S(1)}, bf16[2,192]{1,0:T(2,128)(2,1)}, u32[]{:S(2)}) copy-start(bf16[2,192]{1,0:T(2,128)(2,1)} %param.11) | copy-start | bytes 2308
  6.5 80.3 %all-gather.6.cloned.1.call-start = ((), (), s32[]{:S(2)}) async-start(), calls=%async_computation.16 | async-start | bytes 5898240 | tf_op jit(solution)/shard_map/all_gather | solution.py:98
  7.3 86.8 %all-gather.8.cloned.1.call-start = ((), (), s32[]{:S(2)}) async-start(), calls=%async_computation.17 | async-start | bytes 5898240 | tf_op jit(solution)/shard_map/all_gather | solution.py:103
  20.1 7.8 %copy-start.5 = (f32[2,2,96]{2,1,0:T(2,128)S(1)}, f32[2,2,96]{2,1,0:T(2,128)}, u32[]{:S(2)}) copy-start(f32[2,2,96]{2,1,0:T(2,128)} %param.14) | copy-start | bytes 4612
  20.1 7.8 %copy-start.6 = (f32[2,2,96]{2,1,0:T(2,128)S(1)}, f32[2,2,96]{2,1,0:T(2,128)}, u32[]{:S(2)}) copy-start(f32[2,2,96]{2,1,0:T(2,128)} %param.16) | copy-start | bytes 4612
  22.0 16.2 %all-to-all-start = ((f32[2,1,3,64,192]{4,0,2,1,3:T(2,128)}), f32[2,1,3,64,192]{4,0,2,1,3:T(2,128)S(1)}, u32[]{:S(2)}, u32[]{:S(2)}) async-start(f32[2,1,3,64,192]{4,0,2,1,3:T(2,128)} %copy.567), calls=%async_computation | async-start | bytes 786432 | tf_op jit(solution)/shard_map/all_to_all | solution.py:119
  38.4 2.2 copy-start
  39.9 1.9 copy-start.1
  44.7 5.4 %copy-start.7 = (bf16[768]{0:T(1024)(128)(2,1)S(1)}, bf16[768]{0:T(1024)(128)(2,1)}, u32[]{:S(2)}) copy-start(bf16[768]{0:T(1024)(128)(2,1)} %param.18) | copy-start | bytes 4612
  46.3 14.6 %all-to-all-start.1 = ((f32[2,1,24,8,192]{4,3,1,0,2:T(8,128)}), f32[2,1,24,8,192]{4,3,1,0,2:T(8,128)S(1)}, u32[]{:S(2)}, u32[]{:S(2)}) async-start(f32[2,1,24,8,192]{4,3,1,0,2:T(8,128)} %copy.589), calls=%async_computation.1 | async-start | bytes 786432 | tf_op jit(solution)/shard_map/all_to_all | solution.py:141
  64.3 20.1 %all-to-all-start.2 = ((f32[1,3,180,192]{3,0,1,2:T(1,128)}), f32[1,3,180,192]{3,0,1,2:T(1,128)S(1)}, u32[]{:S(2)}, u32[]{:S(2)}) async-start(f32[1,3,180,192]{3,0,1,2:T(1,128)} %copy.594), calls=%async_computation.2 | async-start | bytes 1105920 | tf_op jit(solution)/shard_map/all_to_all | solution.py:148
Sparse Core Ops, SparseCore 0:
  8.9 40.1 all-gather.5
  50.6 43.4 all-gather.7
where the time goes:
time: 457 us; the launch traced here: 448 us
  blocking collectives  222 us (49%)
  matrix products  72.4 us (16%)
  local copies, waits for them, and re-layouts  69.2 us (15%)
  other arithmetic  36.9 us (8%)
  waiting for transfers between devices  19.4 us (4%)
  between operations  15.4 us (3%)
  starting transfers between devices  13 us (3%)
    all_to_all x3, blocking collectives, local(): lax.all_to_all(jnp.stack((real_lon, imag_lon)), 'lat', split_axis=3, conc...  47.8 us
    all_to_all x3, blocking collectives, local(): lax.all_to_all(jnp.stack((real_rows, imag_rows)), 'lat', split_axis=2, co...  44.7 us
    all_to_all x4, blocking collectives, local(): lax.all_to_all(mixed.reshape(owned.shape), 'ch', split_axis=3, concat_axi...  41.2 us
    all_to_all x3, blocking collectives, local(): lax.all_to_all(values, 'ch', split_axis=2, concat_axis=3, tiled=True)  35.1 us
    dot_general x4, matrix products, local(): jnp.dot(hidden, full_down, preferred_element_type=jnp.float32)  34.7 us
    psum x4, blocking collectives, local(): lax.psum((jnp.sum(values, -1, keepdims=True), jnp.sum(values * values, -1...  26.2 us
    all_to_all x12, local copies, waits for them, and re-layouts, local(): lax.all_to_all(mixed.reshape(owned.shape), 'ch', split_axis=3, concat_axi...  24.4 us
    unnamed x4, other arithmetic  20.4 us
  transfers between devices with their start and end apart: 5, of which 3 were waited for; matrix products, arithmetic and copies ran while one was open for 4% of the time, Pallas kernels for 0%

commit v1 on v0

v1 whole, which is shorter than its diff:
```python
import math

import jax
import jax.numpy as jnp
import numpy as np
from jax import lax
from jax.experimental import pallas as pl
from jax.experimental.pallas import tpu as pltpu
from jax.sharding import PartitionSpec as P


D = 768
M = 64
STEPS = 4
EPS = 1e-05
SHRINK = 0.01
HALF = 64
LANES = 128
BF = jnp.bfloat16
F32 = jnp.float32


class Plan:
    def __init__(self, lat, ch, rows, width):
        self.lat, self.ch, self.rows, self.width = lat, ch, rows, width
        self.height = rows * lat
        self.short = width // ch
        self.padded = -(-self.short // 16) * 16
        self.tokens = rows * self.padded
        self.classes = self.short // 2 + 1
        self.per = -(-self.classes // lat)
        self.wide = D // ch
        self.units = self.wide // HALF
        self.items = rows * self.per
        spare = self.items % 8
        if self.items > 8 and spare and spare * self.units <= 8:
            self.main, self.left = self.items - spare, spare
        else:
            self.main, self.left = -(-self.items // 8) * 8, 0
        self.message = self.units * self.main + (8 if self.left else 0)
        slots = 0
        while (slots // 2) * self.short + (slots % 2) * (self.short - self.short // 2) < M:
            slots += 1
        self.slots = slots
        self.modes = self.per * slots * self.height
        self.peers = lat * ch
        self.spare = self.padded - self.short
        self.packed = self.tokens + self.tokens // 2
        hj = np.arange(self.main)
        self.item_h = np.where(hj < self.items, hj // self.per, 0)
        self.item_j = np.where(hj < self.items, hj % self.per, -1)
        tail = self.main + np.arange(self.left)
        self.tail_h, self.tail_j = tail // self.per, tail % self.per


def split_np(table):
    hi = table.astype(np.float32).astype(BF)
    lo = (table - hi.astype(np.float64)).astype(np.float32).astype(BF)
    return hi, lo


def short_tables(plan):
    g = np.arange(plan.lat)
    item_g = np.concatenate([np.repeat(g, plan.main), np.repeat(g, plan.left)])
    item_h = np.concatenate([np.tile(plan.item_h, plan.lat), np.tile(plan.tail_h, plan.lat)])
    item_j = np.concatenate([np.tile(plan.item_j, plan.lat), np.tile(plan.tail_j, plan.lat)])
    order = item_g * plan.per + item_j
    good = (item_j >= 0) & (order < plan.classes)
    tok_h = np.repeat(np.arange(plan.rows), plan.padded)
    tok_a = np.tile(np.arange(plan.padded), plan.rows)
    mask = good[:, None] & (item_h[:, None] == tok_h[None]) & (tok_a[None] < plan.short)
    angle = 2 * np.pi / plan.short * (order[:, None] * tok_a[None] % plan.short)
    cos, sin = np.cos(angle) * mask, np.sin(angle) * mask
    forward = np.concatenate([cos, -sin], 0)
    inverse = np.concatenate([cos.T, -sin.T], 1)
    return np.stack(split_np(forward)), np.stack(split_np(inverse))


def mode_places(plan):
    j, t, k = (
        v.reshape(-1)
        for v in np.meshgrid(
            np.arange(plan.per), np.arange(plan.slots), np.arange(plan.height), indexing="ij"
        )
    )
    peer = np.arange(plan.peers)
    col_p = np.concatenate([np.repeat(peer, plan.main), np.repeat(peer, plan.left)])
    col_h = np.concatenate([np.tile(plan.item_h, plan.peers), np.tile(plan.tail_h, plan.peers)])
    col_j = np.concatenate([np.tile(plan.item_j, plan.peers), np.tile(plan.tail_j, plan.peers)])
    col_h = (col_p // plan.ch) * plan.rows + col_h
    none = np.zeros_like(j)
    row = np.stack([j, t % 2, (t + 1) // 2, k] + [none] * 4).astype(np.float32)
    none = np.zeros_like(col_p)
    col = np.stack([col_p % plan.ch, col_h, col_j] + [none] * 5).astype(np.float32)
    return row, col


def cos_sin(turns):
    turns = turns - jnp.floor(turns + 0.5)
    quarter = jnp.floor(turns * 4.0 + 0.5)
    x = (turns - quarter * 0.25) * (2.0 * math.pi)
    y = x * x
    sin = x * (1 + y * (-1 / 6 + y * (1 / 120 + y * (-1 / 5040 + y * (1 / 362880)))))
    cos = 1 + y * (-0.5 + y * (1 / 24 + y * (-1 / 720 + y * (1 / 40320 - y * (1 / 3628800)))))
    odd = jnp.abs(quarter) == 1.0
    c, s = jnp.where(odd, sin, cos), jnp.where(odd, cos, sin)
    c = jnp.where((quarter == 1.0) | (jnp.abs(quarter) == 2.0), -c, c)
    s = jnp.where((quarter == -1.0) | (jnp.abs(quarter) == 2.0), -s, s)
    return c, s


def mode_table(plan, first_class, row, col):
    j, odd, times, k = row
    q, h, col_j = col
    order = first_class + j
    mode = times * plan.short + jnp.where(odd == 1.0, -order, order)
    fine = (mode < M) & (order < plan.classes)
    fine = fine & ((order > 0.0) | (times == 0.0) | (odd == 1.0))
    fine = fine & ((2.0 * order != plan.short) | (odd == 0.0))
    scale = 1.0 / math.sqrt(plan.height * plan.width)
    weight = jnp.where(fine, scale, 0.0)
    doubled = jnp.where(mode == 0.0, 1.0, 2.0)
    turn = jnp.where(odd == 1.0, 1.0, -1.0)
    product = k * h
    product = product - plan.height * jnp.floor(product * (1.0 / plan.height) + 1e-4)
    cos, sin = cos_sin(mode * q * (1.0 / plan.width) + product * (1.0 / plan.height))
    keep = jnp.where(j == col_j, weight, 0.0)
    return cos * keep, sin * (keep * turn), doubled


def split(value):
    hi = value.astype(BF)
    return hi, (value - hi.astype(F32)).astype(BF)


def dot(a, b):
    return jnp.dot(a, b, preferred_element_type=F32)


def low_lanes(shape):
    return lax.broadcasted_iota(jnp.int32, shape, len(shape) - 1) % LANES < HALF


def swap(value):
    return pltpu.roll(value, HALF, 1)


def norm(values, gain, shift):
    mean = jnp.sum(values, -1, keepdims=True) * (1.0 / D)
    spread = jnp.sum(values * values, -1, keepdims=True) * (1.0 / D) - mean * mean
    return (values - mean) * lax.rsqrt(spread + EPS) * gain + shift


def emit_wire(plan, normed, fhi, flo, wire_ref, scratch):
    hi, lo = split(normed)
    spec = dot(fhi[...], hi) + dot(flo[...], hi) + dot(fhi[...], lo)
    count = plan.lat * plan.main
    extra = plan.lat * plan.left
    half = count + extra
    low = low_lanes((half, LANES))
    for tile in range(D // LANES):
        lanes = slice(tile * LANES, (tile + 1) * LANES)
        re, im = spec[:half, lanes], spec[half:, lanes]
        pair = (jnp.where(low, re, swap(im)), jnp.where(low, swap(re), im))
        for which in range(2):
            c, u = divmod(2 * tile + which, plan.units)
            part = pair[which]
            scratch[:, c, u * plan.main : (u + 1) * plan.main, :] = part[:count].reshape(
                plan.lat, plan.main, LANES
            )
            for spot in range(plan.left):
                row = plan.units * plan.main + u * plan.left + spot
                for g in range(plan.lat):
                    at = count + g * plan.left + spot
                    scratch[g, c, row : row + 1, :] = part[at : at + 1]
    if plan.left:
        first = plan.units * (plan.main + plan.left)
        if first < plan.message:
            scratch[:, :, first:, :] = jnp.zeros(
                (plan.lat, plan.ch, plan.message - first, LANES), F32
            )
    wire_ref[...] = scratch[...].reshape(plan.peers, plan.message, LANES).astype(BF)


def read_wire(plan, wire_ref, ghi, glo, scratch):
    scratch[...] = wire_ref[...].astype(F32).reshape(plan.lat, plan.ch, plan.message, LANES)
    count = plan.lat * plan.main
    half = count + plan.lat * plan.left
    low = low_lanes((half, LANES))

    def unit(index):
        c, u = divmod(index, plan.units)
        parts = [scratch[:, c, u * plan.main : (u + 1) * plan.main, :].reshape(count, LANES)]
        for g in range(plan.lat):
            for spot in range(plan.left):
                row = plan.units * plan.main + u * plan.left + spot
                parts.append(scratch[g, c, row : row + 1, :])
        return jnp.concatenate(parts, 0) if len(parts) > 1 else parts[0]

    tiles = []
    for tile in range(D // LANES):
        a, b = unit(2 * tile), unit(2 * tile + 1)
        re = jnp.where(low, a, swap(b))
        im = jnp.where(low, swap(a), b)
        tiles.append(jnp.concatenate([re, im], 0).astype(BF))
    right = jnp.concatenate(tiles, 1)
    return dot(ghi[...], right) + dot(glo[...], right)


def pack(values):
    half = values.shape[0] // 2
    tail = values[:, LANES:]
    return jnp.concatenate([values[:, :LANES], jnp.concatenate([tail[:half], tail[half:]], 1)], 0)


def unpack(message):
    tokens = message.shape[0] // 3 * 2
    tail = message[tokens:]
    tail = jnp.concatenate([tail[:, :HALF], tail[:, HALF:]], 0)
    return jnp.concatenate([message[:tokens], tail], 1)


def pack_kernel(plan, state_ref, gain_hbm, bias_hbm, up_hbm, out_ref, scratch, body, tail, *refs):
    gain_ref, bias_ref, up_ref, sem = refs
    copies = fetch([gain_hbm, bias_hbm, up_hbm], [gain_ref, bias_ref, up_ref], sem)
    body[...] = state_ref[:, :, :LANES]
    tail[:, :, :HALF] = state_ref[:, :, LANES:]
    for copy in copies:
        copy.wait()
    line = up_ref[...].astype(F32)
    small = [gain_ref[...].astype(F32), bias_ref[...].astype(F32)]
    small += [line[:, n * plan.wide : (n + 1) * plan.wide] for n in range(plan.ch)]
    small = jnp.concatenate(small, 0)
    count = small.shape[0]
    scratch[...] = jnp.zeros(scratch.shape, F32)
    for n in range(count):
        h, s = divmod(n, plan.spare)
        at = h * plan.padded + plan.short + s
        scratch[at : at + 1, :] = small[n : n + 1]
    for q in range(plan.ch):
        for h in range(plan.rows):
            at = h * plan.padded
            every = pl.ds(q, plan.short, stride=plan.ch)
            scratch[at : at + plan.short, :LANES] = body[h, every, :]
            scratch[at : at + plan.short, LANES:] = tail[h, every, :][:, :HALF]
        out_ref[q] = pack(scratch[...])


def unpack_kernel(plan, got_ref, out_ref, body, tail):
    for q in range(plan.ch):
        values = unpack(got_ref[q])
        wide = jnp.concatenate([values[:, LANES:], values[:, LANES:]], 1)
        for h in range(plan.rows):
            at = slice(h * plan.padded, h * plan.padded + plan.short)
            every = pl.ds(q, plan.short, stride=plan.ch)
            body[h, every, :] = values[at, :LANES]
            tail[h, every, :] = wide[at]
    out_ref[:, :, :LANES] = body[...]
    out_ref[:, :, LANES:] = tail[:, :, :HALF]


def fetch(sources, targets, sem):
    copies = [pltpu.make_async_copy(a, b, sem.at[n]) for n, (a, b) in enumerate(zip(sources, targets))]
    for copy in copies:
        copy.start()
    return copies


def parts_kernel(me_ref, up_ref, down_ref, up_out, near_out, rest_out, *refs):
    mids, sem = refs[:3], refs[3]
    half, third = up_out.shape[1], near_out.shape[0]
    at = pl.multiple_of(me_ref[2] * half, LANES)
    to = pl.multiple_of(me_ref[2] * third, LANES)
    into = fetch(
        [up_ref.at[:, pl.ds(at, half)], down_ref.at[pl.ds(to, third), :], down_ref.at[2 * third :, :]],
        mids,
        sem,
    )
    away = []
    for n, out in enumerate((up_out, near_out, rest_out)):
        into[n].wait()
        away.append(pltpu.make_async_copy(mids[n], out, sem.at[3 + n]))
        away[n].start()
    for copy in away:
        copy.wait()


def prep_kernel(plan, me_ref, rowv, colv, rowt, colt, fin, finb, fout, foutb, *refs):
    count = len(refs) // 2
    outs, (chi, clo, ehi, elo, w1h, w1l, w2h, w2l, b1, b2) = refs[:count], refs[count:-1]
    sem = refs[-1]
    copies = [pltpu.make_async_copy(a, b, sem.at[n]) for n, (a, b) in enumerate(zip(refs[count:], outs))]
    first = (me_ref[0] * plan.per).astype(F32)
    size = plan.modes
    wide = plan.peers * (plan.main + plan.left)
    rows = [rowv[:, n : n + 1] for n in range(4)]
    cols = [colv[n : n + 1, :] for n in range(3)]
    cos, sin, _ = mode_table(plan, first, rows, cols)
    chi[:, :wide], clo[:, :wide] = split(cos)
    chi[:, wide:], clo[:, wide:] = split(sin)
    copies[0].start()
    copies[1].start()
    rows = [rowt[n : n + 1, :] for n in range(4)]
    cols = [colt[:, n : n + 1] for n in range(3)]
    cos, sin, doubled = mode_table(plan, first, rows, cols)
    ehi[:, :size], elo[:, :size] = split(cos * doubled)
    ehi[:, size:], elo[:, size:] = split(-sin * doubled)
    copies[2].start()
    copies[3].start()
    for weights, bias, high, low, out in ((fin, finb, w1h, w1l, b1), (fout, foutb, w2h, w2l, b2)):
        blocks, channels = weights.shape[1], weights.shape[2]
        full = []
        for p in range(2):
            lines = []
            for n in range(blocks):
                cells = [jnp.zeros((channels, channels), F32)] * blocks
                cells[n] = weights[p, n]
                lines.append(jnp.concatenate(cells, 1))
            full.append(jnp.concatenate(lines, 0))
        for u in range(plan.units):
            at = slice(u * HALF, (u + 1) * HALF)
            real, imag = full[0][at], full[1][at]
            for p, (left, right) in enumerate(((real, imag), (-imag, real))):
                cells = []
                for v in range(plan.units):
                    cells += [left[:, v * HALF : (v + 1) * HALF], right[:, v * HALF : (v + 1) * HALF]]
                row = jnp.concatenate(cells, 1)
                to = slice((2 * u + p) * HALF, (2 * u + p + 1) * HALF)
                high[to, :], low[to, :] = split(row)
        lines = [jnp.concatenate([bias[p, n : n + 1] for n in range(blocks)], 1) for p in range(2)]
        cells = []
        for v in range(plan.units):
            cells += [line[:, v * HALF : (v + 1) * HALF] for line in lines]
        out[...] = jnp.concatenate(cells, 1)
    for copy in copies[4:]:
        copy.start()
    for copy in copies:
        copy.wait()


def start_kernel(plan, me_ref, got_ref, tab_hbm, sum_hbm, wire_ref, par_hbm, *refs):
    scratch, tab, sum_ref, par_ref, sem = refs
    bias_ref = par_ref.at[8:16]
    copies = fetch([tab_hbm], [tab], sem)
    got = [unpack(got_ref[c]) for c in range(plan.ch)]
    full = jnp.concatenate(got, 1)
    rows = []
    for h in range(plan.rows):
        for s in range(plan.spare):
            rows.append(h * plan.padded + plan.short + s)
    for n in range(5):
        par_ref[n : n + 1, :] = full[rows[n] : rows[n] + 1, :]
    par_ref[5:8, :] = jnp.zeros((3, D), F32)
    bias_ref[...] = jnp.zeros(bias_ref.shape, F32)
    for s in range(plan.ch):
        source = unpack(got_ref[me_ref[1] ^ s])
        parts = [source[rows[5 + n] : rows[5 + n] + 1, :] for n in range(plan.ch)]
        line = jnp.concatenate(parts, 1)
        bias_ref[s : s + 1, :] = line
    inside = lax.broadcasted_iota(jnp.int32, (plan.tokens, 1), 0) % plan.padded < plan.short
    values = jnp.where(inside, full, 0.0)
    normed = norm(values, par_ref[0:1, :], par_ref[2:3, :])
    sum_ref[...] = values + normed
    copies.append(pltpu.make_async_copy(sum_ref, sum_hbm, sem.at[1]))
    copies.append(pltpu.make_async_copy(par_ref, par_hbm, sem.at[2]))
    copies[1].start()
    copies[2].start()
    copies[0].wait()
    emit_wire(plan, normed, tab.at[0], tab.at[1], wire_ref, scratch)
    copies[1].wait()
    copies[2].wait()


def token_kernel(plan, first, last, *refs):
    copies = []
    if first:
        me_ref, wire_in = refs[:2]
        sources, refs = refs[2:20], refs[20:]
        (sum_out, wire_out, up_all, down_all), refs = refs[:4], refs[4:]
        scratch, sem, (sum_in, ahead, behind, par_ref) = refs[0], refs[1], refs[2:]
        shard = up_all.shape[1] // plan.ch
        half, third = shard // 2, shard // 3
        y = me_ref[2]
        copies = fetch(sources[:4], (sum_in, ahead, behind, par_ref), sem)
        groups = []
        weights = sources[4:]
        for s in range(plan.ch):
            at = s * shard
            if s < plan.ch // 2:
                ups, downs = weights[:1], weights[1:2]
                weights = weights[2:]
                ups = [(ups[0], up_all.at[:, at : at + shard])]
                downs = [(downs[0], down_all.at[at : at + shard, :])]
            else:
                ups, downs = weights[:2], weights[2:5]
                spots = [pl.multiple_of(at + n * half, LANES) for n in (y, 1 - y)]
                ups = [(w, up_all.at[:, pl.ds(n, half)]) for w, n in zip(ups, spots)]
                spots = [pl.multiple_of(at + n * third, LANES) for n in (y, 1 - y)]
                spots.append(at + 2 * third)
                downs = [(w, down_all.at[pl.ds(n, third), :]) for w, n in zip(downs, spots)]
                weights = weights[5:]
            group = []
            for source, target in ups + downs:
                count = len(copies)
                copies.append(pltpu.make_async_copy(source, target, sem.at[count]))
                copies[-1].start()
                group.append(copies[-1])
            groups.append(group)
        for copy in copies[:4]:
            copy.wait()
    else:
        wire_in, sum_in, ahead, behind, par_ref, up_all, down_all = refs[:7]
        outs, scratch = refs[7:-1], refs[-1]
        shard = up_all.shape[1] // plan.ch
        half = shard // 2
    values = sum_in[...] + read_wire(plan, wire_in, behind.at[0], behind.at[1], scratch)
    normed = norm(values, par_ref[1:2, :], par_ref[3:4, :]).astype(BF)
    mixed = par_ref[4:5, :]
    for s in range(2 * plan.ch):
        if first and s % 2 == 0:
            for copy in groups[s // 2]:
                copy.wait()
        at = slice((s % 2) * half, (s % 2 + 1) * half)
        cut = slice(s * half, (s + 1) * half)
        bias = par_ref[8 + s // 2 : 9 + s // 2, at]
        pre = dot(normed, up_all[:, cut]) + bias
        hidden = (0.5 * pre * (1.0 + lax.erf(pre * math.sqrt(0.5)))).astype(BF)
        mixed = mixed + dot(hidden, down_all[cut, :])
    values = values + mixed
    if last:
        for c in range(plan.ch):
            outs[0][c] = pack(values[:, c * plan.wide : (c + 1) * plan.wide])
        return
    if not first:
        sum_out, wire_out = outs
    normed = norm(values, par_ref[0:1, :], par_ref[2:3, :])
    sum_out[...] = values + normed
    emit_wire(plan, normed, ahead.at[0], ahead.at[1], wire_out, scratch)


def spectral_kernel(plan, far, wire_in, *refs):
    copies = []
    if far:
        sources, refs = refs[:11], refs[11:]
        wire_out, scratch, sem, mids = refs[0], refs[1], refs[2], refs[3:]
        copies = fetch(sources, mids, sem)
    else:
        mids, (wire_out, scratch) = refs[:11], refs[11:]
    chi, clo, ehi, elo, w1h, w1l, w2h, w2l, b1, b2, sign_ref = mids
    scratch[...] = wire_in[...].astype(F32)
    count = plan.peers * plan.main
    half = count + plan.peers * plan.left
    low = low_lanes((half, LANES))
    pieces = []
    for u in range(plan.units):
        parts = [scratch[:, u * plan.main : (u + 1) * plan.main, :].reshape(count, LANES)]
        for p in range(plan.peers if plan.left else 0):
            row = plan.units * plan.main + u * plan.left
            parts.append(scratch[p, row : row + plan.left, :])
        data = jnp.concatenate(parts, 0) if len(parts) > 1 else parts[0]
        turned = swap(data)
        turned = jnp.where(low, -turned, turned)
        pieces.append(jnp.concatenate([data, turned], 0).astype(BF))
    right = jnp.concatenate(pieces, 1)

    def ready(*which):
        for n in which if far else ():
            copies[n].wait()

    ready(0, 1, 10)
    spec = dot(chi[...], right) + dot(clo[...], right)
    sign = jnp.concatenate([sign_ref[...]] * plan.units, 1)
    spec = spec * sign

    def layer(value, wh, wl, bias):
        hi, lo = split(value)
        return dot(hi, wh[...]) + dot(hi, wl[...]) + dot(lo, wh[...]) + bias[...]

    ready(4, 5, 8)
    first = jnp.maximum(layer(spec, w1h, w1l, b1), 0.0)
    ready(6, 7, 9)
    second = layer(first, w2h, w2l, b2)
    shrunk = jnp.where(
        second > SHRINK, second - SHRINK, jnp.where(second < -SHRINK, second + SHRINK, 0.0)
    )
    shrunk = shrunk * sign
    low = low_lanes((plan.modes, LANES))
    pieces = []
    for u in range(plan.units):
        part = shrunk[:, u * LANES : (u + 1) * LANES]
        turned = swap(part)
        pieces.append(jnp.concatenate([part, jnp.where(low, -turned, turned)], 0))
    hi, lo = split(jnp.concatenate(pieces, 1))
    ready(2, 3)
    back = dot(ehi[...], hi) + dot(elo[...], hi) + dot(ehi[...], lo)
    for u in range(plan.units):
        part = back[:, u * LANES : (u + 1) * LANES]
        scratch[:, u * plan.main : (u + 1) * plan.main, :] = part[:count].reshape(
            plan.peers, plan.main, LANES
        )
        row = plan.units * plan.main + u * plan.left
        for p in range(plan.peers if plan.left else 0):
            at = count + p * plan.left
            scratch[p, row : row + plan.left, :] = part[at : at + plan.left]
    wire_out[...] = scratch[...].astype(BF)


def call(body, outs, operands, scratch, flops, smem=0, far_in=0, far_out=(), grant=20):
    vmem = pl.BlockSpec(memory_space=pltpu.VMEM)
    anywhere = pl.BlockSpec(memory_space=pl.ANY)
    flat, tree = jax.tree.flatten(outs)
    out_specs = [anywhere if n in far_out else vmem for n in range(len(flat))]
    return pl.pallas_call(
        body,
        out_shape=outs,
        in_specs=[pl.BlockSpec(memory_space=pltpu.SMEM)] * smem
        + [vmem] * (len(operands) - smem - far_in)
        + [anywhere] * far_in,
        out_specs=jax.tree.unflatten(tree, out_specs),
        scratch_shapes=scratch,
        compiler_params=pltpu.CompilerParams(vmem_limit_bytes=grant * 2**20),
        cost_estimate=pl.CostEstimate(flops=flops, bytes_accessed=2**20, transcendentals=0),
    )(*operands)


def local(
    state,
    norm_gains,
    channel_biases,
    filter_in,
    filter_in_bias,
    filter_out,
    filter_out_bias,
    up_weight,
    up_bias,
    down_weight,
):
    _, rows, width, wide = state.shape
    plan = Plan(lax.axis_size("lat"), lax.axis_size("ch"), rows, width)
    ch = plan.ch
    far = ch // 2
    both = ("lat", "ch")
    assert plan.spare * rows >= 5 + ch and up_bias.shape[0] == ch * wide
    lat_me = lax.axis_index("lat").astype(jnp.int32)
    me = jnp.stack([lat_me, lax.axis_index("ch").astype(jnp.int32), lat_me % 2])

    def across(value, step):
        return lax.ppermute(value, "ch", [(i, i ^ step) for i in range(ch)])

    def beside(value):
        return lax.ppermute(value, "lat", [(i, i ^ 1) for i in range(plan.lat)])

    def exchange(value, axes):
        return lax.all_to_all(value, axes, 0, 0, tiled=True)

    def after(value, token):
        return lax.optimization_barrier((value, token))[0]

    message = jax.ShapeDtypeStruct((ch, plan.packed, LANES), F32)
    tokens = call(
        lambda *r: pack_kernel(plan, *r),
        message,
        (state[0], norm_gains, channel_biases, up_bias.reshape(1, ch * wide)),
        [pltpu.VMEM((plan.tokens, wide), F32)]
        + [pltpu.VMEM((rows, width, LANES), F32)] * 2
        + [pltpu.VMEM(v.shape, BF) for v in (norm_gains, channel_biases, up_bias.reshape(1, -1))]
        + [pltpu.SemaphoreType.DMA((3,))],
        10**8,
        far_in=3,
        grant=58,
    )
    got = exchange(tokens, "ch")

    half, third = up_weight.shape[1] // 2, down_weight.shape[0] // 3
    parts = [
        jax.ShapeDtypeStruct((up_weight.shape[0], half), BF),
        jax.ShapeDtypeStruct((third, down_weight.shape[1]), BF),
        jax.ShapeDtypeStruct((third, down_weight.shape[1]), BF),
    ]
    up_part, near_part, rest_part = call(
        parts_kernel,
        tuple(parts),
        (me, up_weight, down_weight),
        [pltpu.VMEM(t.shape, BF) for t in parts] + [pltpu.SemaphoreType.DMA((6,))],
        10**6,
        smem=1,
        far_in=2,
        far_out=(0, 1, 2),
        grant=58,
    )
    up_a = across(up_part, far)
    up_c, down_c = across(up_weight, 1), across(down_weight, 1)

    ahead, behind = (jnp.asarray(table) for table in short_tables(plan))
    odd = np.tile(np.repeat(np.arange(plan.slots) % 2, plan.height), plan.per)
    sign = np.where((odd[:, None] == 1) & (np.arange(LANES)[None] >= HALF), -1.0, 1.0)
    sign = sign.astype(np.float32)

    wire = jax.ShapeDtypeStruct((plan.peers, plan.message, LANES), BF)
    held = jax.ShapeDtypeStruct((plan.tokens, D), F32)
    scratch = [pltpu.VMEM((plan.lat, ch, plan.message, LANES), F32)]
    params = jax.ShapeDtypeStruct((16, D), F32)
    total, sent, params = call(
        lambda *r: start_kernel(plan, *r),
        (held, wire, params),
        (me, got, ahead),
        scratch
        + [pltpu.VMEM(t.shape, t.dtype) for t in (ahead, held, params)]
        + [pltpu.SemaphoreType.DMA((3,))],
        10**9,
        smem=1,
        far_in=1,
        far_out=(0, 2),
        grant=58,
    )
    row, col = mode_places(plan)
    lines = plan.peers * (plan.main + plan.left)
    tables = [
        jax.ShapeDtypeStruct(dims, BF)
        for dims in [(plan.modes, 2 * lines)] * 2
        + [(lines, 2 * plan.modes)] * 2
        + [(2 * wide, 2 * wide)] * 4
    ] + [jax.ShapeDtypeStruct((1, 2 * wide), F32)] * 2
    spectral_in = call(
        lambda *r: prep_kernel(plan, *r),
        tuple(tables),
        (after(me, sent), row.T, col, row, col.T, filter_in, filter_in_bias, filter_out, filter_out_bias),
        [pltpu.VMEM(t.shape, t.dtype) for t in tables] + [pltpu.SemaphoreType.DMA((len(tables),))],
        10**8,
        smem=1,
        far_out=range(len(tables)),
        grant=58,
    )
    for step_index in range(STEPS):
        first, last = step_index == 0, step_index == STEPS - 1
        arrived = exchange(sent, both)
        if first:
            down_a = across(near_part, far)
            up_b = beside(up_a)
            up_ac = across(up_a, 1)
        tabs = (*spectral_in, sign)
        mids = [pltpu.VMEM(t.shape, t.dtype) for t in tabs] if first else []
        sent = call(
            lambda *r: spectral_kernel(plan, first, *r),
            wire,
            (arrived, *tabs),
            [pltpu.VMEM((plan.peers, plan.message, LANES), F32)]
            + ([pltpu.SemaphoreType.DMA((len(tabs),))] if first else [])
            + mids,
            10**9,
            far_in=len(mids),
            grant=58 if first else 20,
        )
        if first:
            down_b = beside(after(down_a, sent))
            down_ac = across(after(down_a, sent), 1)
            up_bc = across(after(up_b, sent), 1)
            rest = across(rest_part, far)
        arrived = exchange(sent, both)
        if first:
            down_bc = across(after(down_b, arrived), 1)
            rest_c = across(after(rest, arrived), 1)
            near = (up_weight, down_weight, up_c, down_c)
            distant = (up_a, up_b, down_a, down_b, rest, up_ac, up_bc, down_ac, down_bc, rest_c)
            sources = (total, ahead, behind, params, *near, *distant)
            total, sent, ups, downs = call(
                lambda *r: token_kernel(plan, True, False, *r),
                (
                    held,
                    wire,
                    jax.ShapeDtypeStruct((D, ch * up_weight.shape[1]), BF),
                    jax.ShapeDtypeStruct((ch * down_weight.shape[0], D), BF),
                ),
                (me, arrived, *sources),
                scratch
                + [pltpu.SemaphoreType.DMA((len(sources),))]
                + [pltpu.VMEM(t.shape, t.dtype) for t in sources[:4]],
                10**10,
                smem=1,
                far_in=len(sources),
                grant=24,
            )
            continue
        result = call(
            lambda *r: token_kernel(plan, False, last, *r),
            message if last else (held, wire),
            (arrived, total, ahead, behind, params, ups, downs),
            scratch,
            10**10,
        )
        if not last:
            total, sent = result
    result = exchange(result, "ch")
    result = call(
        lambda *r: unpack_kernel(plan, *r),
        jax.ShapeDtypeStruct((rows, width, wide), F32),
        (result,),
        [pltpu.VMEM((rows, width, LANES), F32)] * 2,
        10**8,
    )
    return result[None]


def solution(mesh):
    placed = (
        P(None, "lat", None, "ch"),
        P(None, "ch"),
        P(None, "ch"),
        P(None, "ch", None, None),
        P(None, "ch", None),
        P(None, "ch", None, None),
        P(None, "ch", None),
        P(None, "ch"),
        P("ch"),
        P("ch", None),
    )

    return jax.shard_map(
        local, mesh=mesh, in_specs=placed, out_specs=P(None, "lat", None, "ch"), check_vma=False
    )
```

time: 457 us -> 188 us (0.41); the launches traced: 448 us -> 187 us
  blocking collectives: 222 us -> 89 us
  matrix products: 72.4 us -> 0 us
  local copies, waits for them, and re-layouts: 69.2 us -> 7.91 us
  Pallas kernels: 0 us -> 45.4 us
  other arithmetic: 36.9 us -> 0.65 us
  between operations: 15.4 us -> 0.3 us
  starting transfers between devices: 13 us -> 26.6 us
    all_to_all x13 -> x7, blocking collectives: 169 us -> 89 us  [exchange(): return lax.all_to_all(value, axes, 0, 0, tiled=True)]
    dot_general x84 -> x0, matrix products: 72.4 us -> none  [the longest x4 34.7 us: local(): jnp.dot(hidden, full_down, preferred_element_type=jnp.float32)]
    pallas_call x0 -> x13, Pallas kernels: none -> 45.4 us  [call(): pl.pallas_call(body, out_shape=outs, in_specs=[pl.BlockSpec(memory_space=...]
    all_to_all x32 -> x0, local copies, waits for them, and re-layouts: 28.2 us -> none  [the longest x12 24.4 us: local(): lax.all_to_all(mixed.reshape(owned.shape), 'ch', split_axis=3, concat_axi...]
    all_gather x3 -> x0, blocking collectives: 27 us -> none  [the longest x1 16.5 us: local(): lax.all_gather(up_bias, 'ch', axis=0, tiled=True)]
    psum x4 -> x0, blocking collectives: 26.2 us -> none  [local(): lax.psum((jnp.sum(values, -1, keepdims=True), jnp.sum(values * values, -1...]
    unnamed x4 -> x0, other arithmetic: 20.4 us -> none
    unnamed x27 -> x41, local copies, waits for them, and re-layouts: 19.2 us -> 5.26 us
  transfers between devices with their start and end apart: 5 -> 15, of which waited for: 3 -> 8; matrix products, arithmetic and copies ran while one was open for 4% -> 0% of each run, Pallas kernels for 0% -> 9%
where the time goes in v1:
time: 188 us; the launch traced here: 187 us
  blocking collectives  89 us (47%)
  Pallas kernels  45.4 us (24%)
  starting transfers between devices  26.6 us (14%)
  waiting for transfers between devices  17.5 us (9%)
  local copies, waits for them, and re-layouts  7.91 us (4%)
    all_to_all x7, blocking collectives, exchange(): return lax.all_to_all(value, axes, 0, 0, tiled=True)  89 us
    pallas_call x13, Pallas kernels, call(): pl.pallas_call(body, out_shape=outs, in_specs=[pl.BlockSpec(memory_space=...  45.4 us
    all_to_all x3, starting transfers between devices, exchange(): return lax.all_to_all(value, axes, 0, 0, tiled=True)  15.8 us
    all_to_all x3, waiting for transfers between devices, exchange(): return lax.all_to_all(value, axes, 0, 0, tiled=True)  10.6 us
    ppermute x10, starting transfers between devices, across(): return lax.ppermute(value, 'ch', [(i, i ^ step) for i in range(ch)])  6.33 us
    unnamed x41, local copies, waits for them, and re-layouts  5.26 us
    ppermute x2, starting transfers between devices, beside(): return lax.ppermute(value, 'lat', [(i, i ^ 1) for i in range(plan.lat)])  4.46 us
  transfers between devices with their start and end apart: 15, of which 8 were waited for; matrix products, arithmetic and copies ran while one was open for 0% of the time, Pallas kernels for 9%

profile of v1, /device:TPU:0, one launch (start us, length us, event | category | flops | bytes accessed | tf_op | source)
XLA Modules:
  0.0 187.3 jit_solution(2638327794019592946)
XLA Ops:
  1.3 1.9 %copy.21 = f32[1,3,180,192]{3,2,0,1:T(8,128)} copy(f32[1,3,180,192]{3,0,2,1:T(1,128)} %param.17) | data formatting | bytes 829440
  3.2 2.7 %shard_map.163 = f32[4,216,128]{2,1,0:T(8,128)} custom-call(f32[3,180,192]{2,1,0:T(8,128)} %bitcast.8, bf16[2,192]{1,0:T(2,128)(2,1)} %r_1_.2, bf16[3,192]{1,0:T(4,128)(2,1)} %r_2_.6, bf16[1,768]{1,0:T(2,128)(2,1)} %reshape.3.r_3_), custom_call_target="tpu_custom_call" | custom-call | flops 100000000 | bytes 1048576 | tf_op jit(solution)/shard_map/pallas_call | solution.py:513
  5.9 4.2 %all-to-all-start = ((f32[4,216,128]{2,1,0:T(8,128)}), f32[4,216,128]{2,1,0:T(8,128)S(1)}, u32[]{:S(2)}, u32[]{:S(2)}) async-start(f32[4,216,128]{2,1,0:T(8,128)} %shard_map.163), calls=%async_computation | async-start | bytes 884736 | tf_op jit(solution)/shard_map/all_to_all | solution.py:554
  10.8 3.1 %shard_map.167 = (bf16[768,384]{1,0:T(8,128)(2,1)}, bf16[256,768]{1,0:T(8,128)(2,1)}, bf16[256,768]{1,0:T(8,128)(2,1)}) custom-call(s32[3]{0:T(128)} %pad_add_fusion.r_0_.me_ref, bf16[768,768]{1,0:T(8,128)(2,1)} %r_6_.3, bf16[768,768]{1,0:T(8,128)(2,1)} %r_7_.3), custom_call_target="tpu_custom_call" | custom-call | flops 1000000 | bytes 1048576 | tf_op jit(solution)/shard_map/pallas_call | solution.py:513
  13.9 2.3 %collective-permute-start.2 = (bf16[768,384]{1,0:T(8,128)(2,1)}, bf16[768,384]{1,0:T(8,128)(2,1)S(1)}, u32[]{:S(2)}, u32[]{:S(2)}) collective-permute-start(bf16[768,384]{1,0:T(8,128)(2,1)} %get-tuple-element.48), channel_id=1, source_target_pairs={{0,2},{1,3},{2,0},{3,1},{4,6},{5,7},{6,4},{7,5},{8,10},{9,11},{10,... | collective-permute-start | bytes 1769480 | tf_op jit(solution)/shard_map/ppermute | solution.py:548
  16.7 2.1 %all-to-all-done.r_1_ = f32[4,216,128]{2,1,0:T(8,128)S(1)} async-done(((f32[4,216,128]{2,1,0:T(8,128)}), f32[4,216,128]{2,1,0:T(8,128)S(1)}, u32[]{:S(2)}, u32[]{:S(2)}) %all-to-all-start) | async-done | bytes 442400 | tf_op jit(solution)/shard_map/all_to_all | solution.py:554
  19.6 3.2 %shard_map.164 = (f32[144,768]{1,0:T(8,128)}, bf16[32,32,128]{2,1,0:T(8,128)(2,1)}, f32[16,768]{1,0:T(8,128)}) custom-call(s32[3]{0:T(128)} %pad_add_fusion.r_0_.me_ref, f32[4,216,128]{2,1,0:T(8,128)} %copy-done.18, bf16[2,144,144]{2,1,0:T(8,128)(2,1)} %constant.36.clone.r_2_.r_3_), custom_call_target="tpu_custom_call" | custom-call | flops 1000000000 | bytes 1048576 | tf_op jit(solution)/shard_map/pallas_call | solution.py:513
  22.8 5.5 %all-to-all-start.1 = ((bf16[32,32,128]{2,1,0:T(8,128)(2,1)}), bf16[32,32,128]{2,1,0:T(8,128)(2,1)S(1)}, u32[]{:S(2)}, u32[]{:S(2)}) async-start(bf16[32,32,128]{2,1,0:T(8,128)(2,1)} %get-tuple-element.34), calls=%async_computation.1 | async-start | bytes 524288 | tf_op jit(solution)/shard_map/all_to_all | solution.py:554
  28.2 1.8 collective-permute-start.4
  30.8 2.6 %collective-permute-start.3 = (bf16[768,384]{1,0:T(8,128)(2,1)S(1)}, bf16[768,384]{1,0:T(8,128)(2,1)}, u32[]{:S(2)}, u32[]{:S(2)}) collective-permute-start(bf16[768,384]{1,0:T(8,128)(2,1)S(1)} %collective-permute-done.2.r_10_), channel_id=1, source_target_pairs={{0,4},{4,0},{8,12},{12,8},{16,20},{20,16},{24,28},{28,24},{1,5},{5... | collective-permute-start | bytes 1769480 | tf_op jit(solution)/shard_map/ppermute | solution.py:551
  34.0 4.5 %shard_map.165 = (bf16[216,576]{1,0:T(8,128)(2,1)}, bf16[216,576]{1,0:T(8,128)(2,1)}, bf16[288,432]{1,0:T(8,128)(2,1)}, bf16[288,432]{1,0:T(8,128)(2,1)}, bf16[3...) custom-call(s32[3]{0:T(128)} %pad_add_fusion.r_0_.me_ref, ...), custom_call_target="tpu_custom_call" | custom-call | flops 100000000 | bytes 1048576 | tf_op jit(solution)/shard_map/pallas_call | solution.py:513
  39.5 6.1 %shard_map.166 = bf16[32,32,128]{2,1,0:T(8,128)(2,1)} custom-call(bf16[32,32,128]{2,1,0:T(8,128)(2,1)} %copy-done.19, bf16[216,576]{1,0:T(8,128)(2,1)} %get-tuple-element.36.r_1_, bf16[216,576]{1,0:T(8,128)(2,1)} %get-tuple-element.37.r_2_, bf16[288,432]{1,0:T(8,128)(2,1)} %get-tuple-element.38.r_3_, bf16[288,432]{1,0:T(8,128)(2,1)} %get-tuple-element.39.r_4_, ...), custom_call_target="tpu_custom_call" | custom-call | flops 1000000000 | bytes 1048576 | tf_op jit(solution)/shard_map/pallas_call | solution.py:513
  45.6 6.1 %all-to-all-start.2 = ((bf16[32,32,128]{2,1,0:T(8,128)(2,1)}), bf16[32,32,128]{2,1,0:T(8,128)(2,1)S(1)}, u32[]{:S(2)}, u32[]{:S(2)}) async-start(bf16[32,32,128]{2,1,0:T(8,128)(2,1)} %shard_map.166), calls=%async_computation.2 | async-start | bytes 524288 | tf_op jit(solution)/shard_map/all_to_all | solution.py:554
  51.7 1.8 collective-permute-start.5
  54.1 8.2 %all-to-all-done.2.r_1_ = bf16[32,32,128]{2,1,0:T(8,128)(2,1)S(1)} async-done(((bf16[32,32,128]{2,1,0:T(8,128)(2,1)}), bf16[32,32,128]{2,1,0:T(8,128)(2,1)S(1)}, u32[]{:S(2)}, u32[]{:S(2)}) %all-to-all-start.2) | async-done | bytes 262176 | tf_op jit(solution)/shard_map/all_to_all | solution.py:554
  62.3 3.7 %collective-permute-done.5.r_13_ = bf16[256,768]{1,0:T(8,128)(2,1)} collective-permute-done((bf16[256,768]{1,0:T(8,128)(2,1)}, bf16[256,768]{1,0:T(8,128)(2,1)}, u32[]{:S(2)}, u32[]{:S(2)}) %collective-permute-start.5) | collective-permute-done | bytes 393248 | tf_op jit(solution)/shard_map/ppermute | solution.py:551
  66.6 1.3 collective-permute-done.9.r_17_
  71.0 7.0 %shard_map.168 = (f32[144,768]{1,0:T(8,128)S(1)}, bf16[32,32,128]{2,1,0:T(8,128)(2,1)S(1)}, bf16[768,3072]{1,0:T(8,128)(2,1)S(1)}, bf16[3072,768]{1,0:T(8,128)(2,1)S(1)}) custom-call(s32[3]{0:T(128)S(1)} %copy-done.2, bf16[32,32,128]{2,1,0:T(8,128)(2,1)S(1)} %all-to-all-done.2.r_1_, f32[144,768]{1,0:T(8,128)S(1)} %copy-done.16, ...), custom_call_target="tpu_custom_call" | custom-call | flops 10000000000 | bytes 1048576 | tf_op jit(solution)/shard_map/pallas_call | solution.py:513
  78.0 14.8 %all_to_all.50.r_0_ = bf16[32,32,128]{2,1,0:T(8,128)(2,1)S(1)} all-to-all(bf16[32,32,128]{2,1,0:T(8,128)(2,1)S(1)} %get-tuple-element.55), channel_id=1, replica_groups=mesh['lat'=8,'ch'=4] {'lat','ch'}, dimensions={0} | all-to-all | bytes 524288 | tf_op jit(solution)/shard_map/all_to_all | solution.py:554
  92.9 2.4 %shard_map.169 = bf16[32,32,128]{2,1,0:T(8,128)(2,1)S(1)} custom-call(bf16[32,32,128]{2,1,0:T(8,128)(2,1)S(1)} %all_to_all.50.r_0_, bf16[216,576]{1,0:T(8,128)(2,1)S(1)} %copy-done.9, bf16[216,576]{1,0:T(8,128)(2,1)S(1)} %copy-done.10, bf16[288,432]{1,0:T(8,128)(2,1)S(1)} %copy-done.3, bf16[288,432]{1,0:T(8,128)(2,1)S(1)} %copy-done.4, ...), custom_call_target="tpu_custom_call" | custom-call | flops 1000000000 | bytes 1048576 | tf_op jit(solution)/shard_map/pallas_call | solution.py:513
  95.4 12.8 %all_to_all.51.r_0_ = bf16[32,32,128]{2,1,0:T(8,128)(2,1)S(1)} all-to-all(bf16[32,32,128]{2,1,0:T(8,128)(2,1)S(1)} %shard_map.169), channel_id=1, replica_groups=mesh['lat'=8,'ch'=4] {'lat','ch'}, dimensions={0} | all-to-all | bytes 524288 | tf_op jit(solution)/shard_map/all_to_all | solution.py:554
  108.1 3.9 %shard_map.170 = (f32[144,768]{1,0:T(8,128)S(1)}, bf16[32,32,128]{2,1,0:T(8,128)(2,1)S(1)}) custom-call(bf16[32,32,128]{2,1,0:T(8,128)(2,1)S(1)} %all_to_all.51.r_0_, f32[144,768]{1,0:T(8,128)S(1)} %get-tuple-element.56.r_1_, bf16[2,144,144]{2,1,0:T(8,128)(2,1)S(1)} %copy-done.13, bf16[2,144,144]{2,1,0:T(8,128)(2,1)S(1)} %copy-done.14, ...), custom_call_target="tpu_custom_call" | custom-call | flops 10000000000 | bytes 1048576 | tf_op jit(solution)/shard_map/pallas_call | solution.py:513
  112.1 12.8 %all_to_all.52.r_0_ = bf16[32,32,128]{2,1,0:T(8,128)(2,1)S(1)} all-to-all(bf16[32,32,128]{2,1,0:T(8,128)(2,1)S(1)} %get-tuple-element.59), channel_id=1, replica_groups=mesh['lat'=8,'ch'=4] {'lat','ch'}, dimensions={0} | all-to-all | bytes 524288 | tf_op jit(solution)/shard_map/all_to_all | solution.py:554
  124.9 2.4 %shard_map.171 = bf16[32,32,128]{2,1,0:T(8,128)(2,1)S(1)} custom-call(bf16[32,32,128]{2,1,0:T(8,128)(2,1)S(1)} %all_to_all.52.r_0_, bf16[216,576]{1,0:T(8,128)(2,1)S(1)} %copy-done.9, bf16[216,576]{1,0:T(8,128)(2,1)S(1)} %copy-done.10, bf16[288,432]{1,0:T(8,128)(2,1)S(1)} %copy-done.3, bf16[288,432]{1,0:T(8,128)(2,1)S(1)} %copy-done.4, ...), custom_call_target="tpu_custom_call" | custom-call | flops 1000000000 | bytes 1048576 | tf_op jit(solution)/shard_map/pallas_call | solution.py:513
  127.3 12.8 %all_to_all.53.r_0_ = bf16[32,32,128]{2,1,0:T(8,128)(2,1)S(1)} all-to-all(bf16[32,32,128]{2,1,0:T(8,128)(2,1)S(1)} %shard_map.171), channel_id=1, replica_groups=mesh['lat'=8,'ch'=4] {'lat','ch'}, dimensions={0} | all-to-all | bytes 524288 | tf_op jit(solution)/shard_map/all_to_all | solution.py:554
  140.1 3.9 %shard_map.172 = (f32[144,768]{1,0:T(8,128)S(1)}, bf16[32,32,128]{2,1,0:T(8,128)(2,1)S(1)}) custom-call(bf16[32,32,128]{2,1,0:T(8,128)(2,1)S(1)} %all_to_all.53.r_0_, f32[144,768]{1,0:T(8,128)S(1)} %get-tuple-element.60.r_1_, bf16[2,144,144]{2,1,0:T(8,128)(2,1)S(1)} %copy-done.13, bf16[2,144,144]{2,1,0:T(8,128)(2,1)S(1)} %copy-done.14, ...), custom_call_target="tpu_custom_call" | custom-call | flops 10000000000 | bytes 1048576 | tf_op jit(solution)/shard_map/pallas_call | solution.py:513
  144.0 12.8 %all_to_all.54.r_0_ = bf16[32,32,128]{2,1,0:T(8,128)(2,1)S(1)} all-to-all(bf16[32,32,128]{2,1,0:T(8,128)(2,1)S(1)} %get-tuple-element.61), channel_id=1, replica_groups=mesh['lat'=8,'ch'=4] {'lat','ch'}, dimensions={0} | all-to-all | bytes 524288 | tf_op jit(solution)/shard_map/all_to_all | solution.py:554
  156.8 2.4 %shard_map.173 = bf16[32,32,128]{2,1,0:T(8,128)(2,1)S(1)} custom-call(bf16[32,32,128]{2,1,0:T(8,128)(2,1)S(1)} %all_to_all.54.r_0_, bf16[216,576]{1,0:T(8,128)(2,1)S(1)} %copy-done.9, bf16[216,576]{1,0:T(8,128)(2,1)S(1)} %copy-done.10, bf16[288,432]{1,0:T(8,128)(2,1)S(1)} %copy-done.3, bf16[288,432]{1,0:T(8,128)(2,1)S(1)} %copy-done.4, ...), custom_call_target="tpu_custom_call" | custom-call | flops 1000000000 | bytes 1048576 | tf_op jit(solution)/shard_map/pallas_call | solution.py:513
  159.2 12.8 %all_to_all.55.r_0_ = bf16[32,32,128]{2,1,0:T(8,128)(2,1)S(1)} all-to-all(bf16[32,32,128]{2,1,0:T(8,128)(2,1)S(1)} %shard_map.173), channel_id=1, replica_groups=mesh['lat'=8,'ch'=4] {'lat','ch'}, dimensions={0} | all-to-all | bytes 524288 | tf_op jit(solution)/shard_map/all_to_all | solution.py:554
  172.0 3.5 %shard_map.174 = f32[4,216,128]{2,1,0:T(8,128)S(1)} custom-call(bf16[32,32,128]{2,1,0:T(8,128)(2,1)S(1)} %all_to_all.55.r_0_, f32[144,768]{1,0:T(8,128)S(1)} %get-tuple-element.62.r_1_, bf16[2,144,144]{2,1,0:T(8,128)(2,1)S(1)} %copy-done.13, bf16[2,144,144]{2,1,0:T(8,128)(2,1)S(1)} %copy-done.14, f32[16,768]{1,0:T(8,128)S(1)} %copy-done.17, ...), custom_call_target="tpu_custom_call" | custom-call | flops 10000000000 | bytes 1048576 | tf_op jit(solution)/shard_map/pallas_call | solution.py:513
  175.4 10.3 %all_to_all.56.r_0_ = f32[4,216,128]{2,1,0:T(8,128)S(1)} all-to-all(f32[4,216,128]{2,1,0:T(8,128)S(1)} %shard_map.174), channel_id=1, replica_groups=mesh['lat'=8,'ch'=4] {'ch'}, dimensions={0} | all-to-all | bytes 884736 | tf_op jit(solution)/shard_map/all_to_all | solution.py:554
  186.0 1.4 copy.18
  (62 shorter events, 9.8 us)
Async XLA Ops:
  5.9 12.9 %all-to-all-start = ((f32[4,216,128]{2,1,0:T(8,128)}), f32[4,216,128]{2,1,0:T(8,128)S(1)}, u32[]{:S(2)}, u32[]{:S(2)}) async-start(f32[4,216,128]{2,1,0:T(8,128)} %shard_map.163), calls=%async_computation | async-start | bytes 884736 | tf_op jit(solution)/shard_map/all_to_all | solution.py:554
  10.8 5.4 %copy-start = (bf16[768,768]{1,0:T(8,128)(2,1)S(1)}, bf16[768,768]{1,0:T(8,128)(2,1)}, u32[]{:S(2)}) copy-start(bf16[768,768]{1,0:T(8,128)(2,1)} %r_6_.3) | copy-start | bytes 3538948
  10.8 5.4 %copy-start.1 = (bf16[768,768]{1,0:T(8,128)(2,1)S(1)}, bf16[768,768]{1,0:T(8,128)(2,1)}, u32[]{:S(2)}) copy-start(bf16[768,768]{1,0:T(8,128)(2,1)} %r_7_.3) | copy-start | bytes 3538948
  13.9 16.8 %collective-permute-start.2 = (bf16[768,384]{1,0:T(8,128)(2,1)}, bf16[768,384]{1,0:T(8,128)(2,1)S(1)}, u32[]{:S(2)}, u32[]{:S(2)}) collective-permute-start(bf16[768,384]{1,0:T(8,128)(2,1)} %get-tuple-element.48), channel_id=1, source_target_pairs={{0,2},{1,3},{2,0},{3,1},{4,6},{5,7},{6,4},{7,5},{8,10},{9,11},{10,... | collective-permute-start | bytes 1769480 | tf_op jit(solution)/shard_map/ppermute | solution.py:548
  16.2 49.8 %collective-permute-start = (bf16[768,768]{1,0:T(8,128)(2,1)S(1)}, bf16[768,768]{1,0:T(8,128)(2,1)}, u32[]{:S(2)}, u32[]{:S(2)}) collective-permute-start(bf16[768,768]{1,0:T(8,128)(2,1)S(1)} %copy-done), channel_id=1, source_target_pairs={{0,1},{1,0},{2,3},{3,2},{4,5},{5,4},{6,7},{7,6},{8,9},{9,8},{10,11... | collective-permute-start | bytes 3538952 | tf_op jit(solution)/shard_map/ppermute | solution.py:548
  16.2 50.3 %collective-permute-start.1 = (bf16[768,768]{1,0:T(8,128)(2,1)S(1)}, bf16[768,768]{1,0:T(8,128)(2,1)}, u32[]{:S(2)}, u32[]{:S(2)}) collective-permute-start(bf16[768,768]{1,0:T(8,128)(2,1)S(1)} %copy-done.1), channel_id=1, source_target_pairs={{0,1},{1,0},{2,3},{3,2},{4,5},{5,4},{6,7},{7,6},{8,9},{9,8},{10,11... | collective-permute-start | bytes 3538952 | tf_op jit(solution)/shard_map/ppermute | solution.py:548
  22.8 16.0 %all-to-all-start.1 = ((bf16[32,32,128]{2,1,0:T(8,128)(2,1)}), bf16[32,32,128]{2,1,0:T(8,128)(2,1)S(1)}, u32[]{:S(2)}, u32[]{:S(2)}) async-start(bf16[32,32,128]{2,1,0:T(8,128)(2,1)} %get-tuple-element.34), calls=%async_computation.1 | async-start | bytes 524288 | tf_op jit(solution)/shard_map/all_to_all | solution.py:554
  28.2 23.5 %collective-permute-start.4 = (bf16[256,768]{1,0:T(8,128)(2,1)}, bf16[256,768]{1,0:T(8,128)(2,1)}, u32[]{:S(2)}, u32[]{:S(2)}) collective-permute-start(bf16[256,768]{1,0:T(8,128)(2,1)} %get-tuple-element.49), channel_id=1, source_target_pairs={{0,2},{1,3},{2,0},{3,1},{4,6},{5,7},{6,4},{7,5},{8,10},{9,11},{10,... | collective-permute-start | bytes 1179656 | tf_op jit(solution)/shard_map/ppermute | solution.py:548
  30.8 22.8 %collective-permute-start.3 = (bf16[768,384]{1,0:T(8,128)(2,1)S(1)}, bf16[768,384]{1,0:T(8,128)(2,1)}, u32[]{:S(2)}, u32[]{:S(2)}) collective-permute-start(bf16[768,384]{1,0:T(8,128)(2,1)S(1)} %collective-permute-done.2.r_10_), channel_id=1, source_target_pairs={{0,4},{4,0},{8,12},{12,8},{16,20},{20,16},{24,28},{28,24},{1,5},{5... | collective-permute-start | bytes 1769480 | tf_op jit(solution)/shard_map/ppermute | solution.py:551
  33.4 20.2 %collective-permute-start.6 = (bf16[256,768]{1,0:T(8,128)(2,1)}, bf16[256,768]{1,0:T(8,128)(2,1)}, u32[]{:S(2)}, u32[]{:S(2)}) collective-permute-start(bf16[256,768]{1,0:T(8,128)(2,1)} %get-tuple-element.51), channel_id=1, source_target_pairs={{0,2},{1,3},{2,0},{3,1},{4,6},{5,7},{6,4},{7,5},{8,10},{9,11},{10,... | collective-permute-start | bytes 1179656 | tf_op jit(solution)/shard_map/ppermute | solution.py:548
  39.5 29.6 %copy-start.2 = (s32[3]{0:T(128)S(1)}, s32[3]{0:T(128)}, u32[]{:S(2)}) copy-start(s32[3]{0:T(128)} %pad_add_fusion.r_0_.me_ref) | copy-start | bytes 40
  39.5 29.6 %copy-start.13 = (bf16[2,144,144]{2,1,0:T(8,128)(2,1)S(1)}, bf16[2,144,144]{2,1,0:T(8,128)(2,1)}, u32[]{:S(2)}) copy-start(bf16[2,144,144]{2,1,0:T(8,128)(2,1)} %constant.36.clone.r_2_.r_3_) | copy-start | bytes 248836
  39.5 29.6 %copy-start.14 = (bf16[2,144,144]{2,1,0:T(8,128)(2,1)S(1)}, bf16[2,144,144]{2,1,0:T(8,128)(2,1)}, u32[]{:S(2)}) copy-start(bf16[2,144,144]{2,1,0:T(8,128)(2,1)} %constant.37.clone.r_4_.r_3_) | copy-start | bytes 248836
  45.6 16.7 %all-to-all-start.2 = ((bf16[32,32,128]{2,1,0:T(8,128)(2,1)}), bf16[32,32,128]{2,1,0:T(8,128)(2,1)S(1)}, u32[]{:S(2)}, u32[]{:S(2)}) async-start(bf16[32,32,128]{2,1,0:T(8,128)(2,1)} %shard_map.166), calls=%async_computation.2 | async-start | bytes 524288 | tf_op jit(solution)/shard_map/all_to_all | solution.py:554
  51.7 14.3 %collective-permute-start.5 = (bf16[256,768]{1,0:T(8,128)(2,1)}, bf16[256,768]{1,0:T(8,128)(2,1)}, u32[]{:S(2)}, u32[]{:S(2)}) collective-permute-start(bf16[256,768]{1,0:T(8,128)(2,1)} %collective-permute-done.4.r_12_), channel_id=1, source_target_pairs={{0,4},{4,0},{8,12},{12,8},{16,20},{20,16},{24,28},{28,24},{1,5},{5... | collective-permute-start | bytes 1179656 | tf_op jit(solution)/shard_map/ppermute | solution.py:551
  53.6 13.0 %collective-permute-start.7 = (bf16[768,384]{1,0:T(8,128)(2,1)S(1)}, bf16[768,384]{1,0:T(8,128)(2,1)}, u32[]{:S(2)}, u32[]{:S(2)}) collective-permute-start(bf16[768,384]{1,0:T(8,128)(2,1)S(1)} %collective-permute-done.2.r_10_), channel_id=1, source_target_pairs={{0,1},{1,0},{2,3},{3,2},{4,5},{5,4},{6,7},{7,6},{8,9},{9,8},{10,11... | collective-permute-start | bytes 1769480 | tf_op jit(solution)/shard_map/ppermute | solution.py:548
  53.6 15.5 %collective-permute-start.8 = (bf16[768,384]{1,0:T(8,128)(2,1)}, bf16[768,384]{1,0:T(8,128)(2,1)}, u32[]{:S(2)}, u32[]{:S(2)}) collective-permute-start(bf16[768,384]{1,0:T(8,128)(2,1)} %collective-permute-done.3.r_11_), channel_id=1, source_target_pairs={{0,1},{1,0},{2,3},{3,2},{4,5},{5,4},{6,7},{7,6},{8,9},{9,8},{10,11... | collective-permute-start | bytes 1769480 | tf_op jit(solution)/shard_map/ppermute | solution.py:548
  66.0 1.9 %collective-permute-start.9 = (bf16[256,768]{1,0:T(8,128)(2,1)}, bf16[256,768]{1,0:T(8,128)(2,1)S(1)}, u32[]{:S(2)}, u32[]{:S(2)}) collective-permute-start(bf16[256,768]{1,0:T(8,128)(2,1)} %collective-permute-done.4.r_12_), channel_id=1, source_target_pairs={{0,1},{1,0},{2,3},{3,2},{4,5},{5,4},{6,7},{7,6},{8,9},{9,8},{10,11... | collective-permute-start | bytes 1179656 | tf_op jit(solution)/shard_map/ppermute | solution.py:548
  66.0 2.5 %collective-permute-start.11 = (bf16[256,768]{1,0:T(8,128)(2,1)}, bf16[256,768]{1,0:T(8,128)(2,1)S(1)}, u32[]{:S(2)}, u32[]{:S(2)}) collective-permute-start(bf16[256,768]{1,0:T(8,128)(2,1)} %collective-permute-done.6.r_14_), channel_id=1, source_target_pairs={{0,1},{1,0},{2,3},{3,2},{4,5},{5,4},{6,7},{7,6},{8,9},{9,8},{10,11... | collective-permute-start | bytes 1179656 | tf_op jit(solution)/shard_map/ppermute | solution.py:548
  66.5 2.5 %collective-permute-start.10 = (bf16[256,768]{1,0:T(8,128)(2,1)}, bf16[256,768]{1,0:T(8,128)(2,1)S(1)}, u32[]{:S(2)}, u32[]{:S(2)}) collective-permute-start(bf16[256,768]{1,0:T(8,128)(2,1)} %collective-permute-done.5.r_13_), channel_id=1, source_target_pairs={{0,1},{1,0},{2,3},{3,2},{4,5},{5,4},{6,7},{7,6},{8,9},{9,8},{10,11... | collective-permute-start | bytes 1179656 | tf_op jit(solution)/shard_map/ppermute | solution.py:548
  69.1 1.0 copy-start.16
  70.9 21.9 %copy-start.3 = (bf16[288,432]{1,0:T(8,128)(2,1)S(1)}, bf16[288,432]{1,0:T(8,128)(2,1)}, u32[]{:S(2)}) copy-start(bf16[288,432]{1,0:T(8,128)(2,1)} %get-tuple-element.38.r_3_) | copy-start | bytes 746500
  70.9 21.9 %copy-start.4 = (bf16[288,432]{1,0:T(8,128)(2,1)S(1)}, bf16[288,432]{1,0:T(8,128)(2,1)}, u32[]{:S(2)}) copy-start(bf16[288,432]{1,0:T(8,128)(2,1)} %get-tuple-element.39.r_4_) | copy-start | bytes 746500
  70.9 21.9 %copy-start.5 = (bf16[384,384]{1,0:T(8,128)(2,1)S(1)}, bf16[384,384]{1,0:T(8,128)(2,1)}, u32[]{:S(2)}) copy-start(bf16[384,384]{1,0:T(8,128)(2,1)} %get-tuple-element.40.r_5_) | copy-start | bytes 884740
  70.9 21.9 %copy-start.6 = (bf16[384,384]{1,0:T(8,128)(2,1)S(1)}, bf16[384,384]{1,0:T(8,128)(2,1)}, u32[]{:S(2)}) copy-start(bf16[384,384]{1,0:T(8,128)(2,1)} %get-tuple-element.41.r_6_) | copy-start | bytes 884740
  70.9 21.9 %copy-start.7 = (bf16[384,384]{1,0:T(8,128)(2,1)S(1)}, bf16[384,384]{1,0:T(8,128)(2,1)}, u32[]{:S(2)}) copy-start(bf16[384,384]{1,0:T(8,128)(2,1)} %get-tuple-element.42.r_7_) | copy-start | bytes 884740
  70.9 21.9 %copy-start.8 = (bf16[384,384]{1,0:T(8,128)(2,1)S(1)}, bf16[384,384]{1,0:T(8,128)(2,1)}, u32[]{:S(2)}) copy-start(bf16[384,384]{1,0:T(8,128)(2,1)} %get-tuple-element.43.r_8_) | copy-start | bytes 884740
  71.0 21.9 %copy-start.9 = (bf16[216,576]{1,0:T(8,128)(2,1)S(1)}, bf16[216,576]{1,0:T(8,128)(2,1)}, u32[]{:S(2)}) copy-start(bf16[216,576]{1,0:T(8,128)(2,1)} %get-tuple-element.36.r_1_) | copy-start | bytes 746500
  71.0 21.9 %copy-start.10 = (bf16[216,576]{1,0:T(8,128)(2,1)S(1)}, bf16[216,576]{1,0:T(8,128)(2,1)}, u32[]{:S(2)}) copy-start(bf16[216,576]{1,0:T(8,128)(2,1)} %get-tuple-element.37.r_2_) | copy-start | bytes 746500
  71.0 21.9 %copy-start.11 = (f32[1,384]{1,0:T(1,128)S(1)}, f32[1,384]{1,0:T(1,128)}, u32[]{:S(2)}) copy-start(f32[1,384]{1,0:T(1,128)} %get-tuple-element.44.r_9_) | copy-start | bytes 4612
  71.0 21.9 %copy-start.12 = (f32[1,384]{1,0:T(1,128)S(1)}, f32[1,384]{1,0:T(1,128)}, u32[]{:S(2)}) copy-start(f32[1,384]{1,0:T(1,128)} %get-tuple-element.45.r_10_) | copy-start | bytes 4612
  71.0 21.9 %copy-start.15 = (f32[216,128]{1,0:T(8,128)S(1)}, f32[216,128]{1,0:T(8,128)}, u32[]{:S(2)}) copy-start(f32[216,128]{1,0:T(8,128)} %constant.42.clone.r_11_) | copy-start | bytes 331780
  (3 other events, 2.3 us)

commit v2 on v1

--- a/solution.py
+++ b/solution.py
@@ -15,6 +15,7 @@
 EPS = 1e-05
 SHRINK = 0.01
 HALF = 64
+PACK, START, FIRST = 24, 24, 58
 LANES = 128
 BF = jnp.bfloat16
 F32 = jnp.float32
@@ -73,7 +74,9 @@
     cos, sin = np.cos(angle) * mask, np.sin(angle) * mask
     forward = np.concatenate([cos, -sin], 0)
     inverse = np.concatenate([cos.T, -sin.T], 1)
-    return np.stack(split_np(forward)), np.stack(split_np(inverse))
+    side = max(forward.shape)
+    tables = [np.pad(t, [(0, side - n) for n in t.shape]) for t in (forward, inverse)]
+    return np.stack(split_np(tables[0]) + split_np(tables[1]))
 
 
 def mode_places(plan):
@@ -151,12 +154,12 @@
     return (values - mean) * lax.rsqrt(spread + EPS) * gain + shift
 
 
-def emit_wire(plan, normed, fhi, flo, wire_ref, scratch):
+def emit_wire(plan, normed, tab, wire_ref, scratch):
     hi, lo = split(normed)
-    spec = dot(fhi[...], hi) + dot(flo[...], hi) + dot(fhi[...], lo)
     count = plan.lat * plan.main
-    extra = plan.lat * plan.left
-    half = count + extra
+    half = count + plan.lat * plan.left
+    fhi, flo = tab[0, : 2 * half, : plan.tokens], tab[1, : 2 * half, : plan.tokens]
+    spec = dot(fhi, hi) + dot(flo, hi) + dot(fhi, lo)
     low = low_lanes((half, LANES))
     for tile in range(D // LANES):
         lanes = slice(tile * LANES, (tile + 1) * LANES)
@@ -182,7 +185,7 @@
     wire_ref[...] = scratch[...].reshape(plan.peers, plan.message, LANES).astype(BF)
 
 
-def read_wire(plan, wire_ref, ghi, glo, scratch):
+def read_wire(plan, wire_ref, tab, scratch):
     scratch[...] = wire_ref[...].astype(F32).reshape(plan.lat, plan.ch, plan.message, LANES)
     count = plan.lat * plan.main
     half = count + plan.lat * plan.left
@@ -204,7 +207,8 @@
         im = jnp.where(low, swap(a), b)
         tiles.append(jnp.concatenate([re, im], 0).astype(BF))
     right = jnp.concatenate(tiles, 1)
-    return dot(ghi[...], right) + dot(glo[...], right)
+    ghi, glo = tab[2, : plan.tokens, : 2 * half], tab[3, : plan.tokens, : 2 * half]
+    return dot(ghi, right) + dot(glo, right)
 
 
 def pack(values):
@@ -266,18 +270,19 @@
     return copies
 
 
-def parts_kernel(me_ref, up_ref, down_ref, up_out, near_out, rest_out, *refs):
+def parts_kernel(up_ref, down_ref, up_out, own_out, rest_out, *refs):
     mids, sem = refs[:3], refs[3]
-    half, third = up_out.shape[1], near_out.shape[0]
-    at = pl.multiple_of(me_ref[2] * half, LANES)
-    to = pl.multiple_of(me_ref[2] * third, LANES)
+    half, own = up_out.shape[1], own_out.shape[0]
+    side = lax.axis_index("lat") % 2
+    at = pl.multiple_of(side * half, LANES)
+    to = pl.multiple_of(side * own, LANES)
     into = fetch(
-        [up_ref.at[:, pl.ds(at, half)], down_ref.at[pl.ds(to, third), :], down_ref.at[2 * third :, :]],
+        [up_ref.at[:, pl.ds(at, half)], down_ref.at[pl.ds(to, own), :], down_ref.at[2 * own :, :]],
         mids,
         sem,
     )
     away = []
-    for n, out in enumerate((up_out, near_out, rest_out)):
+    for n, out in enumerate((up_out, own_out, rest_out)):
         into[n].wait()
         away.append(pltpu.make_async_copy(mids[n], out, sem.at[3 + n]))
         away[n].start()
@@ -285,12 +290,10 @@
         copy.wait()
 
 
-def prep_kernel(plan, me_ref, rowv, colv, rowt, colt, fin, finb, fout, foutb, *refs):
-    count = len(refs) // 2
-    outs, (chi, clo, ehi, elo, w1h, w1l, w2h, w2l, b1, b2) = refs[:count], refs[count:-1]
-    sem = refs[-1]
-    copies = [pltpu.make_async_copy(a, b, sem.at[n]) for n, (a, b) in enumerate(zip(refs[count:], outs))]
-    first = (me_ref[0] * plan.per).astype(F32)
+def table_kernel(plan, rowv, colv, rowt, colt, *refs):
+    outs, (chi, clo, ehi, elo), sem = refs[:4], refs[4:8], refs[8]
+    copies = [pltpu.make_async_copy(a, b, sem.at[n]) for n, (a, b) in enumerate(zip(refs[4:8], outs))]
+    first = (lax.axis_index("lat") * plan.per).astype(F32)
     size = plan.modes
     wide = plan.peers * (plan.main + plan.left)
     rows = [rowv[:, n : n + 1] for n in range(4)]
@@ -307,6 +310,13 @@
     ehi[:, size:], elo[:, size:] = split(-sin * doubled)
     copies[2].start()
     copies[3].start()
+    for copy in copies:
+        copy.wait()
+
+
+def block_kernel(plan, fin, finb, fout, foutb, *refs):
+    outs, (w1h, w1l, w2h, w2l, b1, b2), sem = refs[:6], refs[6:12], refs[12]
+    copies = [pltpu.make_async_copy(a, b, sem.at[n]) for n, (a, b) in enumerate(zip(refs[6:12], outs))]
     for weights, bias, high, low, out in ((fin, finb, w1h, w1l, b1), (fout, foutb, w2h, w2l, b2)):
         blocks, channels = weights.shape[1], weights.shape[2]
         full = []
@@ -332,14 +342,15 @@
         for v in range(plan.units):
             cells += [line[:, v * HALF : (v + 1) * HALF] for line in lines]
         out[...] = jnp.concatenate(cells, 1)
-    for copy in copies[4:]:
+    for copy in copies:
         copy.start()
     for copy in copies:
         copy.wait()
 
 
-def start_kernel(plan, me_ref, got_ref, tab_hbm, sum_hbm, wire_ref, par_hbm, *refs):
-    scratch, tab, sum_ref, par_ref, sem = refs
+def start_kernel(plan, got_ref, tab_hbm, begun_hbm, wire_ref, *refs):
+    scratch, tab, begun, sem = refs
+    sum_ref, par_ref = begun.at[: plan.tokens], begun.at[plan.tokens :]
     bias_ref = par_ref.at[8:16]
     copies = fetch([tab_hbm], [tab], sem)
     got = [unpack(got_ref[c]) for c in range(plan.ch)]
@@ -353,7 +364,7 @@
     par_ref[5:8, :] = jnp.zeros((3, D), F32)
     bias_ref[...] = jnp.zeros(bias_ref.shape, F32)
     for s in range(plan.ch):
-        source = unpack(got_ref[me_ref[1] ^ s])
+        source = unpack(got_ref[lax.axis_index("ch") ^ s])
         parts = [source[rows[5 + n] : rows[5 + n] + 1, :] for n in range(plan.ch)]
         line = jnp.concatenate(parts, 1)
         bias_ref[s : s + 1, :] = line
@@ -361,29 +372,26 @@
     values = jnp.where(inside, full, 0.0)
     normed = norm(values, par_ref[0:1, :], par_ref[2:3, :])
     sum_ref[...] = values + normed
-    copies.append(pltpu.make_async_copy(sum_ref, sum_hbm, sem.at[1]))
-    copies.append(pltpu.make_async_copy(par_ref, par_hbm, sem.at[2]))
+    copies.append(pltpu.make_async_copy(begun, begun_hbm, sem.at[1]))
     copies[1].start()
-    copies[2].start()
     copies[0].wait()
-    emit_wire(plan, normed, tab.at[0], tab.at[1], wire_ref, scratch)
+    emit_wire(plan, normed, tab, wire_ref, scratch)
     copies[1].wait()
-    copies[2].wait()
 
 
 def token_kernel(plan, first, last, *refs):
     copies = []
     if first:
-        me_ref, wire_in = refs[:2]
-        sources, refs = refs[2:20], refs[20:]
-        (sum_out, wire_out, up_all, down_all), refs = refs[:4], refs[4:]
-        scratch, sem, (sum_in, ahead, behind, par_ref) = refs[0], refs[1], refs[2:]
+        wire_in, sources, refs = refs[0], refs[1:17], refs[17:]
+        (sum_out, wire_out, par_out, up_all, down_all), refs = refs[:5], refs[5:]
+        scratch, sem, (begun, tab) = refs[0], refs[1], refs[2:]
+        sum_in, par_ref = begun.at[: plan.tokens], begun.at[plan.tokens :]
         shard = up_all.shape[1] // plan.ch
-        half, third = shard // 2, shard // 3
-        y = me_ref[2]
-        copies = fetch(sources[:4], (sum_in, ahead, behind, par_ref), sem)
+        half, own = shard // 2, shard // 6
+        y = lax.axis_index("lat") % 2
+        copies = fetch(sources[:2], (begun, tab), sem)
         groups = []
-        weights = sources[4:]
+        weights = sources[2:]
         for s in range(plan.ch):
             at = s * shard
             if s < plan.ch // 2:
@@ -395,9 +403,12 @@
                 ups, downs = weights[:2], weights[2:5]
                 spots = [pl.multiple_of(at + n * half, LANES) for n in (y, 1 - y)]
                 ups = [(w, up_all.at[:, pl.ds(n, half)]) for w, n in zip(ups, spots)]
-                spots = [pl.multiple_of(at + n * third, LANES) for n in (y, 1 - y)]
-                spots.append(at + 2 * third)
-                downs = [(w, down_all.at[pl.ds(n, third), :]) for w, n in zip(downs, spots)]
+                spots = [pl.multiple_of(at + n * own, LANES) for n in (y, 1 - y)]
+                spots.append(at + 2 * own)
+                sizes = (own, own, shard - 2 * own)
+                downs = [
+                    (w, down_all.at[pl.ds(n, size), :]) for w, n, size in zip(downs, spots, sizes)
+                ]
                 weights = weights[5:]
             group = []
             for source, target in ups + downs:
@@ -406,14 +417,15 @@
                 copies[-1].start()
                 group.append(copies[-1])
             groups.append(group)
-        for copy in copies[:4]:
+        for copy in copies[:2]:
             copy.wait()
+        par_out[...] = par_ref[...]
     else:
-        wire_in, sum_in, ahead, behind, par_ref, up_all, down_all = refs[:7]
-        outs, scratch = refs[7:-1], refs[-1]
+        wire_in, sum_in, tab, par_ref, up_all, down_all = refs[:6]
+        outs, scratch = refs[6:-1], refs[-1]
         shard = up_all.shape[1] // plan.ch
         half = shard // 2
-    values = sum_in[...] + read_wire(plan, wire_in, behind.at[0], behind.at[1], scratch)
+    values = sum_in[...] + read_wire(plan, wire_in, tab, scratch)
     normed = norm(values, par_ref[1:2, :], par_ref[3:4, :]).astype(BF)
     mixed = par_ref[4:5, :]
     for s in range(2 * plan.ch):
@@ -435,7 +447,7 @@
         sum_out, wire_out = outs
     normed = norm(values, par_ref[0:1, :], par_ref[2:3, :])
     sum_out[...] = values + normed
-    emit_wire(plan, normed, ahead.at[0], ahead.at[1], wire_out, scratch)
+    emit_wire(plan, normed, tab, wire_out, scratch)
 
 
 def spectral_kernel(plan, far, wire_in, *refs):
@@ -505,7 +517,7 @@
     wire_out[...] = scratch[...].astype(BF)
 
 
-def call(body, outs, operands, scratch, flops, smem=0, far_in=0, far_out=(), grant=20):
+def call(body, outs, operands, scratch, flops, far_in=0, far_out=(), grant=20):
     vmem = pl.BlockSpec(memory_space=pltpu.VMEM)
     anywhere = pl.BlockSpec(memory_space=pl.ANY)
     flat, tree = jax.tree.flatten(outs)
@@ -513,9 +525,7 @@
     return pl.pallas_call(
         body,
         out_shape=outs,
-        in_specs=[pl.BlockSpec(memory_space=pltpu.SMEM)] * smem
-        + [vmem] * (len(operands) - smem - far_in)
-        + [anywhere] * far_in,
+        in_specs=[vmem] * (len(operands) - far_in) + [anywhere] * far_in,
         out_specs=jax.tree.unflatten(tree, out_specs),
         scratch_shapes=scratch,
         compiler_params=pltpu.CompilerParams(vmem_limit_bytes=grant * 2**20),
@@ -541,8 +551,6 @@
     far = ch // 2
     both = ("lat", "ch")
     assert plan.spare * rows >= 5 + ch and up_bias.shape[0] == ch * wide
-    lat_me = lax.axis_index("lat").astype(jnp.int32)
-    me = jnp.stack([lat_me, lax.axis_index("ch").astype(jnp.int32), lat_me % 2])
 
     def across(value, step):
         return lax.ppermute(value, "ch", [(i, i ^ step) for i in range(ch)])
@@ -567,31 +575,39 @@
         + [pltpu.SemaphoreType.DMA((3,))],
         10**8,
         far_in=3,
-        grant=58,
+        grant=PACK,
     )
     got = exchange(tokens, "ch")
 
-    half, third = up_weight.shape[1] // 2, down_weight.shape[0] // 3
-    parts = [
-        jax.ShapeDtypeStruct((up_weight.shape[0], half), BF),
-        jax.ShapeDtypeStruct((third, down_weight.shape[1]), BF),
-        jax.ShapeDtypeStruct((third, down_weight.shape[1]), BF),
-    ]
-    up_part, near_part, rest_part = call(
+    half, own = up_weight.shape[1] // 2, down_weight.shape[0] // 6
+    shapes = [(D, half), (own, D), (down_weight.shape[0] - 2 * own, D)]
+    parts = [jax.ShapeDtypeStruct(shape, BF) for shape in shapes]
+    up_part, own_part, rest_part = call(
         parts_kernel,
         tuple(parts),
-        (me, up_weight, down_weight),
+        (up_weight, down_weight),
         [pltpu.VMEM(t.shape, BF) for t in parts] + [pltpu.SemaphoreType.DMA((6,))],
         10**6,
-        smem=1,
         far_in=2,
         far_out=(0, 1, 2),
         grant=58,
     )
     up_a = across(up_part, far)
+    blocks = [jax.ShapeDtypeStruct((2 * wide, 2 * wide), BF)] * 4
+    blocks += [jax.ShapeDtypeStruct((1, 2 * wide), F32)] * 2
+    blocks = call(
+        lambda *r: block_kernel(plan, *r),
+        tuple(blocks),
+        (filter_in, filter_in_bias, filter_out, filter_out_bias),
+        [pltpu.VMEM(t.shape, t.dtype) for t in blocks] + [pltpu.SemaphoreType.DMA((6,))],
+        10**8,
+        far_out=range(6),
+        grant=58,
+    )
+    got, *blocks = lax.optimization_barrier((got, *blocks))
     up_c, down_c = across(up_weight, 1), across(down_weight, 1)
 
-    ahead, behind = (jnp.asarray(table) for table in short_tables(plan))
+    short = jnp.asarray(short_tables(plan))
     odd = np.tile(np.repeat(np.arange(plan.slots) % 2, plan.height), plan.per)
     sign = np.where((odd[:, None] == 1) & (np.arange(LANES)[None] >= HALF), -1.0, 1.0)
     sign = sign.astype(np.float32)
@@ -599,43 +615,39 @@
     wire = jax.ShapeDtypeStruct((plan.peers, plan.message, LANES), BF)
     held = jax.ShapeDtypeStruct((plan.tokens, D), F32)
     scratch = [pltpu.VMEM((plan.lat, ch, plan.message, LANES), F32)]
-    params = jax.ShapeDtypeStruct((16, D), F32)
-    total, sent, params = call(
+    begun = jax.ShapeDtypeStruct((plan.tokens + 16, D), F32)
+    begun, sent = call(
         lambda *r: start_kernel(plan, *r),
-        (held, wire, params),
-        (me, got, ahead),
+        (begun, wire),
+        (got, short),
         scratch
-        + [pltpu.VMEM(t.shape, t.dtype) for t in (ahead, held, params)]
-        + [pltpu.SemaphoreType.DMA((3,))],
+        + [pltpu.VMEM(t.shape, t.dtype) for t in (short, begun)]
+        + [pltpu.SemaphoreType.DMA((2,))],
         10**9,
-        smem=1,
         far_in=1,
-        far_out=(0, 2),
-        grant=58,
+        far_out=(0,),
+        grant=START,
     )
     row, col = mode_places(plan)
     lines = plan.peers * (plan.main + plan.left)
-    tables = [
-        jax.ShapeDtypeStruct(dims, BF)
-        for dims in [(plan.modes, 2 * lines)] * 2
-        + [(lines, 2 * plan.modes)] * 2
-        + [(2 * wide, 2 * wide)] * 4
-    ] + [jax.ShapeDtypeStruct((1, 2 * wide), F32)] * 2
-    spectral_in = call(
-        lambda *r: prep_kernel(plan, *r),
+    dims = [(plan.modes, 2 * lines)] * 2 + [(lines, 2 * plan.modes)] * 2
+    tables = [jax.ShapeDtypeStruct(shape, BF) for shape in dims]
+    made = call(
+        lambda *r: table_kernel(plan, *r),
         tuple(tables),
-        (after(me, sent), row.T, col, row, col.T, filter_in, filter_in_bias, filter_out, filter_out_bias),
-        [pltpu.VMEM(t.shape, t.dtype) for t in tables] + [pltpu.SemaphoreType.DMA((len(tables),))],
+        (after(jnp.asarray(row.T), sent), col, row, col.T),
+        [pltpu.VMEM(t.shape, t.dtype) for t in tables] + [pltpu.SemaphoreType.DMA((4,))],
         10**8,
-        smem=1,
-        far_out=range(len(tables)),
+        far_out=range(4),
         grant=58,
     )
+    spectral_in = (*made, *blocks)
     for step_index in range(STEPS):
         first, last = step_index == 0, step_index == STEPS - 1
         arrived = exchange(sent, both)
         if first:
-            down_a = across(near_part, far)
+            down_a = across(own_part, far)
+            rest = across(rest_part, far)
             up_b = beside(up_a)
             up_ac = across(up_a, 1)
         tabs = (*spectral_in, sign)
@@ -649,42 +661,41 @@
             + mids,
             10**9,
             far_in=len(mids),
-            grant=58 if first else 20,
+            grant=FIRST if first else 20,
         )
         if first:
+            up_bc = across(after(up_b, sent), 1)
             down_b = beside(after(down_a, sent))
             down_ac = across(after(down_a, sent), 1)
-            up_bc = across(after(up_b, sent), 1)
-            rest = across(rest_part, far)
+            rest_c = across(after(rest, sent), 1)
         arrived = exchange(sent, both)
         if first:
             down_bc = across(after(down_b, arrived), 1)
-            rest_c = across(after(rest, arrived), 1)
             near = (up_weight, down_weight, up_c, down_c)
             distant = (up_a, up_b, down_a, down_b, rest, up_ac, up_bc, down_ac, down_bc, rest_c)
-            sources = (total, ahead, behind, params, *near, *distant)
-            total, sent, ups, downs = call(
+            sources = (begun, short, *near, *distant)
+            total, sent, params, ups, downs = call(
                 lambda *r: token_kernel(plan, True, False, *r),
                 (
                     held,
                     wire,
+                    jax.ShapeDtypeStruct((16, D), F32),
                     jax.ShapeDtypeStruct((D, ch * up_weight.shape[1]), BF),
                     jax.ShapeDtypeStruct((ch * down_weight.shape[0], D), BF),
                 ),
-                (me, arrived, *sources),
+                (arrived, *sources),
                 scratch
                 + [pltpu.SemaphoreType.DMA((len(sources),))]
-                + [pltpu.VMEM(t.shape, t.dtype) for t in sources[:4]],
+                + [pltpu.VMEM(t.shape, t.dtype) for t in sources[:2]],
                 10**10,
-                smem=1,
-                far_in=len(sources),
+                        far_in=len(sources),
                 grant=24,
             )
             continue
         result = call(
             lambda *r: token_kernel(plan, False, last, *r),
             message if last else (held, wire),
-            (arrived, total, ahead, behind, params, ups, downs),
+            (arrived, total, short, params, ups, downs),
             scratch,
             10**10,
         )

time: 188 us -> 188 us (level)
  waiting for transfers between devices: 17.5 us -> 25.7 us
  Pallas kernels: 45.4 us -> 42.2 us
  blocking collectives: 89 us -> 87 us
    all_to_all x3, waiting for transfers between devices: 10.6 us -> 22.8 us  [exchange(): return lax.all_to_all(value, axes, 0, 0, tiled=True)]
    pallas_call x13 -> x14, Pallas kernels: 45.4 us -> 42.2 us  [call(): pl.pallas_call(body, out_shape=outs, in_specs=[vmem] * (len(operands) - f...]
    ppermute x2, waiting for transfers between devices: 3.72 us -> 1.28 us  [beside(): return lax.ppermute(value, 'lat', [(i, i ^ 1) for i in range(plan.lat)])]
    ppermute x2, starting transfers between devices: 4.46 us -> 2.22 us  [beside(): return lax.ppermute(value, 'lat', [(i, i ^ 1) for i in range(plan.lat)])]
    all_to_all x7, blocking collectives: 89 us -> 87 us  [exchange(): return lax.all_to_all(value, axes, 0, 0, tiled=True)]
    unnamed x41 -> x49, local copies, waits for them, and re-layouts: 5.26 us -> 5.6 us
  transfers between devices with their start and end apart: 15 -> 15, of which waited for: 8 -> 6; matrix products, arithmetic and copies ran while one was open for 0% -> 0% of each run, Pallas kernels for 9% -> 8%
where the time goes in v2:
time: 188 us; the launch traced here: 187 us
  blocking collectives  87 us (46%)
  Pallas kernels  42.2 us (22%)
  waiting for transfers between devices  25.7 us (14%)
  starting transfers between devices  24.8 us (13%)
  local copies, waits for them, and re-layouts  6.98 us (4%)
    all_to_all x7, blocking collectives, exchange(): return lax.all_to_all(value, axes, 0, 0, tiled=True)  87 us
    pallas_call x14, Pallas kernels, call(): pl.pallas_call(body, out_shape=outs, in_specs=[vmem] * (len(operands) - f...  42.2 us
    all_to_all x3, waiting for transfers between devices, exchange(): return lax.all_to_all(value, axes, 0, 0, tiled=True)  22.8 us
    all_to_all x3, starting transfers between devices, exchange(): return lax.all_to_all(value, axes, 0, 0, tiled=True)  15.2 us
    ppermute x10, starting transfers between devices, across(): return lax.ppermute(value, 'ch', [(i, i ^ step) for i in range(ch)])  7.37 us
    unnamed x49, local copies, waits for them, and re-layouts  5.6 us
  transfers between devices with their start and end apart: 15, of which 6 were waited for; matrix products, arithmetic and copies ran while one was open for 0% of the time, Pallas kernels for 8%

profile of v2, /device:TPU:0, one launch (start us, length us, event | category | flops | bytes accessed | tf_op | source)
XLA Modules:
  0.0 187.1 jit_solution(9596176280273855866)
XLA Ops:
  0.0 2.4 %shard_map.159 = (bf16[768,384]{1,0:T(8,128)(2,1)}, bf16[128,768]{1,0:T(8,128)(2,1)}, bf16[512,768]{1,0:T(8,128)(2,1)}) custom-call(bf16[768,768]{1,0:T(8,128)(2,1)} %r_3_.4, bf16[768,768]{1,0:T(8,128)(2,1)} %r_4_.1), custom_call_target="tpu_custom_call" | custom-call | flops 1000000 | bytes 1048576 | tf_op jit(solution)/shard_map/pallas_call | solution.py:525
  2.4 3.0 %collective-permute-start.2 = (bf16[768,384]{1,0:T(8,128)(2,1)}, bf16[768,384]{1,0:T(8,128)(2,1)S(1)}, u32[]{:S(2)}, u32[]{:S(2)}) collective-permute-start(bf16[768,384]{1,0:T(8,128)(2,1)} %get-tuple-element.61), channel_id=1, source_target_pairs={{0,2},{1,3},{2,0},{3,1},{4,6},{5,7},{6,4},{7,5},{8,10},{9,11},{10,... | collective-permute-start | bytes 1769480 | tf_op jit(solution)/shard_map/ppermute | solution.py:556
  6.5 3.5 %all-to-all-start = ((f32[4,216,128]{2,1,0:T(8,128)}), f32[4,216,128]{2,1,0:T(8,128)S(1)}, u32[]{:S(2)}, u32[]{:S(2)}) async-start(f32[4,216,128]{2,1,0:T(8,128)} %shard_map.154), calls=%async_computation | async-start | bytes 884736 | tf_op jit(solution)/shard_map/all_to_all | solution.py:562
  10.0 2.0 %collective-permute-start.6 = (bf16[512,768]{1,0:T(8,128)(2,1)}, bf16[512,768]{1,0:T(8,128)(2,1)}, u32[]{:S(2)}, u32[]{:S(2)}) collective-permute-start(bf16[512,768]{1,0:T(8,128)(2,1)} %get-tuple-element.64), channel_id=1, source_target_pairs={{0,2},{1,3},{2,0},{3,1},{4,6},{5,7},{6,4},{7,5},{8,10},{9,11},{10,... | collective-permute-start | bytes 2359304 | tf_op jit(solution)/shard_map/ppermute | solution.py:556
  12.0 2.4 %shard_map.155 = (bf16[384,384]{1,0:T(8,128)(2,1)}, bf16[384,384]{1,0:T(8,128)(2,1)}, bf16[384,384]{1,0:T(8,128)(2,1)}, bf16[384,384]{1,0:T(8,128)(2,1)}, f32[1,384]{1,0:T(1,128)}, /*index=5*/f32[1,384]{1,0:T(1,128)}) custom-call(f32[2,2,96,96]{3,2,1,0:T(8,128)} %r_0_.1, f32[2,2,96]{2,1,0:T(2,128)} %r_1_.5, f32[2,2,96,96]{3,2,1,0:T(8,128)} %r_2_.8, ...), custom_call_target="tpu_custom_call" | custom-call | flops 100000000 | bytes 1048576 | tf_op jit(solution)/shard_map/pallas_call | solution.py:525
  14.4 10.2 %all-to-all-done.r_0_ = f32[4,216,128]{2,1,0:T(8,128)S(1)} async-done(((f32[4,216,128]{2,1,0:T(8,128)}), f32[4,216,128]{2,1,0:T(8,128)S(1)}, u32[]{:S(2)}, u32[]{:S(2)}) %all-to-all-start) | async-done | bytes 442400 | tf_op jit(solution)/shard_map/all_to_all | solution.py:562
  25.5 2.0 %shard_map.156 = (f32[160,768]{1,0:T(8,128)S(1)}, bf16[32,32,128]{2,1,0:T(8,128)(2,1)}) custom-call(f32[4,216,128]{2,1,0:T(8,128)S(1)} %all-to-all-done.r_0_, bf16[4,144,144]{2,1,0:T(8,128)(2,1)S(1)} %copy-done.12), custom_call_target="tpu_custom_call" | custom-call | flops 1000000000 | bytes 1048576 | tf_op jit(solution)/shard_map/pallas_call | solution.py:525
  28.3 6.4 %all-to-all-start.1 = ((bf16[32,32,128]{2,1,0:T(8,128)(2,1)}), bf16[32,32,128]{2,1,0:T(8,128)(2,1)S(1)}, u32[]{:S(2)}, u32[]{:S(2)}) async-start(bf16[32,32,128]{2,1,0:T(8,128)(2,1)} %get-tuple-element.48), calls=%async_computation.1 | async-start | bytes 524288 | tf_op jit(solution)/shard_map/all_to_all | solution.py:562
  35.0 1.6 collective-permute-start.3
  36.8 1.5 collective-permute-start.4
  38.2 3.9 %shard_map.157 = (bf16[216,576]{1,0:T(8,128)(2,1)}, bf16[216,576]{1,0:T(8,128)(2,1)}, bf16[288,432]{1,0:T(8,128)(2,1)}, bf16[288,432]{1,0:T(8,128)(2,1)}) custom-call(f32[216,8]{1,0:T(8,128)} %constant.13.clone.r_0_, f32[8,288]{1,0:T(8,128)} %constant.14.clone.r_1_, f32[8,216]{1,0:T(8,128)} %constant.15.clone.r_2_, f32[288,8]{1,0:T(8,128)} %constant.16.clone.r_3_), custom_call_target="tpu_custom_call" | custom-call | flops 100000000 | bytes 1048576 | tf_op jit(solution)/shard_map/pallas_call | solution.py:525
  42.1 3.6 %all-to-all-done.1.r_0_ = bf16[32,32,128]{2,1,0:T(8,128)(2,1)S(1)} async-done(((bf16[32,32,128]{2,1,0:T(8,128)(2,1)}), bf16[32,32,128]{2,1,0:T(8,128)(2,1)S(1)}, u32[]{:S(2)}, u32[]{:S(2)}) %all-to-all-start.1) | async-done | bytes 262176 | tf_op jit(solution)/shard_map/all_to_all | solution.py:562
  46.4 6.1 %shard_map.158 = bf16[32,32,128]{2,1,0:T(8,128)(2,1)} custom-call(bf16[32,32,128]{2,1,0:T(8,128)(2,1)} %copy-done.22, bf16[216,576]{1,0:T(8,128)(2,1)} %get-tuple-element.50.r_1_, bf16[216,576]{1,0:T(8,128)(2,1)} %get-tuple-element.51.r_2_, bf16[288,432]{1,0:T(8,128)(2,1)} %get-tuple-element.52.r_3_, bf16[288,432]{1,0:T(8,128)(2,1)} %get-tuple-element.53.r_4_, ...), custom_call_target="tpu_custom_call" | custom-call | flops 1000000000 | bytes 1048576 | tf_op jit(solution)/shard_map/pallas_call | solution.py:525
  53.3 5.4 %all-to-all-start.2 = ((bf16[32,32,128]{2,1,0:T(8,128)(2,1)}), bf16[32,32,128]{2,1,0:T(8,128)(2,1)S(1)}, u32[]{:S(2)}, u32[]{:S(2)}) async-start(bf16[32,32,128]{2,1,0:T(8,128)(2,1)} %shard_map.158), calls=%async_computation.2 | async-start | bytes 524288 | tf_op jit(solution)/shard_map/all_to_all | solution.py:562
  59.0 1.2 collective-permute-done.5.r_10_
  60.2 9.1 %all-to-all-done.2.r_0_ = bf16[32,32,128]{2,1,0:T(8,128)(2,1)S(1)} async-done(((bf16[32,32,128]{2,1,0:T(8,128)(2,1)}), bf16[32,32,128]{2,1,0:T(8,128)(2,1)S(1)}, u32[]{:S(2)}, u32[]{:S(2)}) %all-to-all-start.2) | async-done | bytes 262176 | tf_op jit(solution)/shard_map/all_to_all | solution.py:562
  69.3 1.6 collective-permute-done.10.r_15_
  74.1 5.8 %shard_map.160 = (f32[144,768]{1,0:T(8,128)S(1)}, bf16[32,32,128]{2,1,0:T(8,128)(2,1)S(1)}, f32[16,768]{1,0:T(8,128)S(1)}, bf16[768,3072]{1,0:T(8,128)(2,1)S(1)}, bf16[3072,768]{1,0:T(8,128)(2,1)S(1)}) custom-call(bf16[32,32,128]{2,1,0:T(8,128)(2,1)S(1)} %all-to-all-done.2.r_0_, f32[160,768]{1,0:T(8,128)S(1)} %copy-done.20, ...), custom_call_target="tpu_custom_call" | custom-call | flops 10000000000 | bytes 1048576 | tf_op jit(solution)/shard_map/pallas_call | solution.py:525
  79.9 12.8 %all_to_all.50.r_0_ = bf16[32,32,128]{2,1,0:T(8,128)(2,1)S(1)} all-to-all(bf16[32,32,128]{2,1,0:T(8,128)(2,1)S(1)} %get-tuple-element.68), channel_id=1, replica_groups=mesh['lat'=8,'ch'=4] {'lat','ch'}, dimensions={0} | all-to-all | bytes 524288 | tf_op jit(solution)/shard_map/all_to_all | solution.py:562
  92.7 2.4 %shard_map.161 = bf16[32,32,128]{2,1,0:T(8,128)(2,1)S(1)} custom-call(bf16[32,32,128]{2,1,0:T(8,128)(2,1)S(1)} %all_to_all.50.r_0_, bf16[216,576]{1,0:T(8,128)(2,1)S(1)} %copy-done.17, bf16[216,576]{1,0:T(8,128)(2,1)S(1)} %copy-done.18, bf16[288,432]{1,0:T(8,128)(2,1)S(1)} %copy-done.15, bf16[288,432]{1,0:T(8,128)(2,1)S(1)} %copy-done.16, ...), custom_call_target="tpu_custom_call" | custom-call | flops 1000000000 | bytes 1048576 | tf_op jit(solution)/shard_map/pallas_call | solution.py:525
  95.2 12.8 %all_to_all.51.r_0_ = bf16[32,32,128]{2,1,0:T(8,128)(2,1)S(1)} all-to-all(bf16[32,32,128]{2,1,0:T(8,128)(2,1)S(1)} %shard_map.161), channel_id=1, replica_groups=mesh['lat'=8,'ch'=4] {'lat','ch'}, dimensions={0} | all-to-all | bytes 524288 | tf_op jit(solution)/shard_map/all_to_all | solution.py:562
  107.9 3.9 %shard_map.162 = (f32[144,768]{1,0:T(8,128)S(1)}, bf16[32,32,128]{2,1,0:T(8,128)(2,1)S(1)}) custom-call(bf16[32,32,128]{2,1,0:T(8,128)(2,1)S(1)} %all_to_all.51.r_0_, f32[144,768]{1,0:T(8,128)S(1)} %get-tuple-element.69.r_1_, bf16[4,144,144]{2,1,0:T(8,128)(2,1)S(1)} %copy-done.13, f32[16,768]{1,0:T(8,128)S(1)} %get-tuple-element.70.r_3_, ...), custom_call_target="tpu_custom_call" | custom-call | flops 10000000000 | bytes 1048576 | tf_op jit(solution)/shard_map/pallas_call | solution.py:525
  111.9 12.8 %all_to_all.52.r_0_ = bf16[32,32,128]{2,1,0:T(8,128)(2,1)S(1)} all-to-all(bf16[32,32,128]{2,1,0:T(8,128)(2,1)S(1)} %get-tuple-element.73), channel_id=1, replica_groups=mesh['lat'=8,'ch'=4] {'lat','ch'}, dimensions={0} | all-to-all | bytes 524288 | tf_op jit(solution)/shard_map/all_to_all | solution.py:562
  124.6 2.4 %shard_map.163 = bf16[32,32,128]{2,1,0:T(8,128)(2,1)S(1)} custom-call(bf16[32,32,128]{2,1,0:T(8,128)(2,1)S(1)} %all_to_all.52.r_0_, bf16[216,576]{1,0:T(8,128)(2,1)S(1)} %copy-done.17, bf16[216,576]{1,0:T(8,128)(2,1)S(1)} %copy-done.18, bf16[288,432]{1,0:T(8,128)(2,1)S(1)} %copy-done.15, bf16[288,432]{1,0:T(8,128)(2,1)S(1)} %copy-done.16, ...), custom_call_target="tpu_custom_call" | custom-call | flops 1000000000 | bytes 1048576 | tf_op jit(solution)/shard_map/pallas_call | solution.py:525
  127.1 12.8 %all_to_all.53.r_0_ = bf16[32,32,128]{2,1,0:T(8,128)(2,1)S(1)} all-to-all(bf16[32,32,128]{2,1,0:T(8,128)(2,1)S(1)} %shard_map.163), channel_id=1, replica_groups=mesh['lat'=8,'ch'=4] {'lat','ch'}, dimensions={0} | all-to-all | bytes 524288 | tf_op jit(solution)/shard_map/all_to_all | solution.py:562
  139.8 3.9 %shard_map.164 = (f32[144,768]{1,0:T(8,128)S(1)}, bf16[32,32,128]{2,1,0:T(8,128)(2,1)S(1)}) custom-call(bf16[32,32,128]{2,1,0:T(8,128)(2,1)S(1)} %all_to_all.53.r_0_, f32[144,768]{1,0:T(8,128)S(1)} %get-tuple-element.74.r_1_, bf16[4,144,144]{2,1,0:T(8,128)(2,1)S(1)} %copy-done.13, f32[16,768]{1,0:T(8,128)S(1)} %get-tuple-element.70.r_3_, ...), custom_call_target="tpu_custom_call" | custom-call | flops 10000000000 | bytes 1048576 | tf_op jit(solution)/shard_map/pallas_call | solution.py:525
  143.7 12.8 %all_to_all.54.r_0_ = bf16[32,32,128]{2,1,0:T(8,128)(2,1)S(1)} all-to-all(bf16[32,32,128]{2,1,0:T(8,128)(2,1)S(1)} %get-tuple-element.75), channel_id=1, replica_groups=mesh['lat'=8,'ch'=4] {'lat','ch'}, dimensions={0} | all-to-all | bytes 524288 | tf_op jit(solution)/shard_map/all_to_all | solution.py:562
  156.5 2.4 %shard_map.165 = bf16[32,32,128]{2,1,0:T(8,128)(2,1)S(1)} custom-call(bf16[32,32,128]{2,1,0:T(8,128)(2,1)S(1)} %all_to_all.54.r_0_, bf16[216,576]{1,0:T(8,128)(2,1)S(1)} %copy-done.17, bf16[216,576]{1,0:T(8,128)(2,1)S(1)} %copy-done.18, bf16[288,432]{1,0:T(8,128)(2,1)S(1)} %copy-done.15, bf16[288,432]{1,0:T(8,128)(2,1)S(1)} %copy-done.16, ...), custom_call_target="tpu_custom_call" | custom-call | flops 1000000000 | bytes 1048576 | tf_op jit(solution)/shard_map/pallas_call | solution.py:525
  159.0 12.8 %all_to_all.55.r_0_ = bf16[32,32,128]{2,1,0:T(8,128)(2,1)S(1)} all-to-all(bf16[32,32,128]{2,1,0:T(8,128)(2,1)S(1)} %shard_map.165), channel_id=1, replica_groups=mesh['lat'=8,'ch'=4] {'lat','ch'}, dimensions={0} | all-to-all | bytes 524288 | tf_op jit(solution)/shard_map/all_to_all | solution.py:562
  171.7 3.5 %shard_map.166 = f32[4,216,128]{2,1,0:T(8,128)S(1)} custom-call(bf16[32,32,128]{2,1,0:T(8,128)(2,1)S(1)} %all_to_all.55.r_0_, f32[144,768]{1,0:T(8,128)S(1)} %get-tuple-element.76.r_1_, bf16[4,144,144]{2,1,0:T(8,128)(2,1)S(1)} %copy-done.13, f32[16,768]{1,0:T(8,128)S(1)} %get-tuple-element.70.r_3_, bf16[768,3072]{1,0:T(8,128)(2,1)S(1)} %get-tuple-element.71.r_4_, ...), custom_call_target="tpu_custom_call" | custom-call | flops 10000000000 | bytes 1048576 | tf_op jit(solution)/shard_map/pallas_call | solution.py:525
  175.2 10.3 %all_to_all.56.r_0_ = f32[4,216,128]{2,1,0:T(8,128)S(1)} all-to-all(f32[4,216,128]{2,1,0:T(8,128)S(1)} %shard_map.166), channel_id=1, replica_groups=mesh['lat'=8,'ch'=4] {'ch'}, dimensions={0} | all-to-all | bytes 884736 | tf_op jit(solution)/shard_map/all_to_all | solution.py:562
  185.7 1.4 copy.17
  (70 shorter events, 8.4 us)
Async XLA Ops:
  0.0 5.4 %copy-start.21 = (f32[1,3,180,192]{3,0,2,1:T(1,128)S(1)}, f32[1,3,180,192]{3,0,2,1:T(1,128)}, u32[]{:S(2)}) copy-start(f32[1,3,180,192]{3,0,2,1:T(1,128)} %param.16) | copy-start | bytes 1244164
  0.0 5.5 %copy-start.2 = (bf16[3,192]{1,0:T(4,128)(2,1)S(1)}, bf16[3,192]{1,0:T(4,128)(2,1)}, u32[]{:S(2)}) copy-start(bf16[3,192]{1,0:T(4,128)(2,1)} %r_2_.7) | copy-start | bytes 3460
  0.0 5.5 %copy-start.3 = (bf16[2,192]{1,0:T(2,128)(2,1)S(1)}, bf16[2,192]{1,0:T(2,128)(2,1)}, u32[]{:S(2)}) copy-start(bf16[2,192]{1,0:T(2,128)(2,1)} %r_1_.4) | copy-start | bytes 2308
  2.4 32.6 %collective-permute-start.2 = (bf16[768,384]{1,0:T(8,128)(2,1)}, bf16[768,384]{1,0:T(8,128)(2,1)S(1)}, u32[]{:S(2)}, u32[]{:S(2)}) collective-permute-start(bf16[768,384]{1,0:T(8,128)(2,1)} %get-tuple-element.61), channel_id=1, source_target_pairs={{0,2},{1,3},{2,0},{3,1},{4,6},{5,7},{6,4},{7,5},{8,10},{9,11},{10,... | collective-permute-start | bytes 1769480 | tf_op jit(solution)/shard_map/ppermute | solution.py:556
  6.5 18.0 %all-to-all-start = ((f32[4,216,128]{2,1,0:T(8,128)}), f32[4,216,128]{2,1,0:T(8,128)S(1)}, u32[]{:S(2)}, u32[]{:S(2)}) async-start(f32[4,216,128]{2,1,0:T(8,128)} %shard_map.154), calls=%async_computation | async-start | bytes 884736 | tf_op jit(solution)/shard_map/all_to_all | solution.py:562
  10.0 42.5 %collective-permute-start.6 = (bf16[512,768]{1,0:T(8,128)(2,1)}, bf16[512,768]{1,0:T(8,128)(2,1)}, u32[]{:S(2)}, u32[]{:S(2)}) collective-permute-start(bf16[512,768]{1,0:T(8,128)(2,1)} %get-tuple-element.64), channel_id=1, source_target_pairs={{0,2},{1,3},{2,0},{3,1},{4,6},{5,7},{6,4},{7,5},{8,10},{9,11},{10,... | collective-permute-start | bytes 2359304 | tf_op jit(solution)/shard_map/ppermute | solution.py:556
  25.5 9.1 %copy-start = (bf16[768,768]{1,0:T(8,128)(2,1)S(1)}, bf16[768,768]{1,0:T(8,128)(2,1)}, u32[]{:S(2)}) copy-start(bf16[768,768]{1,0:T(8,128)(2,1)} %r_3_.4) | copy-start | bytes 3538948
  25.5 11.1 %copy-start.1 = (bf16[768,768]{1,0:T(8,128)(2,1)S(1)}, bf16[768,768]{1,0:T(8,128)(2,1)}, u32[]{:S(2)}) copy-start(bf16[768,768]{1,0:T(8,128)(2,1)} %r_4_.1) | copy-start | bytes 3538948
  28.3 17.4 %all-to-all-start.1 = ((bf16[32,32,128]{2,1,0:T(8,128)(2,1)}), bf16[32,32,128]{2,1,0:T(8,128)(2,1)S(1)}, u32[]{:S(2)}, u32[]{:S(2)}) async-start(bf16[32,32,128]{2,1,0:T(8,128)(2,1)} %get-tuple-element.48), calls=%async_computation.1 | async-start | bytes 524288 | tf_op jit(solution)/shard_map/all_to_all | solution.py:562
  34.7 34.6 %collective-permute-start = (bf16[768,768]{1,0:T(8,128)(2,1)S(1)}, bf16[768,768]{1,0:T(8,128)(2,1)}, u32[]{:S(2)}, u32[]{:S(2)}) collective-permute-start(bf16[768,768]{1,0:T(8,128)(2,1)S(1)} %copy-done), channel_id=1, source_target_pairs={{0,1},{1,0},{2,3},{3,2},{4,5},{5,4},{6,7},{7,6},{8,9},{9,8},{10,11... | collective-permute-start | bytes 3538952 | tf_op jit(solution)/shard_map/ppermute | solution.py:556
  35.0 17.5 %copy-start.4 = (bf16[768,384]{1,0:T(8,128)(2,1)}, bf16[768,384]{1,0:T(8,128)(2,1)S(1)}, u32[]{:S(2)}) copy-start(bf16[768,384]{1,0:T(8,128)(2,1)S(1)} %collective-permute-done.2.r_7_) | copy-start | bytes 1769476
  35.0 18.3 %collective-permute-start.3 = (bf16[768,384]{1,0:T(8,128)(2,1)S(1)}, bf16[768,384]{1,0:T(8,128)(2,1)}, u32[]{:S(2)}, u32[]{:S(2)}) collective-permute-start(bf16[768,384]{1,0:T(8,128)(2,1)S(1)} %collective-permute-done.2.r_7_), channel_id=1, source_target_pairs={{0,4},{4,0},{8,12},{12,8},{16,20},{20,16},{24,28},{28,24},{1,5},{5... | collective-permute-start | bytes 1769480 | tf_op jit(solution)/shard_map/ppermute | solution.py:559
  36.6 32.6 %collective-permute-start.1 = (bf16[768,768]{1,0:T(8,128)(2,1)S(1)}, bf16[768,768]{1,0:T(8,128)(2,1)}, u32[]{:S(2)}, u32[]{:S(2)}) collective-permute-start(bf16[768,768]{1,0:T(8,128)(2,1)S(1)} %copy-done.1), channel_id=1, source_target_pairs={{0,1},{1,0},{2,3},{3,2},{4,5},{5,4},{6,7},{7,6},{8,9},{9,8},{10,11... | collective-permute-start | bytes 3538952 | tf_op jit(solution)/shard_map/ppermute | solution.py:556
  36.8 15.7 %collective-permute-start.4 = (bf16[128,768]{1,0:T(8,128)(2,1)}, bf16[128,768]{1,0:T(8,128)(2,1)}, u32[]{:S(2)}, u32[]{:S(2)}) collective-permute-start(bf16[128,768]{1,0:T(8,128)(2,1)} %get-tuple-element.62), channel_id=1, source_target_pairs={{0,2},{1,3},{2,0},{3,1},{4,6},{5,7},{6,4},{7,5},{8,10},{9,11},{10,... | collective-permute-start | bytes 589832 | tf_op jit(solution)/shard_map/ppermute | solution.py:556
  52.5 6.2 %collective-permute-start.9 = (bf16[128,768]{1,0:T(8,128)(2,1)}, bf16[128,768]{1,0:T(8,128)(2,1)}, u32[]{:S(2)}, u32[]{:S(2)}) collective-permute-start(bf16[128,768]{1,0:T(8,128)(2,1)} %collective-permute-done.4.r_9_), channel_id=1, source_target_pairs={{0,1},{1,0},{2,3},{3,2},{4,5},{5,4},{6,7},{7,6},{8,9},{9,8},{10,11... | collective-permute-start | bytes 589832 | tf_op jit(solution)/shard_map/ppermute | solution.py:556
  52.6 7.6 %collective-permute-start.5 = (bf16[128,768]{1,0:T(8,128)(2,1)}, bf16[128,768]{1,0:T(8,128)(2,1)}, u32[]{:S(2)}, u32[]{:S(2)}) collective-permute-start(bf16[128,768]{1,0:T(8,128)(2,1)} %collective-permute-done.4.r_9_), channel_id=1, source_target_pairs={{0,4},{4,0},{8,12},{12,8},{16,20},{20,16},{24,28},{28,24},{1,5},{5... | collective-permute-start | bytes 589832 | tf_op jit(solution)/shard_map/ppermute | solution.py:559
  53.3 17.7 %collective-permute-start.11 = (bf16[512,768]{1,0:T(8,128)(2,1)}, bf16[512,768]{1,0:T(8,128)(2,1)S(1)}, u32[]{:S(2)}, u32[]{:S(2)}) collective-permute-start(bf16[512,768]{1,0:T(8,128)(2,1)} %collective-permute-done.6.r_11_), channel_id=1, source_target_pairs={{0,1},{1,0},{2,3},{3,2},{4,5},{5,4},{6,7},{7,6},{8,9},{9,8},{10,11... | collective-permute-start | bytes 2359304 | tf_op jit(solution)/shard_map/ppermute | solution.py:556
  53.3 15.9 %all-to-all-start.2 = ((bf16[32,32,128]{2,1,0:T(8,128)(2,1)}), bf16[32,32,128]{2,1,0:T(8,128)(2,1)S(1)}, u32[]{:S(2)}, u32[]{:S(2)}) async-start(bf16[32,32,128]{2,1,0:T(8,128)(2,1)} %shard_map.158), calls=%async_computation.2 | async-start | bytes 524288 | tf_op jit(solution)/shard_map/all_to_all | solution.py:562
  58.7 10.6 %collective-permute-start.7 = (bf16[768,384]{1,0:T(8,128)(2,1)}, bf16[768,384]{1,0:T(8,128)(2,1)}, u32[]{:S(2)}, u32[]{:S(2)}) collective-permute-start(bf16[768,384]{1,0:T(8,128)(2,1)} %copy-done.4), channel_id=1, source_target_pairs={{0,1},{1,0},{2,3},{3,2},{4,5},{5,4},{6,7},{7,6},{8,9},{9,8},{10,11... | collective-permute-start | bytes 1769480 | tf_op jit(solution)/shard_map/ppermute | solution.py:556
  60.2 10.7 %collective-permute-start.8 = (bf16[768,384]{1,0:T(8,128)(2,1)}, bf16[768,384]{1,0:T(8,128)(2,1)}, u32[]{:S(2)}, u32[]{:S(2)}) collective-permute-start(bf16[768,384]{1,0:T(8,128)(2,1)} %collective-permute-done.3.r_8_), channel_id=1, source_target_pairs={{0,1},{1,0},{2,3},{3,2},{4,5},{5,4},{6,7},{7,6},{8,9},{9,8},{10,11... | collective-permute-start | bytes 1769480 | tf_op jit(solution)/shard_map/ppermute | solution.py:556
  69.3 1.7 collective-permute-start.10
  74.0 18.7 %copy-start.6 = (bf16[384,384]{1,0:T(8,128)(2,1)S(1)}, bf16[384,384]{1,0:T(8,128)(2,1)}, u32[]{:S(2)}) copy-start(bf16[384,384]{1,0:T(8,128)(2,1)} %get-tuple-element.54.r_5_) | copy-start | bytes 884740
  74.0 18.7 %copy-start.7 = (bf16[384,384]{1,0:T(8,128)(2,1)S(1)}, bf16[384,384]{1,0:T(8,128)(2,1)}, u32[]{:S(2)}) copy-start(bf16[384,384]{1,0:T(8,128)(2,1)} %get-tuple-element.55.r_6_) | copy-start | bytes 884740
  74.0 18.7 %copy-start.8 = (bf16[384,384]{1,0:T(8,128)(2,1)S(1)}, bf16[384,384]{1,0:T(8,128)(2,1)}, u32[]{:S(2)}) copy-start(bf16[384,384]{1,0:T(8,128)(2,1)} %get-tuple-element.56.r_7_) | copy-start | bytes 884740
  74.0 18.7 %copy-start.9 = (bf16[384,384]{1,0:T(8,128)(2,1)S(1)}, bf16[384,384]{1,0:T(8,128)(2,1)}, u32[]{:S(2)}) copy-start(bf16[384,384]{1,0:T(8,128)(2,1)} %get-tuple-element.57.r_8_) | copy-start | bytes 884740
  74.0 18.7 %copy-start.10 = (f32[1,384]{1,0:T(1,128)S(1)}, f32[1,384]{1,0:T(1,128)}, u32[]{:S(2)}) copy-start(f32[1,384]{1,0:T(1,128)} %get-tuple-element.58.r_9_) | copy-start | bytes 4612
  74.0 18.7 %copy-start.11 = (f32[1,384]{1,0:T(1,128)S(1)}, f32[1,384]{1,0:T(1,128)}, u32[]{:S(2)}) copy-start(f32[1,384]{1,0:T(1,128)} %get-tuple-element.59.r_10_) | copy-start | bytes 4612
  74.0 18.7 %copy-start.14 = (f32[216,128]{1,0:T(8,128)S(1)}, f32[216,128]{1,0:T(8,128)}, u32[]{:S(2)}) copy-start(f32[216,128]{1,0:T(8,128)} %constant.17.clone.r_11_) | copy-start | bytes 331780
  74.0 18.7 %copy-start.15 = (bf16[288,432]{1,0:T(8,128)(2,1)S(1)}, bf16[288,432]{1,0:T(8,128)(2,1)}, u32[]{:S(2)}) copy-start(bf16[288,432]{1,0:T(8,128)(2,1)} %get-tuple-element.52.r_3_) | copy-start | bytes 746500
  74.0 18.7 %copy-start.16 = (bf16[288,432]{1,0:T(8,128)(2,1)S(1)}, bf16[288,432]{1,0:T(8,128)(2,1)}, u32[]{:S(2)}) copy-start(bf16[288,432]{1,0:T(8,128)(2,1)} %get-tuple-element.53.r_4_) | copy-start | bytes 746500
  74.0 18.7 %copy-start.17 = (bf16[216,576]{1,0:T(8,128)(2,1)S(1)}, bf16[216,576]{1,0:T(8,128)(2,1)}, u32[]{:S(2)}) copy-start(bf16[216,576]{1,0:T(8,128)(2,1)} %get-tuple-element.50.r_1_) | copy-start | bytes 746500
  74.1 18.7 %copy-start.18 = (bf16[216,576]{1,0:T(8,128)(2,1)S(1)}, bf16[216,576]{1,0:T(8,128)(2,1)}, u32[]{:S(2)}) copy-start(bf16[216,576]{1,0:T(8,128)(2,1)} %get-tuple-element.51.r_2_) | copy-start | bytes 746500
  (7 other events, 10.9 us)

commit v3 on v2

--- a/solution.py
+++ b/solution.py
@@ -16,6 +16,7 @@
 SHRINK = 0.01
 HALF = 64
 PACK, START, FIRST = 24, 24, 58
+PART = 4
 LANES = 128
 BF = jnp.bfloat16
 F32 = jnp.float32
@@ -275,7 +276,7 @@
     half, own = up_out.shape[1], own_out.shape[0]
     side = lax.axis_index("lat") % 2
     at = pl.multiple_of(side * half, LANES)
-    to = pl.multiple_of(side * own, LANES)
+    to = pl.multiple_of(side * own, HALF)
     into = fetch(
         [up_ref.at[:, pl.ds(at, half)], down_ref.at[pl.ds(to, own), :], down_ref.at[2 * own :, :]],
         mids,
@@ -290,9 +291,7 @@
         copy.wait()
 
 
-def table_kernel(plan, rowv, colv, rowt, colt, *refs):
-    outs, (chi, clo, ehi, elo), sem = refs[:4], refs[4:8], refs[8]
-    copies = [pltpu.make_async_copy(a, b, sem.at[n]) for n, (a, b) in enumerate(zip(refs[4:8], outs))]
+def fill_tables(plan, rowv, colv, rowt, colt, chi, clo, ehi, elo):
     first = (lax.axis_index("lat") * plan.per).astype(F32)
     size = plan.modes
     wide = plan.peers * (plan.main + plan.left)
@@ -301,42 +300,42 @@
     cos, sin, _ = mode_table(plan, first, rows, cols)
     chi[:, :wide], clo[:, :wide] = split(cos)
     chi[:, wide:], clo[:, wide:] = split(sin)
-    copies[0].start()
-    copies[1].start()
     rows = [rowt[n : n + 1, :] for n in range(4)]
     cols = [colt[:, n : n + 1] for n in range(3)]
     cos, sin, doubled = mode_table(plan, first, rows, cols)
     ehi[:, :size], elo[:, :size] = split(cos * doubled)
     ehi[:, size:], elo[:, size:] = split(-sin * doubled)
-    copies[2].start()
-    copies[3].start()
-    for copy in copies:
-        copy.wait()
+
+
+def high_units(plan):
+    return plan.units - 1
 
 
 def block_kernel(plan, fin, finb, fout, foutb, *refs):
     outs, (w1h, w1l, w2h, w2l, b1, b2), sem = refs[:6], refs[6:12], refs[12]
     copies = [pltpu.make_async_copy(a, b, sem.at[n]) for n, (a, b) in enumerate(zip(refs[6:12], outs))]
+    span = high_units(plan)
     for weights, bias, high, low, out in ((fin, finb, w1h, w1l, b1), (fout, foutb, w2h, w2l, b2)):
         blocks, channels = weights.shape[1], weights.shape[2]
-        full = []
-        for p in range(2):
-            lines = []
-            for n in range(blocks):
+        for n in range(blocks):
+            full = []
+            for p in range(2):
+                lines = [jnp.zeros((channels, blocks * channels), F32)] * blocks
                 cells = [jnp.zeros((channels, channels), F32)] * blocks
                 cells[n] = weights[p, n]
-                lines.append(jnp.concatenate(cells, 1))
-            full.append(jnp.concatenate(lines, 0))
-        for u in range(plan.units):
-            at = slice(u * HALF, (u + 1) * HALF)
-            real, imag = full[0][at], full[1][at]
-            for p, (left, right) in enumerate(((real, imag), (-imag, real))):
-                cells = []
-                for v in range(plan.units):
-                    cells += [left[:, v * HALF : (v + 1) * HALF], right[:, v * HALF : (v + 1) * HALF]]
-                row = jnp.concatenate(cells, 1)
-                to = slice((2 * u + p) * HALF, (2 * u + p + 1) * HALF)
-                high[to, :], low[to, :] = split(row)
+                lines[n] = jnp.concatenate(cells, 1)
+                full.append(jnp.concatenate(lines, 0))
+            for u in range(n, n + span):
+                at = slice(u * HALF, (u + 1) * HALF)
+                real, imag = full[0][at], full[1][at]
+                for p, (left, right) in enumerate(((real, imag), (-imag, real))):
+                    cells = []
+                    for v in range(n, n + span):
+                        cut = slice(v * HALF, (v + 1) * HALF)
+                        cells += [left[:, cut], right[:, cut]]
+                    row = jnp.concatenate(cells, 1)
+                    to = slice((2 * (u - n) + p) * HALF, (2 * (u - n) + p + 1) * HALF)
+                    high[n, to, :], low[n, to, :] = split(row)
         lines = [jnp.concatenate([bias[p, n : n + 1] for n in range(blocks)], 1) for p in range(2)]
         cells = []
         for v in range(plan.units):
@@ -350,7 +349,7 @@
 
 def start_kernel(plan, got_ref, tab_hbm, begun_hbm, wire_ref, *refs):
     scratch, tab, begun, sem = refs
-    sum_ref, par_ref = begun.at[: plan.tokens], begun.at[plan.tokens :]
+    sum_ref, par_ref = begun.at[: plan.tokens], begun.at[plan.tokens : plan.tokens + 16]
     bias_ref = par_ref.at[8:16]
     copies = fetch([tab_hbm], [tab], sem)
     got = [unpack(got_ref[c]) for c in range(plan.ch)]
@@ -372,9 +371,14 @@
     values = jnp.where(inside, full, 0.0)
     normed = norm(values, par_ref[0:1, :], par_ref[2:3, :])
     sum_ref[...] = values + normed
+    copies[0].wait()
+    side = tab.shape[1]
+    rows = slice(plan.tokens + 16, plan.tokens + 16 + side)
+    for n in range(2):
+        whole = tab[2 * n].astype(F32) + tab[2 * n + 1].astype(F32)
+        begun[rows, 256 * n : 256 * n + side] = whole
     copies.append(pltpu.make_async_copy(begun, begun_hbm, sem.at[1]))
     copies[1].start()
-    copies[0].wait()
     emit_wire(plan, normed, tab, wire_ref, scratch)
     copies[1].wait()
 
@@ -382,16 +386,16 @@
 def token_kernel(plan, first, last, *refs):
     copies = []
     if first:
-        wire_in, sources, refs = refs[0], refs[1:17], refs[17:]
+        wire_in, sources, refs = refs[0], refs[1:16], refs[16:]
         (sum_out, wire_out, par_out, up_all, down_all), refs = refs[:5], refs[5:]
         scratch, sem, (begun, tab) = refs[0], refs[1], refs[2:]
-        sum_in, par_ref = begun.at[: plan.tokens], begun.at[plan.tokens :]
+        sum_in, par_ref = begun.at[: plan.tokens], begun.at[plan.tokens : plan.tokens + 16]
         shard = up_all.shape[1] // plan.ch
-        half, own = shard // 2, shard // 6
+        half, own = shard // 2, shard // PART
         y = lax.axis_index("lat") % 2
-        copies = fetch(sources[:2], (begun, tab), sem)
+        copies = fetch(sources[:1], (begun,), sem)
         groups = []
-        weights = sources[2:]
+        weights = sources[1:]
         for s in range(plan.ch):
             at = s * shard
             if s < plan.ch // 2:
@@ -403,7 +407,7 @@
                 ups, downs = weights[:2], weights[2:5]
                 spots = [pl.multiple_of(at + n * half, LANES) for n in (y, 1 - y)]
                 ups = [(w, up_all.at[:, pl.ds(n, half)]) for w, n in zip(ups, spots)]
-                spots = [pl.multiple_of(at + n * own, LANES) for n in (y, 1 - y)]
+                spots = [pl.multiple_of(at + n * own, HALF) for n in (y, 1 - y)]
                 spots.append(at + 2 * own)
                 sizes = (own, own, shard - 2 * own)
                 downs = [
@@ -417,8 +421,11 @@
                 copies[-1].start()
                 group.append(copies[-1])
             groups.append(group)
-        for copy in copies[:2]:
-            copy.wait()
+        copies[0].wait()
+        side = tab.shape[1]
+        for n in range(2):
+            whole = begun[plan.tokens + 16 :, 256 * n : 256 * n + side]
+            tab[2 * n], tab[2 * n + 1] = split(whole)
         par_out[...] = par_ref[...]
     else:
         wire_in, sum_in, tab, par_ref, up_all, down_all = refs[:6]
@@ -451,14 +458,19 @@
 
 
 def spectral_kernel(plan, far, wire_in, *refs):
-    copies = []
+    copies, away = [], []
     if far:
-        sources, refs = refs[:11], refs[11:]
-        wire_out, scratch, sem, mids = refs[0], refs[1], refs[2], refs[3:]
+        places, sign_ref, sources, wire_out = refs[:4], refs[4], refs[5:11], refs[11]
+        outs, scratch, sem = refs[12:16], refs[16], refs[17]
+        chi, clo, ehi, elo = tables = refs[18:22]
+        w1h, w1l, w2h, w2l, b1, b2 = mids = refs[22:]
         copies = fetch(sources, mids, sem)
+        fill_tables(plan, *places, *tables)
+        for n, (table, out) in enumerate(zip(tables, outs)):
+            away.append(pltpu.make_async_copy(table, out, sem.at[6 + n]))
+            away[n].start()
     else:
-        mids, (wire_out, scratch) = refs[:11], refs[11:]
-    chi, clo, ehi, elo, w1h, w1l, w2h, w2l, b1, b2, sign_ref = mids
+        chi, clo, ehi, elo, w1h, w1l, w2h, w2l, b1, b2, sign_ref, wire_out, scratch = refs
     scratch[...] = wire_in[...].astype(F32)
     count = plan.peers * plan.main
     half = count + plan.peers * plan.left
@@ -479,18 +491,25 @@
         for n in which if far else ():
             copies[n].wait()
 
-    ready(0, 1, 10)
     spec = dot(chi[...], right) + dot(clo[...], right)
     sign = jnp.concatenate([sign_ref[...]] * plan.units, 1)
     spec = spec * sign
 
     def layer(value, wh, wl, bias):
         hi, lo = split(value)
-        return dot(hi, wh[...]) + dot(hi, wl[...]) + dot(lo, wh[...]) + bias[...]
-
-    ready(4, 5, 8)
+        span, total = wh.shape[1], 0.0
+        for n in range(wh.shape[0]):
+            cut = slice(n * LANES, n * LANES + span)
+            part = dot(hi[:, cut], wh[n]) + dot(hi[:, cut], wl[n]) + dot(lo[:, cut], wh[n])
+            sides = [(part.shape[0], n * LANES), (part.shape[0], value.shape[1] - span - n * LANES)]
+            cells = [jnp.zeros(sides[0], F32)] * (n > 0) + [part]
+            cells += [jnp.zeros(sides[1], F32)] * (sides[1][1] > 0)
+            total = total + jnp.concatenate(cells, 1)
+        return total + bias[...]
+
+    ready(0, 1, 4)
     first = jnp.maximum(layer(spec, w1h, w1l, b1), 0.0)
-    ready(6, 7, 9)
+    ready(2, 3, 5)
     second = layer(first, w2h, w2l, b2)
     shrunk = jnp.where(
         second > SHRINK, second - SHRINK, jnp.where(second < -SHRINK, second + SHRINK, 0.0)
@@ -503,7 +522,6 @@
         turned = swap(part)
         pieces.append(jnp.concatenate([part, jnp.where(low, -turned, turned)], 0))
     hi, lo = split(jnp.concatenate(pieces, 1))
-    ready(2, 3)
     back = dot(ehi[...], hi) + dot(elo[...], hi) + dot(ehi[...], lo)
     for u in range(plan.units):
         part = back[:, u * LANES : (u + 1) * LANES]
@@ -515,6 +533,8 @@
             at = count + p * plan.left
             scratch[p, row : row + plan.left, :] = part[at : at + plan.left]
     wire_out[...] = scratch[...].astype(BF)
+    for copy in away:
+        copy.wait()
 
 
 def call(body, outs, operands, scratch, flops, far_in=0, far_out=(), grant=20):
@@ -579,7 +599,7 @@
     )
     got = exchange(tokens, "ch")
 
-    half, own = up_weight.shape[1] // 2, down_weight.shape[0] // 6
+    half, own = up_weight.shape[1] // 2, down_weight.shape[0] // PART
     shapes = [(D, half), (own, D), (down_weight.shape[0] - 2 * own, D)]
     parts = [jax.ShapeDtypeStruct(shape, BF) for shape in shapes]
     up_part, own_part, rest_part = call(
@@ -593,7 +613,8 @@
         grant=58,
     )
     up_a = across(up_part, far)
-    blocks = [jax.ShapeDtypeStruct((2 * wide, 2 * wide), BF)] * 4
+    span = LANES * high_units(plan)
+    blocks = [jax.ShapeDtypeStruct((filter_in.shape[1], span, span), BF)] * 4
     blocks += [jax.ShapeDtypeStruct((1, 2 * wide), F32)] * 2
     blocks = call(
         lambda *r: block_kernel(plan, *r),
@@ -615,7 +636,8 @@
     wire = jax.ShapeDtypeStruct((plan.peers, plan.message, LANES), BF)
     held = jax.ShapeDtypeStruct((plan.tokens, D), F32)
     scratch = [pltpu.VMEM((plan.lat, ch, plan.message, LANES), F32)]
-    begun = jax.ShapeDtypeStruct((plan.tokens + 16, D), F32)
+    begun = jax.ShapeDtypeStruct((plan.tokens + 16 + short.shape[1], D), F32)
+    assert short.shape[1] <= D - 256
     begun, sent = call(
         lambda *r: start_kernel(plan, *r),
         (begun, wire),
@@ -632,16 +654,6 @@
     lines = plan.peers * (plan.main + plan.left)
     dims = [(plan.modes, 2 * lines)] * 2 + [(lines, 2 * plan.modes)] * 2
     tables = [jax.ShapeDtypeStruct(shape, BF) for shape in dims]
-    made = call(
-        lambda *r: table_kernel(plan, *r),
-        tuple(tables),
-        (after(jnp.asarray(row.T), sent), col, row, col.T),
-        [pltpu.VMEM(t.shape, t.dtype) for t in tables] + [pltpu.SemaphoreType.DMA((4,))],
-        10**8,
-        far_out=range(4),
-        grant=58,
-    )
-    spectral_in = (*made, *blocks)
     for step_index in range(STEPS):
         first, last = step_index == 0, step_index == STEPS - 1
         arrived = exchange(sent, both)
@@ -650,30 +662,38 @@
             rest = across(rest_part, far)
             up_b = beside(up_a)
             up_ac = across(up_a, 1)
-        tabs = (*spectral_in, sign)
-        mids = [pltpu.VMEM(t.shape, t.dtype) for t in tabs] if first else []
-        sent = call(
-            lambda *r: spectral_kernel(plan, first, *r),
-            wire,
-            (arrived, *tabs),
-            [pltpu.VMEM((plan.peers, plan.message, LANES), F32)]
-            + ([pltpu.SemaphoreType.DMA((len(tabs),))] if first else [])
-            + mids,
-            10**9,
-            far_in=len(mids),
-            grant=FIRST if first else 20,
-        )
+        if first:
+            sent, *tables = call(
+                lambda *r: spectral_kernel(plan, True, *r),
+                (wire, *tables),
+                (arrived, row.T, col, row, col.T, sign, *blocks),
+                [pltpu.VMEM((plan.peers, plan.message, LANES), F32)]
+                + [pltpu.SemaphoreType.DMA((10,))]
+                + [pltpu.VMEM(t.shape, t.dtype) for t in (*tables, *blocks)],
+                10**9,
+                far_in=6,
+                far_out=range(1, 5),
+                grant=FIRST,
+            )
+        else:
+            sent = call(
+                lambda *r: spectral_kernel(plan, False, *r),
+                wire,
+                (arrived, *tables, *blocks, sign),
+                [pltpu.VMEM((plan.peers, plan.message, LANES), F32)],
+                10**9,
+            )
         if first:
             up_bc = across(after(up_b, sent), 1)
             down_b = beside(after(down_a, sent))
             down_ac = across(after(down_a, sent), 1)
+            down_bc = across(after(down_b, sent), 1)
             rest_c = across(after(rest, sent), 1)
         arrived = exchange(sent, both)
         if first:
-            down_bc = across(after(down_b, arrived), 1)
             near = (up_weight, down_weight, up_c, down_c)
             distant = (up_a, up_b, down_a, down_b, rest, up_ac, up_bc, down_ac, down_bc, rest_c)
-            sources = (begun, short, *near, *distant)
+            sources = (begun, *near, *distant)
             total, sent, params, ups, downs = call(
                 lambda *r: token_kernel(plan, True, False, *r),
                 (
@@ -686,7 +706,7 @@
                 (arrived, *sources),
                 scratch
                 + [pltpu.SemaphoreType.DMA((len(sources),))]
-                + [pltpu.VMEM(t.shape, t.dtype) for t in sources[:2]],
+                + [pltpu.VMEM(t.shape, t.dtype) for t in (begun, short)],
                 10**10,
                         far_in=len(sources),
                 grant=24,

time: 188 us -> 191 us (1.016)
  Pallas kernels: 42.2 us -> 35.5 us
  waiting for transfers between devices: 25.7 us -> 31.1 us
  local copies, waits for them, and re-layouts: 6.98 us -> 11.7 us
    pallas_call x14 -> x13, Pallas kernels: 42.2 us -> 35.5 us  [call(): pl.pallas_call(body, out_shape=outs, in_specs=[vmem] * (len(operands) - f...]
    ppermute x10, waiting for transfers between devices: 1.66 us -> 8.13 us  [across(): return lax.ppermute(value, 'ch', [(i, i ^ step) for i in range(ch)])]
    all_to_all x3, waiting for transfers between devices: 22.8 us -> 17.2 us  [exchange(): return lax.all_to_all(value, axes, 0, 0, tiled=True)]
    ppermute x2, waiting for transfers between devices: 1.28 us -> 5.74 us  [beside(): return lax.ppermute(value, 'lat', [(i, i ^ 1) for i in range(plan.lat)])]
    unnamed x49, local copies, waits for them, and re-layouts: 5.6 us -> 9.61 us
    ppermute x2, starting transfers between devices: 2.22 us -> 4.7 us  [beside(): return lax.ppermute(value, 'lat', [(i, i ^ 1) for i in range(plan.lat)])]
    ppermute x10, starting transfers between devices: 7.37 us -> 5.2 us  [across(): return lax.ppermute(value, 'ch', [(i, i ^ step) for i in range(ch)])]
  transfers between devices with their start and end apart: 15 -> 15, of which waited for: 6 -> 6; matrix products, arithmetic and copies ran while one was open for 0% -> 0% of each run, Pallas kernels for 8% -> 6%
where the time goes in v3:
time: 191 us; the launch traced here: 190 us
  blocking collectives  87 us (46%)
  Pallas kernels  35.5 us (19%)
  waiting for transfers between devices  31.1 us (16%)
  starting transfers between devices  24.9 us (13%)
  local copies, waits for them, and re-layouts  11.7 us (6%)
    all_to_all x7, blocking collectives, exchange(): return lax.all_to_all(value, axes, 0, 0, tiled=True)  87 us
    pallas_call x13, Pallas kernels, call(): pl.pallas_call(body, out_shape=outs, in_specs=[vmem] * (len(operands) - f...  35.5 us
    all_to_all x3, waiting for transfers between devices, exchange(): return lax.all_to_all(value, axes, 0, 0, tiled=True)  17.2 us
    all_to_all x3, starting transfers between devices, exchange(): return lax.all_to_all(value, axes, 0, 0, tiled=True)  15 us
    unnamed x49, local copies, waits for them, and re-layouts  9.61 us
    ppermute x10, waiting for transfers between devices, across(): return lax.ppermute(value, 'ch', [(i, i ^ step) for i in range(ch)])  8.13 us
    ppermute x2, waiting for transfers between devices, beside(): return lax.ppermute(value, 'lat', [(i, i ^ 1) for i in range(plan.lat)])  5.74 us
    ppermute x10, starting transfers between devices, across(): return lax.ppermute(value, 'ch', [(i, i ^ step) for i in range(ch)])  5.2 us
  transfers between devices with their start and end apart: 15, of which 6 were waited for; matrix products, arithmetic and copies ran while one was open for 0% of the time, Pallas kernels for 6%

profile of v3, /device:TPU:0, one launch (start us, length us, event | category | flops | bytes accessed | tf_op | source)
XLA Modules:
  0.0 190.3 jit_solution(10473746182501936174)
XLA Ops:
  4.2 4.2 %all-to-all-start = ((f32[4,216,128]{2,1,0:T(8,128)}), f32[4,216,128]{2,1,0:T(8,128)S(1)}, u32[]{:S(2)}, u32[]{:S(2)}) async-start(f32[4,216,128]{2,1,0:T(8,128)} %shard_map.154), calls=%async_computation | async-start | bytes 884736 | tf_op jit(solution)/shard_map/all_to_all | solution.py:582
  8.4 2.3 %shard_map.158 = (bf16[768,384]{1,0:T(8,128)(2,1)}, bf16[192,768]{1,0:T(8,128)(2,1)}, bf16[384,768]{1,0:T(8,128)(2,1)}) custom-call(bf16[768,768]{1,0:T(8,128)(2,1)} %r_2_.9, bf16[768,768]{1,0:T(8,128)(2,1)} %r_3_.4), custom_call_target="tpu_custom_call" | custom-call | flops 1000000 | bytes 1048576 | tf_op jit(solution)/shard_map/pallas_call | solution.py:545
  10.7 2.3 %collective-permute-start.2 = (bf16[768,384]{1,0:T(8,128)(2,1)}, bf16[768,384]{1,0:T(8,128)(2,1)S(1)}, u32[]{:S(2)}, u32[]{:S(2)}) collective-permute-start(bf16[768,384]{1,0:T(8,128)(2,1)} %get-tuple-element.57), channel_id=1, source_target_pairs={{0,2},{1,3},{2,0},{3,1},{4,6},{5,7},{6,4},{7,5},{8,10},{9,11},{10,... | collective-permute-start | bytes 1769480 | tf_op jit(solution)/shard_map/ppermute | solution.py:576
  13.0 2.4 %shard_map.155 = (bf16[2,256,256]{2,1,0:T(8,128)(2,1)}, bf16[2,256,256]{2,1,0:T(8,128)(2,1)}, bf16[2,256,256]{2,1,0:T(8,128)(2,1)}, bf16[2,256,256]{2,1,0:T(8,12...) custom-call(f32[2,2,96,96]{3,2,1,0:T(8,128)} %r_0_.1, f32[2,2,96]{2,1,0:T(2,128)} %r_1_.5, f32[2,2,96,96]{3,2,1,0:T(8,128)} %r_2_.8, ...), custom_call_target="tpu_custom_call" | custom-call | flops 100000000 | bytes 1048576 | tf_op jit(solution)/shard_map/pallas_call | solution.py:545
  15.4 1.7 all-to-all-done.r_0_
  18.0 1.9 %shard_map.156 = (f32[304,768]{1,0:T(8,128)S(1)}, bf16[32,32,128]{2,1,0:T(8,128)(2,1)}) custom-call(f32[4,216,128]{2,1,0:T(8,128)S(1)} %all-to-all-done.r_0_, bf16[4,144,144]{2,1,0:T(8,128)(2,1)S(1)} %copy-done.14), custom_call_target="tpu_custom_call" | custom-call | flops 1000000000 | bytes 1048576 | tf_op jit(solution)/shard_map/pallas_call | solution.py:545
  20.9 5.4 %all-to-all-start.1 = ((bf16[32,32,128]{2,1,0:T(8,128)(2,1)}), bf16[32,32,128]{2,1,0:T(8,128)(2,1)S(1)}, u32[]{:S(2)}, u32[]{:S(2)}) async-start(bf16[32,32,128]{2,1,0:T(8,128)(2,1)} %get-tuple-element.48), calls=%async_computation.1 | async-start | bytes 524288 | tf_op jit(solution)/shard_map/all_to_all | solution.py:582
  26.4 1.8 collective-permute-start.6
  29.0 2.7 %collective-permute-start.3 = (bf16[768,384]{1,0:T(8,128)(2,1)S(1)}, bf16[768,384]{1,0:T(8,128)(2,1)}, u32[]{:S(2)}, u32[]{:S(2)}) collective-permute-start(bf16[768,384]{1,0:T(8,128)(2,1)S(1)} %collective-permute-done.2.r_6_), channel_id=1, source_target_pairs={{0,4},{4,0},{8,12},{12,8},{16,20},{20,16},{24,28},{28,24},{1,5},{5... | collective-permute-start | bytes 1769480 | tf_op jit(solution)/shard_map/ppermute | solution.py:579
  31.7 5.2 %all-to-all-done.1.r_0_ = bf16[32,32,128]{2,1,0:T(8,128)(2,1)S(1)} async-done(((bf16[32,32,128]{2,1,0:T(8,128)(2,1)}), bf16[32,32,128]{2,1,0:T(8,128)(2,1)S(1)}, u32[]{:S(2)}, u32[]{:S(2)}) %all-to-all-start.1) | async-done | bytes 262176 | tf_op jit(solution)/shard_map/all_to_all | solution.py:582
  37.6 5.7 %shard_map.157 = (bf16[32,32,128]{2,1,0:T(8,128)(2,1)}, bf16[216,576]{1,0:T(8,128)(2,1)}, bf16[216,576]{1,0:T(8,128)(2,1)}, bf16[288,432]{1,0:T(8,128)(2,1)}, bf16[288,432]{1,0:T(8,128)(2,1)}) custom-call(bf16[32,32,128]{2,1,0:T(8,128)(2,1)} %copy-done.23, f32[216,8]{1,0:T(8,128)} %constant.13.clone.r_1_, f32[8,288]{1,0:T(8,128)} %constant.14.clone.r_2_, ...), custom_call_target="tpu_custom_call" | custom-call | flops 1000000000 | bytes 1048576 | tf_op jit(solution)/shard_map/pallas_call | solution.py:545
  43.4 7.6 %collective-permute-done.4.r_8_ = bf16[192,768]{1,0:T(8,128)(2,1)S(1)} collective-permute-done((bf16[192,768]{1,0:T(8,128)(2,1)}, bf16[192,768]{1,0:T(8,128)(2,1)S(1)}, u32[]{:S(2)}, u32[]{:S(2)}) %collective-permute-start.4) | collective-permute-done | bytes 294944 | tf_op jit(solution)/shard_map/ppermute | solution.py:576
  51.0 2.0 %collective-permute-start.5 = (bf16[192,768]{1,0:T(8,128)(2,1)S(1)}, bf16[192,768]{1,0:T(8,128)(2,1)S(1)}, u32[]{:S(2)}, u32[]{:S(2)}) collective-permute-start(bf16[192,768]{1,0:T(8,128)(2,1)S(1)} %collective-permute-done.4.r_8_), channel_id=1, source_target_pairs={{0,4},{4,0},{8,12},{12,8},{16,20},{20,16},{24,28},{28,24},{1,5},{5... | collective-permute-start | bytes 884744 | tf_op jit(solution)/shard_map/ppermute | solution.py:579
  54.9 5.7 %collective-permute-done.5.r_9_ = bf16[192,768]{1,0:T(8,128)(2,1)S(1)} collective-permute-done((bf16[192,768]{1,0:T(8,128)(2,1)S(1)}, bf16[192,768]{1,0:T(8,128)(2,1)S(1)}, u32[]{:S(2)}, u32[]{:S(2)}) %collective-permute-start.5) | collective-permute-done | bytes 294944 | tf_op jit(solution)/shard_map/ppermute | solution.py:579
  60.6 5.3 %all-to-all-start.2 = ((bf16[32,32,128]{2,1,0:T(8,128)(2,1)}), bf16[32,32,128]{2,1,0:T(8,128)(2,1)S(1)}, u32[]{:S(2)}, u32[]{:S(2)}) async-start(bf16[32,32,128]{2,1,0:T(8,128)(2,1)} %get-tuple-element.55), calls=%async_computation.2 | async-start | bytes 524288 | tf_op jit(solution)/shard_map/all_to_all | solution.py:582
  66.2 10.2 %all-to-all-done.2.r_0_ = bf16[32,32,128]{2,1,0:T(8,128)(2,1)S(1)} async-done(((bf16[32,32,128]{2,1,0:T(8,128)(2,1)}), bf16[32,32,128]{2,1,0:T(8,128)(2,1)S(1)}, u32[]{:S(2)}, u32[]{:S(2)}) %all-to-all-start.2) | async-done | bytes 262176 | tf_op jit(solution)/shard_map/all_to_all | solution.py:582
  78.4 1.2 copy-done.22
  79.7 5.5 %shard_map.159 = (f32[144,768]{1,0:T(8,128)S(1)}, bf16[32,32,128]{2,1,0:T(8,128)(2,1)S(1)}, f32[16,768]{1,0:T(8,128)S(1)}, bf16[768,3072]{1,0:T(8,128)(2,1)S(1)}, bf16[3072,768]{1,0:T(8,128)(2,1)S(1)}) custom-call(bf16[32,32,128]{2,1,0:T(8,128)(2,1)S(1)} %all-to-all-done.2.r_0_, f32[304,768]{1,0:T(8,128)S(1)} %copy-done.22, bf16[768,768]{1,0:T(8,128)(2,1)S(1)} %copy-done, ...), custom_call_target="tpu_custom_call" | custom-call | flops 10000000000 | bytes 1048576 | tf_op jit(solution)/shard_map/pallas_call | solution.py:545
  85.2 12.8 %all_to_all.50.r_0_ = bf16[32,32,128]{2,1,0:T(8,128)(2,1)S(1)} all-to-all(bf16[32,32,128]{2,1,0:T(8,128)(2,1)S(1)} %get-tuple-element.64), channel_id=1, replica_groups=mesh['lat'=8,'ch'=4] {'lat','ch'}, dimensions={0} | all-to-all | bytes 524288 | tf_op jit(solution)/shard_map/all_to_all | solution.py:582
  98.1 1.7 shard_map.160
  99.8 12.8 %all_to_all.51.r_0_ = bf16[32,32,128]{2,1,0:T(8,128)(2,1)S(1)} all-to-all(bf16[32,32,128]{2,1,0:T(8,128)(2,1)S(1)} %shard_map.160), channel_id=1, replica_groups=mesh['lat'=8,'ch'=4] {'lat','ch'}, dimensions={0} | all-to-all | bytes 524288 | tf_op jit(solution)/shard_map/all_to_all | solution.py:582
  112.6 3.9 %shard_map.161 = (f32[144,768]{1,0:T(8,128)S(1)}, bf16[32,32,128]{2,1,0:T(8,128)(2,1)S(1)}) custom-call(bf16[32,32,128]{2,1,0:T(8,128)(2,1)S(1)} %all_to_all.51.r_0_, f32[144,768]{1,0:T(8,128)S(1)} %get-tuple-element.69.r_1_, bf16[4,144,144]{2,1,0:T(8,128)(2,1)S(1)} %copy-done.15, f32[16,768]{1,0:T(8,128)S(1)} %get-tuple-element.70.r_3_, ...), custom_call_target="tpu_custom_call" | custom-call | flops 10000000000 | bytes 1048576 | tf_op jit(solution)/shard_map/pallas_call | solution.py:545
  116.5 12.8 %all_to_all.52.r_0_ = bf16[32,32,128]{2,1,0:T(8,128)(2,1)S(1)} all-to-all(bf16[32,32,128]{2,1,0:T(8,128)(2,1)S(1)} %get-tuple-element.73), channel_id=1, replica_groups=mesh['lat'=8,'ch'=4] {'lat','ch'}, dimensions={0} | all-to-all | bytes 524288 | tf_op jit(solution)/shard_map/all_to_all | solution.py:582
  129.3 1.7 shard_map.162
  131.0 12.8 %all_to_all.53.r_0_ = bf16[32,32,128]{2,1,0:T(8,128)(2,1)S(1)} all-to-all(bf16[32,32,128]{2,1,0:T(8,128)(2,1)S(1)} %shard_map.162), channel_id=1, replica_groups=mesh['lat'=8,'ch'=4] {'lat','ch'}, dimensions={0} | all-to-all | bytes 524288 | tf_op jit(solution)/shard_map/all_to_all | solution.py:582
  143.8 3.9 %shard_map.163 = (f32[144,768]{1,0:T(8,128)S(1)}, bf16[32,32,128]{2,1,0:T(8,128)(2,1)S(1)}) custom-call(bf16[32,32,128]{2,1,0:T(8,128)(2,1)S(1)} %all_to_all.53.r_0_, f32[144,768]{1,0:T(8,128)S(1)} %get-tuple-element.74.r_1_, bf16[4,144,144]{2,1,0:T(8,128)(2,1)S(1)} %copy-done.15, f32[16,768]{1,0:T(8,128)S(1)} %get-tuple-element.70.r_3_, ...), custom_call_target="tpu_custom_call" | custom-call | flops 10000000000 | bytes 1048576 | tf_op jit(solution)/shard_map/pallas_call | solution.py:545
  147.7 12.8 %all_to_all.54.r_0_ = bf16[32,32,128]{2,1,0:T(8,128)(2,1)S(1)} all-to-all(bf16[32,32,128]{2,1,0:T(8,128)(2,1)S(1)} %get-tuple-element.75), channel_id=1, replica_groups=mesh['lat'=8,'ch'=4] {'lat','ch'}, dimensions={0} | all-to-all | bytes 524288 | tf_op jit(solution)/shard_map/all_to_all | solution.py:582
  160.5 1.7 shard_map.164
  162.2 12.8 %all_to_all.55.r_0_ = bf16[32,32,128]{2,1,0:T(8,128)(2,1)S(1)} all-to-all(bf16[32,32,128]{2,1,0:T(8,128)(2,1)S(1)} %shard_map.164), channel_id=1, replica_groups=mesh['lat'=8,'ch'=4] {'lat','ch'}, dimensions={0} | all-to-all | bytes 524288 | tf_op jit(solution)/shard_map/all_to_all | solution.py:582
  175.0 3.5 %shard_map.165 = f32[4,216,128]{2,1,0:T(8,128)S(1)} custom-call(bf16[32,32,128]{2,1,0:T(8,128)(2,1)S(1)} %all_to_all.55.r_0_, f32[144,768]{1,0:T(8,128)S(1)} %get-tuple-element.76.r_1_, bf16[4,144,144]{2,1,0:T(8,128)(2,1)S(1)} %copy-done.15, f32[16,768]{1,0:T(8,128)S(1)} %get-tuple-element.70.r_3_, bf16[768,3072]{1,0:T(8,128)(2,1)S(1)} %get-tuple-element.71.r_4_, ...), custom_call_target="tpu_custom_call" | custom-call | flops 10000000000 | bytes 1048576 | tf_op jit(solution)/shard_map/pallas_call | solution.py:545
  178.4 10.3 %all_to_all.56.r_0_ = f32[4,216,128]{2,1,0:T(8,128)S(1)} all-to-all(f32[4,216,128]{2,1,0:T(8,128)S(1)} %shard_map.165), channel_id=1, replica_groups=mesh['lat'=8,'ch'=4] {'ch'}, dimensions={0} | all-to-all | bytes 884736 | tf_op jit(solution)/shard_map/all_to_all | solution.py:582
  189.0 1.4 copy.17
  (69 shorter events, 12.0 us)
Async XLA Ops:
  4.2 12.9 %all-to-all-start = ((f32[4,216,128]{2,1,0:T(8,128)}), f32[4,216,128]{2,1,0:T(8,128)S(1)}, u32[]{:S(2)}, u32[]{:S(2)}) async-start(f32[4,216,128]{2,1,0:T(8,128)} %shard_map.154), calls=%async_computation | async-start | bytes 884736 | tf_op jit(solution)/shard_map/all_to_all | solution.py:582
  10.7 18.3 %collective-permute-start.2 = (bf16[768,384]{1,0:T(8,128)(2,1)}, bf16[768,384]{1,0:T(8,128)(2,1)S(1)}, u32[]{:S(2)}, u32[]{:S(2)}) collective-permute-start(bf16[768,384]{1,0:T(8,128)(2,1)} %get-tuple-element.57), channel_id=1, source_target_pairs={{0,2},{1,3},{2,0},{3,1},{4,6},{5,7},{6,4},{7,5},{8,10},{9,11},{10,... | collective-permute-start | bytes 1769480 | tf_op jit(solution)/shard_map/ppermute | solution.py:576
  17.1 1.0 copy-start.14
  18.0 10.2 %copy-start = (bf16[768,768]{1,0:T(8,128)(2,1)S(1)}, bf16[768,768]{1,0:T(8,128)(2,1)}, u32[]{:S(2)}) copy-start(bf16[768,768]{1,0:T(8,128)(2,1)} %r_2_.9) | copy-start | bytes 3538948
  18.0 13.7 %copy-start.1 = (bf16[768,768]{1,0:T(8,128)(2,1)S(1)}, bf16[768,768]{1,0:T(8,128)(2,1)}, u32[]{:S(2)}) copy-start(bf16[768,768]{1,0:T(8,128)(2,1)} %r_3_.4) | copy-start | bytes 3538948
  20.9 16.0 %all-to-all-start.1 = ((bf16[32,32,128]{2,1,0:T(8,128)(2,1)}), bf16[32,32,128]{2,1,0:T(8,128)(2,1)S(1)}, u32[]{:S(2)}, u32[]{:S(2)}) async-start(bf16[32,32,128]{2,1,0:T(8,128)(2,1)} %get-tuple-element.48), calls=%async_computation.1 | async-start | bytes 524288 | tf_op jit(solution)/shard_map/all_to_all | solution.py:582
  26.4 24.6 %collective-permute-start.6 = (bf16[384,768]{1,0:T(8,128)(2,1)}, bf16[384,768]{1,0:T(8,128)(2,1)}, u32[]{:S(2)}, u32[]{:S(2)}) collective-permute-start(bf16[384,768]{1,0:T(8,128)(2,1)} %get-tuple-element.60), channel_id=1, source_target_pairs={{0,2},{1,3},{2,0},{3,1},{4,6},{5,7},{6,4},{7,5},{8,10},{9,11},{10,... | collective-permute-start | bytes 1769480 | tf_op jit(solution)/shard_map/ppermute | solution.py:576
  28.2 37.7 %collective-permute-start = (bf16[768,768]{1,0:T(8,128)(2,1)S(1)}, bf16[768,768]{1,0:T(8,128)(2,1)}, u32[]{:S(2)}, u32[]{:S(2)}) collective-permute-start(bf16[768,768]{1,0:T(8,128)(2,1)S(1)} %copy-done), channel_id=1, source_target_pairs={{0,1},{1,0},{2,3},{3,2},{4,5},{5,4},{6,7},{7,6},{8,9},{9,8},{10,11... | collective-permute-start | bytes 3538952 | tf_op jit(solution)/shard_map/ppermute | solution.py:576
  28.2 22.8 %collective-permute-start.4 = (bf16[192,768]{1,0:T(8,128)(2,1)}, bf16[192,768]{1,0:T(8,128)(2,1)S(1)}, u32[]{:S(2)}, u32[]{:S(2)}) collective-permute-start(bf16[192,768]{1,0:T(8,128)(2,1)} %get-tuple-element.58), channel_id=1, source_target_pairs={{0,2},{1,3},{2,0},{3,1},{4,6},{5,7},{6,4},{7,5},{8,10},{9,11},{10,... | collective-permute-start | bytes 884744 | tf_op jit(solution)/shard_map/ppermute | solution.py:576
  29.0 24.7 %collective-permute-start.3 = (bf16[768,384]{1,0:T(8,128)(2,1)S(1)}, bf16[768,384]{1,0:T(8,128)(2,1)}, u32[]{:S(2)}, u32[]{:S(2)}) collective-permute-start(bf16[768,384]{1,0:T(8,128)(2,1)S(1)} %collective-permute-done.2.r_6_), channel_id=1, source_target_pairs={{0,4},{4,0},{8,12},{12,8},{16,20},{20,16},{24,28},{28,24},{1,5},{5... | collective-permute-start | bytes 1769480 | tf_op jit(solution)/shard_map/ppermute | solution.py:579
  31.7 34.5 %collective-permute-start.1 = (bf16[768,768]{1,0:T(8,128)(2,1)S(1)}, bf16[768,768]{1,0:T(8,128)(2,1)}, u32[]{:S(2)}, u32[]{:S(2)}) collective-permute-start(bf16[768,768]{1,0:T(8,128)(2,1)S(1)} %copy-done.1), channel_id=1, source_target_pairs={{0,1},{1,0},{2,3},{3,2},{4,5},{5,4},{6,7},{7,6},{8,9},{9,8},{10,11... | collective-permute-start | bytes 3538952 | tf_op jit(solution)/shard_map/ppermute | solution.py:576
  51.0 2.9 %collective-permute-start.9 = (bf16[192,768]{1,0:T(8,128)(2,1)S(1)}, bf16[192,768]{1,0:T(8,128)(2,1)S(1)}, u32[]{:S(2)}, u32[]{:S(2)}) collective-permute-start(bf16[192,768]{1,0:T(8,128)(2,1)S(1)} %collective-permute-done.4.r_8_), channel_id=1, source_target_pairs={{0,1},{1,0},{2,3},{3,2},{4,5},{5,4},{6,7},{7,6},{8,9},{9,8},{10,11... | collective-permute-start | bytes 884744 | tf_op jit(solution)/shard_map/ppermute | solution.py:576
  51.0 9.7 %collective-permute-start.5 = (bf16[192,768]{1,0:T(8,128)(2,1)S(1)}, bf16[192,768]{1,0:T(8,128)(2,1)S(1)}, u32[]{:S(2)}, u32[]{:S(2)}) collective-permute-start(bf16[192,768]{1,0:T(8,128)(2,1)S(1)} %collective-permute-done.4.r_8_), channel_id=1, source_target_pairs={{0,4},{4,0},{8,12},{12,8},{16,20},{20,16},{24,28},{28,24},{1,5},{5... | collective-permute-start | bytes 884744 | tf_op jit(solution)/shard_map/ppermute | solution.py:579
  53.7 12.6 %collective-permute-start.7 = (bf16[768,384]{1,0:T(8,128)(2,1)S(1)}, bf16[768,384]{1,0:T(8,128)(2,1)}, u32[]{:S(2)}, u32[]{:S(2)}) collective-permute-start(bf16[768,384]{1,0:T(8,128)(2,1)S(1)} %collective-permute-done.2.r_6_), channel_id=1, source_target_pairs={{0,1},{1,0},{2,3},{3,2},{4,5},{5,4},{6,7},{7,6},{8,9},{9,8},{10,11... | collective-permute-start | bytes 1769480 | tf_op jit(solution)/shard_map/ppermute | solution.py:576
  54.6 21.9 %collective-permute-start.11 = (bf16[384,768]{1,0:T(8,128)(2,1)}, bf16[384,768]{1,0:T(8,128)(2,1)}, u32[]{:S(2)}, u32[]{:S(2)}) collective-permute-start(bf16[384,768]{1,0:T(8,128)(2,1)} %collective-permute-done.6.r_10_), channel_id=1, source_target_pairs={{0,1},{1,0},{2,3},{3,2},{4,5},{5,4},{6,7},{7,6},{8,9},{9,8},{10,11... | collective-permute-start | bytes 1769480 | tf_op jit(solution)/shard_map/ppermute | solution.py:576
  60.6 15.9 %collective-permute-start.8 = (bf16[768,384]{1,0:T(8,128)(2,1)}, bf16[768,384]{1,0:T(8,128)(2,1)}, u32[]{:S(2)}, u32[]{:S(2)}) collective-permute-start(bf16[768,384]{1,0:T(8,128)(2,1)} %collective-permute-done.3.r_7_), channel_id=1, source_target_pairs={{0,1},{1,0},{2,3},{3,2},{4,5},{5,4},{6,7},{7,6},{8,9},{9,8},{10,11... | collective-permute-start | bytes 1769480 | tf_op jit(solution)/shard_map/ppermute | solution.py:576
  60.6 15.8 %all-to-all-start.2 = ((bf16[32,32,128]{2,1,0:T(8,128)(2,1)}), bf16[32,32,128]{2,1,0:T(8,128)(2,1)S(1)}, u32[]{:S(2)}, u32[]{:S(2)}) async-start(bf16[32,32,128]{2,1,0:T(8,128)(2,1)} %get-tuple-element.55), calls=%async_computation.2 | async-start | bytes 524288 | tf_op jit(solution)/shard_map/all_to_all | solution.py:582
  65.9 10.6 %collective-permute-start.10 = (bf16[192,768]{1,0:T(8,128)(2,1)S(1)}, bf16[192,768]{1,0:T(8,128)(2,1)}, u32[]{:S(2)}, u32[]{:S(2)}) collective-permute-start(bf16[192,768]{1,0:T(8,128)(2,1)S(1)} %collective-permute-done.5.r_9_), channel_id=1, source_target_pairs={{0,1},{1,0},{2,3},{3,2},{4,5},{5,4},{6,7},{7,6},{8,9},{9,8},{10,11... | collective-permute-start | bytes 884744 | tf_op jit(solution)/shard_map/ppermute | solution.py:576
  76.5 1.0 copy-start.5
  78.4 1.2 copy-start.22
  79.6 18.4 %copy-start.8 = (bf16[2,256,256]{2,1,0:T(8,128)(2,1)S(1)}, bf16[2,256,256]{2,1,0:T(8,128)(2,1)}, u32[]{:S(2)}) copy-start(bf16[2,256,256]{2,1,0:T(8,128)(2,1)} %get-tuple-element.49.r_6_.r_5_) | copy-start | bytes 786436
  79.6 18.4 %copy-start.9 = (bf16[2,256,256]{2,1,0:T(8,128)(2,1)S(1)}, bf16[2,256,256]{2,1,0:T(8,128)(2,1)}, u32[]{:S(2)}) copy-start(bf16[2,256,256]{2,1,0:T(8,128)(2,1)} %get-tuple-element.50.r_7_.r_6_) | copy-start | bytes 786436
  79.6 18.4 %copy-start.10 = (bf16[2,256,256]{2,1,0:T(8,128)(2,1)S(1)}, bf16[2,256,256]{2,1,0:T(8,128)(2,1)}, u32[]{:S(2)}) copy-start(bf16[2,256,256]{2,1,0:T(8,128)(2,1)} %get-tuple-element.51.r_8_.r_7_) | copy-start | bytes 786436
  79.6 18.4 %copy-start.11 = (bf16[2,256,256]{2,1,0:T(8,128)(2,1)S(1)}, bf16[2,256,256]{2,1,0:T(8,128)(2,1)}, u32[]{:S(2)}) copy-start(bf16[2,256,256]{2,1,0:T(8,128)(2,1)} %get-tuple-element.52.r_9_.r_8_) | copy-start | bytes 786436
  79.6 18.4 %copy-start.12 = (f32[1,384]{1,0:T(1,128)S(1)}, f32[1,384]{1,0:T(1,128)}, u32[]{:S(2)}) copy-start(f32[1,384]{1,0:T(1,128)} %get-tuple-element.53.r_10_.r_9_) | copy-start | bytes 4612
  79.6 18.4 %copy-start.13 = (f32[1,384]{1,0:T(1,128)S(1)}, f32[1,384]{1,0:T(1,128)}, u32[]{:S(2)}) copy-start(f32[1,384]{1,0:T(1,128)} %get-tuple-element.54.r_11_.r_10_) | copy-start | bytes 4612
  79.6 18.4 %copy-start.16 = (f32[216,128]{1,0:T(8,128)S(1)}, f32[216,128]{1,0:T(8,128)}, u32[]{:S(2)}) copy-start(f32[216,128]{1,0:T(8,128)} %constant.17.clone.r_5_.r_11_) | copy-start | bytes 331780
  79.7 18.4 %copy-start.17 = (bf16[288,432]{1,0:T(8,128)(2,1)S(1)}, bf16[288,432]{1,0:T(8,128)(2,1)}, u32[]{:S(2)}) copy-start(bf16[288,432]{1,0:T(8,128)(2,1)} %get-tuple-element.67.r_3_) | copy-start | bytes 746500
  79.7 18.4 %copy-start.18 = (bf16[288,432]{1,0:T(8,128)(2,1)S(1)}, bf16[288,432]{1,0:T(8,128)(2,1)}, u32[]{:S(2)}) copy-start(bf16[288,432]{1,0:T(8,128)(2,1)} %get-tuple-element.68.r_4_) | copy-start | bytes 746500
  79.7 18.4 %copy-start.19 = (bf16[216,576]{1,0:T(8,128)(2,1)S(1)}, bf16[216,576]{1,0:T(8,128)(2,1)}, u32[]{:S(2)}) copy-start(bf16[216,576]{1,0:T(8,128)(2,1)} %get-tuple-element.65.r_1_) | copy-start | bytes 746500
  79.7 18.4 %copy-start.20 = (bf16[216,576]{1,0:T(8,128)(2,1)S(1)}, bf16[216,576]{1,0:T(8,128)(2,1)}, u32[]{:S(2)}) copy-start(bf16[216,576]{1,0:T(8,128)(2,1)} %get-tuple-element.66.r_2_) | copy-start | bytes 746500
  98.0 14.5 %copy-start.15 = (bf16[4,144,144]{2,1,0:T(8,128)(2,1)S(1)}, bf16[4,144,144]{2,1,0:T(8,128)(2,1)}, u32[]{:S(2)}) copy-start(bf16[4,144,144]{2,1,0:T(8,128)(2,1)} %constant.12.clone.r_1_.r_2_) | copy-start | bytes 497668
  (7 other events, 5.4 us)

commit v4 on v3

--- a/solution.py
+++ b/solution.py
@@ -225,8 +225,8 @@
     return jnp.concatenate([message[:tokens], tail], 1)
 
 
-def pack_kernel(plan, state_ref, gain_hbm, bias_hbm, up_hbm, out_ref, scratch, body, tail, *refs):
-    gain_ref, bias_ref, up_ref, sem = refs
+def pack_kernel(plan, state_ref, gain_hbm, bias_hbm, up_hbm, *refs):
+    outs, (scratch, body, tail, out_ref, gain_ref, bias_ref, up_ref, sem) = refs[: plan.ch], refs[plan.ch :]
     copies = fetch([gain_hbm, bias_hbm, up_hbm], [gain_ref, bias_ref, up_ref], sem)
     body[...] = state_ref[:, :, :LANES]
     tail[:, :, :HALF] = state_ref[:, :, LANES:]
@@ -249,11 +249,15 @@
             scratch[at : at + plan.short, :LANES] = body[h, every, :]
             scratch[at : at + plan.short, LANES:] = tail[h, every, :][:, :HALF]
         out_ref[q] = pack(scratch[...])
-
-
-def unpack_kernel(plan, got_ref, out_ref, body, tail):
-    for q in range(plan.ch):
-        values = unpack(got_ref[q])
+    for n in range(plan.ch):
+        outs[n][...] = out_ref[lax.axis_index("ch") ^ n]
+
+
+def unpack_kernel(plan, *refs):
+    got, (out_ref, body, tail) = refs[: plan.ch], refs[plan.ch :]
+    for n in range(plan.ch):
+        q = lax.axis_index("ch") ^ n
+        values = unpack(got[n][...])
         wide = jnp.concatenate([values[:, LANES:], values[:, LANES:]], 1)
         for h in range(plan.rows):
             at = slice(h * plan.padded, h * plan.padded + plan.short)
@@ -347,8 +351,10 @@
         copy.wait()
 
 
-def start_kernel(plan, got_ref, tab_hbm, begun_hbm, wire_ref, *refs):
-    scratch, tab, begun, sem = refs
+def start_kernel(plan, *refs):
+    came, (tab_hbm, begun_hbm, wire_ref, scratch, got_ref, tab, begun, sem) = refs[: plan.ch], refs[plan.ch :]
+    for n in range(plan.ch):
+        got_ref[lax.axis_index("ch") ^ n] = came[n][...]
     sum_ref, par_ref = begun.at[: plan.tokens], begun.at[plan.tokens : plan.tokens + 16]
     bias_ref = par_ref.at[8:16]
     copies = fetch([tab_hbm], [tab], sem)
@@ -363,7 +369,7 @@
     par_ref[5:8, :] = jnp.zeros((3, D), F32)
     bias_ref[...] = jnp.zeros(bias_ref.shape, F32)
     for s in range(plan.ch):
-        source = unpack(got_ref[lax.axis_index("ch") ^ s])
+        source = unpack(came[s][...])
         parts = [source[rows[5 + n] : rows[5 + n] + 1, :] for n in range(plan.ch)]
         line = jnp.concatenate(parts, 1)
         bias_ref[s : s + 1, :] = line
@@ -429,7 +435,9 @@
         par_out[...] = par_ref[...]
     else:
         wire_in, sum_in, tab, par_ref, up_all, down_all = refs[:6]
-        outs, scratch = refs[6:-1], refs[-1]
+        outs, scratch = refs[6:], refs[-1]
+        if last:
+            outs, scratch = refs[6:], refs[-2]
         shard = up_all.shape[1] // plan.ch
         half = shard // 2
     values = sum_in[...] + read_wire(plan, wire_in, tab, scratch)
@@ -448,10 +456,12 @@
     values = values + mixed
     if last:
         for c in range(plan.ch):
-            outs[0][c] = pack(values[:, c * plan.wide : (c + 1) * plan.wide])
+            refs[-1][c] = pack(values[:, c * plan.wide : (c + 1) * plan.wide])
+        for n in range(plan.ch):
+            outs[n][...] = refs[-1][lax.axis_index("ch") ^ n]
         return
     if not first:
-        sum_out, wire_out = outs
+        sum_out, wire_out = outs[:2]
     normed = norm(values, par_ref[0:1, :], par_ref[2:3, :])
     sum_out[...] = values + normed
     emit_wire(plan, normed, tab, wire_out, scratch)
@@ -584,20 +594,22 @@
     def after(value, token):
         return lax.optimization_barrier((value, token))[0]
 
-    message = jax.ShapeDtypeStruct((ch, plan.packed, LANES), F32)
+    message = (jax.ShapeDtypeStruct((plan.packed, LANES), F32),) * ch
+    mail = pltpu.VMEM((ch, plan.packed, LANES), F32)
     tokens = call(
         lambda *r: pack_kernel(plan, *r),
         message,
         (state[0], norm_gains, channel_biases, up_bias.reshape(1, ch * wide)),
         [pltpu.VMEM((plan.tokens, wide), F32)]
         + [pltpu.VMEM((rows, width, LANES), F32)] * 2
+        + [mail]
         + [pltpu.VMEM(v.shape, BF) for v in (norm_gains, channel_biases, up_bias.reshape(1, -1))]
         + [pltpu.SemaphoreType.DMA((3,))],
         10**8,
         far_in=3,
         grant=PACK,
     )
-    got = exchange(tokens, "ch")
+    got = [tokens[0]] + [across(tokens[n], n) for n in range(1, ch)]
 
     half, own = up_weight.shape[1] // 2, down_weight.shape[0] // PART
     shapes = [(D, half), (own, D), (down_weight.shape[0] - 2 * own, D)]
@@ -625,7 +637,7 @@
         far_out=range(6),
         grant=58,
     )
-    got, *blocks = lax.optimization_barrier((got, *blocks))
+    got[1], *blocks = lax.optimization_barrier((got[1], *blocks))
     up_c, down_c = across(up_weight, 1), across(down_weight, 1)
 
     short = jnp.asarray(short_tables(plan))
@@ -641,8 +653,9 @@
     begun, sent = call(
         lambda *r: start_kernel(plan, *r),
         (begun, wire),
-        (got, short),
+        (*got, short),
         scratch
+        + [mail]
         + [pltpu.VMEM(t.shape, t.dtype) for t in (short, begun)]
         + [pltpu.SemaphoreType.DMA((2,))],
         10**9,
@@ -716,16 +729,16 @@
             lambda *r: token_kernel(plan, False, last, *r),
             message if last else (held, wire),
             (arrived, total, short, params, ups, downs),
-            scratch,
+            scratch + [mail] * last,
             10**10,
         )
         if not last:
             total, sent = result
-    result = exchange(result, "ch")
+    result = [result[0]] + [across(result[n], n) for n in range(1, ch)]
     result = call(
         lambda *r: unpack_kernel(plan, *r),
         jax.ShapeDtypeStruct((rows, width, wide), F32),
-        (result,),
+        tuple(result),
         [pltpu.VMEM((rows, width, LANES), F32)] * 2,
         10**8,
     )

time: 191 us -> 194 us (1.016)
  waiting for transfers between devices: 31.1 us -> 49.4 us
  blocking collectives: 87 us -> 76.7 us
  local copies, waits for them, and re-layouts: 11.7 us -> 7.68 us
    ppermute x10 -> x16, waiting for transfers between devices: 8.13 us -> 25.9 us  [across(): return lax.ppermute(value, 'ch', [(i, i ^ step) for i in range(ch)])]
    all_to_all x7 -> x6, blocking collectives: 87 us -> 76.7 us  [exchange(): return lax.all_to_all(value, axes, 0, 0, tiled=True)]
    ppermute x10 -> x16, starting transfers between devices: 5.2 us -> 9.81 us  [across(): return lax.ppermute(value, 'ch', [(i, i ^ step) for i in range(ch)])]
    all_to_all x3 -> x2, starting transfers between devices: 15 us -> 11 us  [exchange(): return lax.all_to_all(value, axes, 0, 0, tiled=True)]
    unnamed x49 -> x53, local copies, waits for them, and re-layouts: 9.61 us -> 6.3 us
    all_to_all x3 -> x2, waiting for transfers between devices: 17.2 us -> 16.9 us  [exchange(): return lax.all_to_all(value, axes, 0, 0, tiled=True)]
  transfers between devices with their start and end apart: 15 -> 20, of which waited for: 6 -> 8; matrix products, arithmetic and copies ran while one was open for 0% -> 0% of each run, Pallas kernels for 6% -> 5%
where the time goes in v4:
time: 194 us; the launch traced here: 193 us
  blocking collectives  76.7 us (40%)
  waiting for transfers between devices  49.4 us (25%)
  Pallas kernels  34.9 us (18%)
  starting transfers between devices  24.1 us (12%)
  local copies, waits for them, and re-layouts  7.68 us (4%)
    all_to_all x6, blocking collectives, exchange(): return lax.all_to_all(value, axes, 0, 0, tiled=True)  76.7 us
    pallas_call x13, Pallas kernels, call(): pl.pallas_call(body, out_shape=outs, in_specs=[vmem] * (len(operands) - f...  34.9 us
    ppermute x16, waiting for transfers between devices, across(): return lax.ppermute(value, 'ch', [(i, i ^ step) for i in range(ch)])  25.9 us
    all_to_all x2, waiting for transfers between devices, exchange(): return lax.all_to_all(value, axes, 0, 0, tiled=True)  16.9 us
    all_to_all x2, starting transfers between devices, exchange(): return lax.all_to_all(value, axes, 0, 0, tiled=True)  11 us
    ppermute x16, starting transfers between devices, across(): return lax.ppermute(value, 'ch', [(i, i ^ step) for i in range(ch)])  9.81 us
    ppermute x2, waiting for transfers between devices, beside(): return lax.ppermute(value, 'lat', [(i, i ^ 1) for i in range(plan.lat)])  6.61 us
    unnamed x53, local copies, waits for them, and re-layouts  6.3 us
  transfers between devices with their start and end apart: 20, of which 8 were waited for; matrix products, arithmetic and copies ran while one was open for 0% of the time, Pallas kernels for 5%

profile of v4, /device:TPU:0, one launch (start us, length us, event | category | flops | bytes accessed | tf_op | source)
XLA Modules:
  0.0 193.2 jit_solution(16922092620255846118)
XLA Ops:
  0.0 2.3 %shard_map.158 = (bf16[768,384]{1,0:T(8,128)(2,1)}, bf16[192,768]{1,0:T(8,128)(2,1)}, bf16[384,768]{1,0:T(8,128)(2,1)}) custom-call(bf16[768,768]{1,0:T(8,128)(2,1)} %r_2_.9, bf16[768,768]{1,0:T(8,128)(2,1)} %r_3_.4), custom_call_target="tpu_custom_call" | custom-call | flops 1000000 | bytes 1048576 | tf_op jit(solution)/shard_map/pallas_call | solution.py:555
  2.4 3.0 %collective-permute-start.5 = (bf16[768,384]{1,0:T(8,128)(2,1)}, bf16[768,384]{1,0:T(8,128)(2,1)S(1)}, u32[]{:S(2)}, u32[]{:S(2)}) collective-permute-start(bf16[768,384]{1,0:T(8,128)(2,1)} %get-tuple-element.69), channel_id=1, source_target_pairs={{0,2},{1,3},{2,0},{3,1},{4,6},{5,7},{6,4},{7,5},{8,10},{9,11},{10,... | collective-permute-start | bytes 1769480 | tf_op jit(solution)/shard_map/ppermute | solution.py:586
  6.0 1.7 collective-permute-start.2
  7.7 2.4 %shard_map.155 = (bf16[2,256,256]{2,1,0:T(8,128)(2,1)}, bf16[2,256,256]{2,1,0:T(8,128)(2,1)}, bf16[2,256,256]{2,1,0:T(8,128)(2,1)}, bf16[2,256,256]{2,1,0:T(8,12...) custom-call(f32[2,2,96,96]{3,2,1,0:T(8,128)} %r_0_.1, f32[2,2,96]{2,1,0:T(2,128)} %r_1_.4, f32[2,2,96,96]{3,2,1,0:T(8,128)} %r_2_.8, ...), custom_call_target="tpu_custom_call" | custom-call | flops 100000000 | bytes 1048576 | tf_op jit(solution)/shard_map/pallas_call | solution.py:555
  10.1 12.1 %collective-permute-done.1.r_2_ = f32[216,128]{1,0:T(8,128)S(1)} collective-permute-done((f32[216,128]{1,0:T(8,128)S(1)}, f32[216,128]{1,0:T(8,128)S(1)}, u32[]{:S(2)}, u32[]{:S(2)}) %collective-permute-start.1) | collective-permute-done | bytes 110624 | tf_op jit(solution)/shard_map/ppermute | solution.py:586
  22.9 2.0 %shard_map.156 = (f32[304,768]{1,0:T(8,128)S(1)}, bf16[32,32,128]{2,1,0:T(8,128)(2,1)}) custom-call(f32[216,128]{1,0:T(8,128)S(1)} %get-tuple-element.49.r_0_, f32[216,128]{1,0:T(8,128)S(1)} %collective-permute-done.r_1_, f32[216,128]{1,0:T(8,128)S(1)} %collective-permute-done.1.r_2_, f32[216,128]{1,0:T(8,128)S(1)} %collective-permute-done.2.r_3_, ...), custom_call_target="tpu_custom_call" | custom-call | flops 1000000000 | bytes 1048576 | tf_op jit(solution)/shard_map/pallas_call | solution.py:555
  25.9 6.3 %all-to-all-start = ((bf16[32,32,128]{2,1,0:T(8,128)(2,1)}), bf16[32,32,128]{2,1,0:T(8,128)(2,1)S(1)}, u32[]{:S(2)}, u32[]{:S(2)}) async-start(bf16[32,32,128]{2,1,0:T(8,128)(2,1)} %get-tuple-element.60), calls=%async_computation | async-start | bytes 524288 | tf_op jit(solution)/shard_map/all_to_all | solution.py:592
  32.2 1.8 collective-permute-start.9
  34.3 1.8 collective-permute-start.6
  36.0 6.7 %all-to-all-done.r_0_ = bf16[32,32,128]{2,1,0:T(8,128)(2,1)S(1)} async-done(((bf16[32,32,128]{2,1,0:T(8,128)(2,1)}), bf16[32,32,128]{2,1,0:T(8,128)(2,1)S(1)}, u32[]{:S(2)}, u32[]{:S(2)}) %all-to-all-start) | async-done | bytes 262176 | tf_op jit(solution)/shard_map/all_to_all | solution.py:592
  43.4 5.7 %shard_map.157 = (bf16[32,32,128]{2,1,0:T(8,128)(2,1)}, bf16[216,576]{1,0:T(8,128)(2,1)}, bf16[216,576]{1,0:T(8,128)(2,1)}, bf16[288,432]{1,0:T(8,128)(2,1)}, bf16[288,432]{1,0:T(8,128)(2,1)}) custom-call(bf16[32,32,128]{2,1,0:T(8,128)(2,1)} %copy-done.24, f32[216,8]{1,0:T(8,128)} %constant.13.clone.r_1_, f32[8,288]{1,0:T(8,128)} %constant.14.clone.r_2_, ...), custom_call_target="tpu_custom_call" | custom-call | flops 1000000000 | bytes 1048576 | tf_op jit(solution)/shard_map/pallas_call | solution.py:555
  49.2 7.6 %collective-permute-done.7.r_8_ = bf16[192,768]{1,0:T(8,128)(2,1)S(1)} collective-permute-done((bf16[192,768]{1,0:T(8,128)(2,1)}, bf16[192,768]{1,0:T(8,128)(2,1)S(1)}, u32[]{:S(2)}, u32[]{:S(2)}) %collective-permute-start.7) | collective-permute-done | bytes 294944 | tf_op jit(solution)/shard_map/ppermute | solution.py:586
  56.8 1.6 collective-permute-start.8
  59.6 6.6 %collective-permute-done.8.r_9_ = bf16[192,768]{1,0:T(8,128)(2,1)S(1)} collective-permute-done((bf16[192,768]{1,0:T(8,128)(2,1)S(1)}, bf16[192,768]{1,0:T(8,128)(2,1)S(1)}, u32[]{:S(2)}, u32[]{:S(2)}) %collective-permute-start.8) | collective-permute-done | bytes 294944 | tf_op jit(solution)/shard_map/ppermute | solution.py:589
  66.9 4.7 %all-to-all-start.1 = ((bf16[32,32,128]{2,1,0:T(8,128)(2,1)}), bf16[32,32,128]{2,1,0:T(8,128)(2,1)S(1)}, u32[]{:S(2)}, u32[]{:S(2)}) async-start(bf16[32,32,128]{2,1,0:T(8,128)(2,1)} %get-tuple-element.67), calls=%async_computation.1 | async-start | bytes 524288 | tf_op jit(solution)/shard_map/all_to_all | solution.py:592
  71.9 10.2 %all-to-all-done.1.r_0_ = bf16[32,32,128]{2,1,0:T(8,128)(2,1)S(1)} async-done(((bf16[32,32,128]{2,1,0:T(8,128)(2,1)}), bf16[32,32,128]{2,1,0:T(8,128)(2,1)S(1)}, u32[]{:S(2)}, u32[]{:S(2)}) %all-to-all-start.1) | async-done | bytes 262176 | tf_op jit(solution)/shard_map/all_to_all | solution.py:592
  85.4 5.5 %shard_map.159 = (f32[144,768]{1,0:T(8,128)S(1)}, bf16[32,32,128]{2,1,0:T(8,128)(2,1)S(1)}, f32[16,768]{1,0:T(8,128)S(1)}, bf16[768,3072]{1,0:T(8,128)(2,1)S(1)}, bf16[3072,768]{1,0:T(8,128)(2,1)S(1)}) custom-call(bf16[32,32,128]{2,1,0:T(8,128)(2,1)S(1)} %all-to-all-done.1.r_0_, f32[304,768]{1,0:T(8,128)S(1)} %copy-done.22, bf16[768,768]{1,0:T(8,128)(2,1)S(1)} %copy-done, ...), custom_call_target="tpu_custom_call" | custom-call | flops 10000000000 | bytes 1048576 | tf_op jit(solution)/shard_map/pallas_call | solution.py:555
  90.9 12.8 %all_to_all.40.r_0_ = bf16[32,32,128]{2,1,0:T(8,128)(2,1)S(1)} all-to-all(bf16[32,32,128]{2,1,0:T(8,128)(2,1)S(1)} %get-tuple-element.76), channel_id=1, replica_groups=mesh['lat'=8,'ch'=4] {'lat','ch'}, dimensions={0} | all-to-all | bytes 524288 | tf_op jit(solution)/shard_map/all_to_all | solution.py:592
  103.8 1.7 shard_map.160
  105.5 12.8 %all_to_all.41.r_0_ = bf16[32,32,128]{2,1,0:T(8,128)(2,1)S(1)} all-to-all(bf16[32,32,128]{2,1,0:T(8,128)(2,1)S(1)} %shard_map.160), channel_id=1, replica_groups=mesh['lat'=8,'ch'=4] {'lat','ch'}, dimensions={0} | all-to-all | bytes 524288 | tf_op jit(solution)/shard_map/all_to_all | solution.py:592
  118.3 3.9 %shard_map.161 = (f32[144,768]{1,0:T(8,128)S(1)}, bf16[32,32,128]{2,1,0:T(8,128)(2,1)S(1)}) custom-call(bf16[32,32,128]{2,1,0:T(8,128)(2,1)S(1)} %all_to_all.41.r_0_, f32[144,768]{1,0:T(8,128)S(1)} %get-tuple-element.81.r_1_, bf16[4,144,144]{2,1,0:T(8,128)(2,1)S(1)} %copy-done.15, f32[16,768]{1,0:T(8,128)S(1)} %get-tuple-element.82.r_3_, ...), custom_call_target="tpu_custom_call" | custom-call | flops 10000000000 | bytes 1048576 | tf_op jit(solution)/shard_map/pallas_call | solution.py:555
  122.2 12.8 %all_to_all.42.r_0_ = bf16[32,32,128]{2,1,0:T(8,128)(2,1)S(1)} all-to-all(bf16[32,32,128]{2,1,0:T(8,128)(2,1)S(1)} %get-tuple-element.85), channel_id=1, replica_groups=mesh['lat'=8,'ch'=4] {'lat','ch'}, dimensions={0} | all-to-all | bytes 524288 | tf_op jit(solution)/shard_map/all_to_all | solution.py:592
  135.0 1.7 shard_map.162
  136.7 12.8 %all_to_all.43.r_0_ = bf16[32,32,128]{2,1,0:T(8,128)(2,1)S(1)} all-to-all(bf16[32,32,128]{2,1,0:T(8,128)(2,1)S(1)} %shard_map.162), channel_id=1, replica_groups=mesh['lat'=8,'ch'=4] {'lat','ch'}, dimensions={0} | all-to-all | bytes 524288 | tf_op jit(solution)/shard_map/all_to_all | solution.py:592
  149.5 3.9 %shard_map.163 = (f32[144,768]{1,0:T(8,128)S(1)}, bf16[32,32,128]{2,1,0:T(8,128)(2,1)S(1)}) custom-call(bf16[32,32,128]{2,1,0:T(8,128)(2,1)S(1)} %all_to_all.43.r_0_, f32[144,768]{1,0:T(8,128)S(1)} %get-tuple-element.86.r_1_, bf16[4,144,144]{2,1,0:T(8,128)(2,1)S(1)} %copy-done.15, f32[16,768]{1,0:T(8,128)S(1)} %get-tuple-element.82.r_3_, ...), custom_call_target="tpu_custom_call" | custom-call | flops 10000000000 | bytes 1048576 | tf_op jit(solution)/shard_map/pallas_call | solution.py:555
  153.4 12.8 %all_to_all.44.r_0_ = bf16[32,32,128]{2,1,0:T(8,128)(2,1)S(1)} all-to-all(bf16[32,32,128]{2,1,0:T(8,128)(2,1)S(1)} %get-tuple-element.87), channel_id=1, replica_groups=mesh['lat'=8,'ch'=4] {'lat','ch'}, dimensions={0} | all-to-all | bytes 524288 | tf_op jit(solution)/shard_map/all_to_all | solution.py:592
  166.2 1.7 shard_map.164
  167.9 12.8 %all_to_all.45.r_0_ = bf16[32,32,128]{2,1,0:T(8,128)(2,1)S(1)} all-to-all(bf16[32,32,128]{2,1,0:T(8,128)(2,1)S(1)} %shard_map.164), channel_id=1, replica_groups=mesh['lat'=8,'ch'=4] {'lat','ch'}, dimensions={0} | all-to-all | bytes 524288 | tf_op jit(solution)/shard_map/all_to_all | solution.py:592
  180.7 3.5 %shard_map.165 = (f32[216,128]{1,0:T(8,128)S(1)}, f32[216,128]{1,0:T(8,128)S(1)}, f32[216,128]{1,0:T(8,128)S(1)}, f32[216,128]{1,0:T(8,128)S(1)}) custom-call(bf16[32,32,128]{2,1,0:T(8,128)(2,1)S(1)} %all_to_all.45.r_0_, f32[144,768]{1,0:T(8,128)S(1)} %get-tuple-element.88.r_1_, bf16[4,144,144]{2,1,0:T(8,128)(2,1)S(1)} %copy-done.15, ...), custom_call_target="tpu_custom_call" | custom-call | flops 10000000000 | bytes 1048576 | tf_op jit(solution)/shard_map/pallas_call | solution.py:555
  186.2 4.1 %collective-permute-done.16.r_2_ = f32[216,128]{1,0:T(8,128)S(1)} collective-permute-done((f32[216,128]{1,0:T(8,128)S(1)}, f32[216,128]{1,0:T(8,128)S(1)}, u32[]{:S(2)}, u32[]{:S(2)}) %collective-permute-start.16) | collective-permute-done | bytes 110624 | tf_op jit(solution)/shard_map/ppermute | solution.py:586
  190.3 1.3 collective-permute-done.17.r_3_
  191.8 1.4 copy.17
  (82 shorter events, 10.8 us)
Async XLA Ops:
  2.3 20.6 %copy-start.14 = (bf16[4,144,144]{2,1,0:T(8,128)(2,1)S(1)}, bf16[4,144,144]{2,1,0:T(8,128)(2,1)}, u32[]{:S(2)}) copy-start(bf16[4,144,144]{2,1,0:T(8,128)(2,1)} %constant.12.clone.r_4_.r_2_) | copy-start | bytes 497668
  2.4 31.9 %collective-permute-start.5 = (bf16[768,384]{1,0:T(8,128)(2,1)}, bf16[768,384]{1,0:T(8,128)(2,1)S(1)}, u32[]{:S(2)}, u32[]{:S(2)}) collective-permute-start(bf16[768,384]{1,0:T(8,128)(2,1)} %get-tuple-element.69), channel_id=1, source_target_pairs={{0,2},{1,3},{2,0},{3,1},{4,6},{5,7},{6,4},{7,5},{8,10},{9,11},{10,... | collective-permute-start | bytes 1769480 | tf_op jit(solution)/shard_map/ppermute | solution.py:586
  5.8 4.3 %collective-permute-start = (f32[216,128]{1,0:T(8,128)S(1)}, f32[216,128]{1,0:T(8,128)S(1)}, u32[]{:S(2)}, u32[]{:S(2)}) collective-permute-start(f32[216,128]{1,0:T(8,128)S(1)} %get-tuple-element.50), channel_id=1, source_target_pairs={{0,1},{1,0},{2,3},{3,2},{4,5},{5,4},{6,7},{7,6},{8,9},{9,8},{10,11... | collective-permute-start | bytes 331784 | tf_op jit(solution)/shard_map/ppermute | solution.py:586
  5.9 16.3 %collective-permute-start.1 = (f32[216,128]{1,0:T(8,128)S(1)}, f32[216,128]{1,0:T(8,128)S(1)}, u32[]{:S(2)}, u32[]{:S(2)}) collective-permute-start(f32[216,128]{1,0:T(8,128)S(1)} %get-tuple-element.58), channel_id=1, source_target_pairs={{0,2},{1,3},{2,0},{3,1},{4,6},{5,7},{6,4},{7,5},{8,10},{9,11},{10,... | collective-permute-start | bytes 331784 | tf_op jit(solution)/shard_map/ppermute | solution.py:586
  6.0 17.0 %collective-permute-start.2 = (f32[216,128]{1,0:T(8,128)S(1)}, f32[216,128]{1,0:T(8,128)S(1)}, u32[]{:S(2)}, u32[]{:S(2)}) collective-permute-start(f32[216,128]{1,0:T(8,128)S(1)} %get-tuple-element.59), channel_id=1, source_target_pairs={{0,3},{1,2},{2,1},{3,0},{4,7},{5,6},{6,5},{7,4},{8,11},{9,10},{10,... | collective-permute-start | bytes 331784 | tf_op jit(solution)/shard_map/ppermute | solution.py:586
  25.9 16.8 %all-to-all-start = ((bf16[32,32,128]{2,1,0:T(8,128)(2,1)}), bf16[32,32,128]{2,1,0:T(8,128)(2,1)S(1)}, u32[]{:S(2)}, u32[]{:S(2)}) async-start(bf16[32,32,128]{2,1,0:T(8,128)(2,1)} %get-tuple-element.60), calls=%async_computation | async-start | bytes 524288 | tf_op jit(solution)/shard_map/all_to_all | solution.py:592
  32.2 24.6 %collective-permute-start.9 = (bf16[384,768]{1,0:T(8,128)(2,1)}, bf16[384,768]{1,0:T(8,128)(2,1)}, u32[]{:S(2)}, u32[]{:S(2)}) collective-permute-start(bf16[384,768]{1,0:T(8,128)(2,1)} %get-tuple-element.72), channel_id=1, source_target_pairs={{0,2},{1,3},{2,0},{3,1},{4,6},{5,7},{6,4},{7,5},{8,10},{9,11},{10,... | collective-permute-start | bytes 1769480 | tf_op jit(solution)/shard_map/ppermute | solution.py:586
  34.0 37.6 %collective-permute-start.3 = (bf16[768,768]{1,0:T(8,128)(2,1)S(1)}, bf16[768,768]{1,0:T(8,128)(2,1)}, u32[]{:S(2)}, u32[]{:S(2)}) collective-permute-start(bf16[768,768]{1,0:T(8,128)(2,1)S(1)} %copy-done), channel_id=1, source_target_pairs={{0,1},{1,0},{2,3},{3,2},{4,5},{5,4},{6,7},{7,6},{8,9},{9,8},{10,11... | collective-permute-start | bytes 3538952 | tf_op jit(solution)/shard_map/ppermute | solution.py:586
  34.0 22.8 %collective-permute-start.7 = (bf16[192,768]{1,0:T(8,128)(2,1)}, bf16[192,768]{1,0:T(8,128)(2,1)S(1)}, u32[]{:S(2)}, u32[]{:S(2)}) collective-permute-start(bf16[192,768]{1,0:T(8,128)(2,1)} %get-tuple-element.70), channel_id=1, source_target_pairs={{0,2},{1,3},{2,0},{3,1},{4,6},{5,7},{6,4},{7,5},{8,10},{9,11},{10,... | collective-permute-start | bytes 884744 | tf_op jit(solution)/shard_map/ppermute | solution.py:586
  34.3 24.1 %collective-permute-start.6 = (bf16[768,384]{1,0:T(8,128)(2,1)S(1)}, bf16[768,384]{1,0:T(8,128)(2,1)}, u32[]{:S(2)}, u32[]{:S(2)}) collective-permute-start(bf16[768,384]{1,0:T(8,128)(2,1)S(1)} %collective-permute-done.5.r_6_), channel_id=1, source_target_pairs={{0,4},{4,0},{8,12},{12,8},{16,20},{20,16},{24,28},{28,24},{1,5},{5... | collective-permute-start | bytes 1769480 | tf_op jit(solution)/shard_map/ppermute | solution.py:589
  36.0 46.2 %collective-permute-start.4 = (bf16[768,768]{1,0:T(8,128)(2,1)S(1)}, bf16[768,768]{1,0:T(8,128)(2,1)}, u32[]{:S(2)}, u32[]{:S(2)}) collective-permute-start(bf16[768,768]{1,0:T(8,128)(2,1)S(1)} %copy-done.1), channel_id=1, source_target_pairs={{0,1},{1,0},{2,3},{3,2},{4,5},{5,4},{6,7},{7,6},{8,9},{9,8},{10,11... | collective-permute-start | bytes 3538952 | tf_op jit(solution)/shard_map/ppermute | solution.py:586
  56.7 1.8 collective-permute-start.12
  56.8 9.4 %collective-permute-start.8 = (bf16[192,768]{1,0:T(8,128)(2,1)S(1)}, bf16[192,768]{1,0:T(8,128)(2,1)S(1)}, u32[]{:S(2)}, u32[]{:S(2)}) collective-permute-start(bf16[192,768]{1,0:T(8,128)(2,1)S(1)} %collective-permute-done.7.r_8_), channel_id=1, source_target_pairs={{0,4},{4,0},{8,12},{12,8},{16,20},{20,16},{24,28},{28,24},{1,5},{5... | collective-permute-start | bytes 884744 | tf_op jit(solution)/shard_map/ppermute | solution.py:589
  58.3 23.9 %collective-permute-start.10 = (bf16[768,384]{1,0:T(8,128)(2,1)S(1)}, bf16[768,384]{1,0:T(8,128)(2,1)}, u32[]{:S(2)}, u32[]{:S(2)}) collective-permute-start(bf16[768,384]{1,0:T(8,128)(2,1)S(1)} %collective-permute-done.5.r_6_), channel_id=1, source_target_pairs={{0,1},{1,0},{2,3},{3,2},{4,5},{5,4},{6,7},{7,6},{8,9},{9,8},{10,11... | collective-permute-start | bytes 1769480 | tf_op jit(solution)/shard_map/ppermute | solution.py:586
  59.3 22.9 %collective-permute-start.14 = (bf16[384,768]{1,0:T(8,128)(2,1)}, bf16[384,768]{1,0:T(8,128)(2,1)}, u32[]{:S(2)}, u32[]{:S(2)}) collective-permute-start(bf16[384,768]{1,0:T(8,128)(2,1)} %collective-permute-done.9.r_10_), channel_id=1, source_target_pairs={{0,1},{1,0},{2,3},{3,2},{4,5},{5,4},{6,7},{7,6},{8,9},{9,8},{10,11... | collective-permute-start | bytes 1769480 | tf_op jit(solution)/shard_map/ppermute | solution.py:586
  66.9 15.3 %collective-permute-start.11 = (bf16[768,384]{1,0:T(8,128)(2,1)}, bf16[768,384]{1,0:T(8,128)(2,1)}, u32[]{:S(2)}, u32[]{:S(2)}) collective-permute-start(bf16[768,384]{1,0:T(8,128)(2,1)} %collective-permute-done.6.r_7_), channel_id=1, source_target_pairs={{0,1},{1,0},{2,3},{3,2},{4,5},{5,4},{6,7},{7,6},{8,9},{9,8},{10,11... | collective-permute-start | bytes 1769480 | tf_op jit(solution)/shard_map/ppermute | solution.py:586
  66.9 15.3 %all-to-all-start.1 = ((bf16[32,32,128]{2,1,0:T(8,128)(2,1)}), bf16[32,32,128]{2,1,0:T(8,128)(2,1)S(1)}, u32[]{:S(2)}, u32[]{:S(2)}) async-start(bf16[32,32,128]{2,1,0:T(8,128)(2,1)} %get-tuple-element.67), calls=%async_computation.1 | async-start | bytes 524288 | tf_op jit(solution)/shard_map/all_to_all | solution.py:592
  71.6 10.6 %collective-permute-start.13 = (bf16[192,768]{1,0:T(8,128)(2,1)}, bf16[192,768]{1,0:T(8,128)(2,1)}, u32[]{:S(2)}, u32[]{:S(2)}) collective-permute-start(bf16[192,768]{1,0:T(8,128)(2,1)} %copy-done.6), channel_id=1, source_target_pairs={{0,1},{1,0},{2,3},{3,2},{4,5},{5,4},{6,7},{7,6},{8,9},{9,8},{10,11... | collective-permute-start | bytes 884744 | tf_op jit(solution)/shard_map/ppermute | solution.py:586
  85.3 18.4 %copy-start.8 = (bf16[2,256,256]{2,1,0:T(8,128)(2,1)S(1)}, bf16[2,256,256]{2,1,0:T(8,128)(2,1)}, u32[]{:S(2)}) copy-start(bf16[2,256,256]{2,1,0:T(8,128)(2,1)} %get-tuple-element.61.r_6_.r_5_) | copy-start | bytes 786436
  85.3 18.4 %copy-start.9 = (bf16[2,256,256]{2,1,0:T(8,128)(2,1)S(1)}, bf16[2,256,256]{2,1,0:T(8,128)(2,1)}, u32[]{:S(2)}) copy-start(bf16[2,256,256]{2,1,0:T(8,128)(2,1)} %get-tuple-element.62.r_7_.r_6_) | copy-start | bytes 786436
  85.3 18.4 %copy-start.10 = (bf16[2,256,256]{2,1,0:T(8,128)(2,1)S(1)}, bf16[2,256,256]{2,1,0:T(8,128)(2,1)}, u32[]{:S(2)}) copy-start(bf16[2,256,256]{2,1,0:T(8,128)(2,1)} %get-tuple-element.63.r_8_.r_7_) | copy-start | bytes 786436
  85.3 18.4 %copy-start.11 = (bf16[2,256,256]{2,1,0:T(8,128)(2,1)S(1)}, bf16[2,256,256]{2,1,0:T(8,128)(2,1)}, u32[]{:S(2)}) copy-start(bf16[2,256,256]{2,1,0:T(8,128)(2,1)} %get-tuple-element.64.r_9_.r_8_) | copy-start | bytes 786436
  85.3 18.4 %copy-start.12 = (f32[1,384]{1,0:T(1,128)S(1)}, f32[1,384]{1,0:T(1,128)}, u32[]{:S(2)}) copy-start(f32[1,384]{1,0:T(1,128)} %get-tuple-element.65.r_10_.r_9_) | copy-start | bytes 4612
  85.3 18.4 %copy-start.13 = (f32[1,384]{1,0:T(1,128)S(1)}, f32[1,384]{1,0:T(1,128)}, u32[]{:S(2)}) copy-start(f32[1,384]{1,0:T(1,128)} %get-tuple-element.66.r_11_.r_10_) | copy-start | bytes 4612
  85.4 18.4 %copy-start.16 = (f32[216,128]{1,0:T(8,128)S(1)}, f32[216,128]{1,0:T(8,128)}, u32[]{:S(2)}) copy-start(f32[216,128]{1,0:T(8,128)} %constant.17.clone.r_5_.r_11_) | copy-start | bytes 331780
  85.4 18.4 %copy-start.17 = (bf16[288,432]{1,0:T(8,128)(2,1)S(1)}, bf16[288,432]{1,0:T(8,128)(2,1)}, u32[]{:S(2)}) copy-start(bf16[288,432]{1,0:T(8,128)(2,1)} %get-tuple-element.79.r_3_) | copy-start | bytes 746500
  85.4 18.4 %copy-start.18 = (bf16[288,432]{1,0:T(8,128)(2,1)S(1)}, bf16[288,432]{1,0:T(8,128)(2,1)}, u32[]{:S(2)}) copy-start(bf16[288,432]{1,0:T(8,128)(2,1)} %get-tuple-element.80.r_4_) | copy-start | bytes 746500
  85.4 18.4 %copy-start.19 = (bf16[216,576]{1,0:T(8,128)(2,1)S(1)}, bf16[216,576]{1,0:T(8,128)(2,1)}, u32[]{:S(2)}) copy-start(bf16[216,576]{1,0:T(8,128)(2,1)} %get-tuple-element.77.r_1_) | copy-start | bytes 746500
  85.4 18.4 %copy-start.20 = (bf16[216,576]{1,0:T(8,128)(2,1)S(1)}, bf16[216,576]{1,0:T(8,128)(2,1)}, u32[]{:S(2)}) copy-start(bf16[216,576]{1,0:T(8,128)(2,1)} %get-tuple-element.78.r_2_) | copy-start | bytes 746500
  184.2 1.9 collective-permute-start.15
  184.3 6.0 %collective-permute-start.16 = (f32[216,128]{1,0:T(8,128)S(1)}, f32[216,128]{1,0:T(8,128)S(1)}, u32[]{:S(2)}, u32[]{:S(2)}) collective-permute-start(f32[216,128]{1,0:T(8,128)S(1)} %get-tuple-element.91), channel_id=1, source_target_pairs={{0,2},{1,3},{2,0},{3,1},{4,6},{5,7},{6,4},{7,5},{8,10},{9,11},{10,... | collective-permute-start | bytes 331784 | tf_op jit(solution)/shard_map/ppermute | solution.py:586
  185.1 6.5 %collective-permute-start.17 = (f32[216,128]{1,0:T(8,128)S(1)}, f32[216,128]{1,0:T(8,128)S(1)}, u32[]{:S(2)}, u32[]{:S(2)}) collective-permute-start(f32[216,128]{1,0:T(8,128)S(1)} %get-tuple-element.92), channel_id=1, source_target_pairs={{0,3},{1,2},{2,1},{3,0},{4,7},{5,6},{6,5},{7,4},{8,11},{9,10},{10,... | collective-permute-start | bytes 331784 | tf_op jit(solution)/shard_map/ppermute | solution.py:586
  (14 other events, 66.6 us)

commit v5 on v4

--- a/solution.py
+++ b/solution.py
@@ -232,7 +232,7 @@
     tail[:, :, :HALF] = state_ref[:, :, LANES:]
     for copy in copies:
         copy.wait()
-    line = up_ref[...].astype(F32)
+    line = up_ref[...].astype(F32).reshape(1, -1)
     small = [gain_ref[...].astype(F32), bias_ref[...].astype(F32)]
     small += [line[:, n * plan.wide : (n + 1) * plan.wide] for n in range(plan.ch)]
     small = jnp.concatenate(small, 0)
@@ -599,11 +599,11 @@
     tokens = call(
         lambda *r: pack_kernel(plan, *r),
         message,
-        (state[0], norm_gains, channel_biases, up_bias.reshape(1, ch * wide)),
+        (state[0], norm_gains, channel_biases, up_bias),
         [pltpu.VMEM((plan.tokens, wide), F32)]
         + [pltpu.VMEM((rows, width, LANES), F32)] * 2
         + [mail]
-        + [pltpu.VMEM(v.shape, BF) for v in (norm_gains, channel_biases, up_bias.reshape(1, -1))]
+        + [pltpu.VMEM(v.shape, BF) for v in (norm_gains, channel_biases, up_bias)]
         + [pltpu.SemaphoreType.DMA((3,))],
         10**8,
         far_in=3,

time: 194 us -> 194 us (level)
  no operation moved by 1% of the time
where the time goes in v5:
time: 194 us; the launch traced here: 193 us
  blocking collectives  76.7 us (40%)
  waiting for transfers between devices  49.4 us (25%)
  Pallas kernels  34.9 us (18%)
  starting transfers between devices  24.1 us (12%)
  local copies, waits for them, and re-layouts  7.68 us (4%)
    all_to_all x6, blocking collectives, exchange(): return lax.all_to_all(value, axes, 0, 0, tiled=True)  76.7 us
    pallas_call x13, Pallas kernels, call(): pl.pallas_call(body, out_shape=outs, in_specs=[vmem] * (len(operands) - f...  34.9 us
    ppermute x16, waiting for transfers between devices, across(): return lax.ppermute(value, 'ch', [(i, i ^ step) for i in range(ch)])  25.9 us
    all_to_all x2, waiting for transfers between devices, exchange(): return lax.all_to_all(value, axes, 0, 0, tiled=True)  16.9 us
    all_to_all x2, starting transfers between devices, exchange(): return lax.all_to_all(value, axes, 0, 0, tiled=True)  11 us
    ppermute x16, starting transfers between devices, across(): return lax.ppermute(value, 'ch', [(i, i ^ step) for i in range(ch)])  9.81 us
    ppermute x2, waiting for transfers between devices, beside(): return lax.ppermute(value, 'lat', [(i, i ^ 1) for i in range(plan.lat)])  6.61 us
    unnamed x53, local copies, waits for them, and re-layouts  6.31 us
  transfers between devices with their start and end apart: 20, of which 8 were waited for; matrix products, arithmetic and copies ran while one was open for 0% of the time, Pallas kernels for 5%

profile of v5, /device:TPU:0, one launch (start us, length us, event | category | flops | bytes accessed | tf_op | source)
XLA Modules:
  0.0 193.2 jit_solution(12875793598910353581)
XLA Ops:
  0.0 2.3 %shard_map.158 = (bf16[768,384]{1,0:T(8,128)(2,1)}, bf16[192,768]{1,0:T(8,128)(2,1)}, bf16[384,768]{1,0:T(8,128)(2,1)}) custom-call(bf16[768,768]{1,0:T(8,128)(2,1)} %r_2_.9, bf16[768,768]{1,0:T(8,128)(2,1)} %r_3_.6), custom_call_target="tpu_custom_call" | custom-call | flops 1000000 | bytes 1048576 | tf_op jit(solution)/shard_map/pallas_call | solution.py:555
  2.4 3.0 %collective-permute-start.5 = (bf16[768,384]{1,0:T(8,128)(2,1)}, bf16[768,384]{1,0:T(8,128)(2,1)S(1)}, u32[]{:S(2)}, u32[]{:S(2)}) collective-permute-start(bf16[768,384]{1,0:T(8,128)(2,1)} %get-tuple-element.69), channel_id=1, source_target_pairs={{0,2},{1,3},{2,0},{3,1},{4,6},{5,7},{6,4},{7,5},{8,10},{9,11},{10,... | collective-permute-start | bytes 1769480 | tf_op jit(solution)/shard_map/ppermute | solution.py:586
  5.9 1.8 collective-permute-start.2
  7.7 2.4 %shard_map.155 = (bf16[2,256,256]{2,1,0:T(8,128)(2,1)}, bf16[2,256,256]{2,1,0:T(8,128)(2,1)}, bf16[2,256,256]{2,1,0:T(8,128)(2,1)}, bf16[2,256,256]{2,1,0:T(8,12...) custom-call(f32[2,2,96,96]{3,2,1,0:T(8,128)} %r_0_.1, f32[2,2,96]{2,1,0:T(2,128)} %r_1_.4, f32[2,2,96,96]{3,2,1,0:T(8,128)} %r_2_.8, ...), custom_call_target="tpu_custom_call" | custom-call | flops 100000000 | bytes 1048576 | tf_op jit(solution)/shard_map/pallas_call | solution.py:555
  10.1 12.1 %collective-permute-done.1.r_2_ = f32[216,128]{1,0:T(8,128)S(1)} collective-permute-done((f32[216,128]{1,0:T(8,128)S(1)}, f32[216,128]{1,0:T(8,128)S(1)}, u32[]{:S(2)}, u32[]{:S(2)}) %collective-permute-start.1) | collective-permute-done | bytes 110624 | tf_op jit(solution)/shard_map/ppermute | solution.py:586
  22.9 2.0 %shard_map.156 = (f32[304,768]{1,0:T(8,128)S(1)}, bf16[32,32,128]{2,1,0:T(8,128)(2,1)}) custom-call(f32[216,128]{1,0:T(8,128)S(1)} %get-tuple-element.49.r_0_, f32[216,128]{1,0:T(8,128)S(1)} %collective-permute-done.r_1_, f32[216,128]{1,0:T(8,128)S(1)} %collective-permute-done.1.r_2_, f32[216,128]{1,0:T(8,128)S(1)} %collective-permute-done.2.r_3_, ...), custom_call_target="tpu_custom_call" | custom-call | flops 1000000000 | bytes 1048576 | tf_op jit(solution)/shard_map/pallas_call | solution.py:555
  25.9 6.3 %all-to-all-start = ((bf16[32,32,128]{2,1,0:T(8,128)(2,1)}), bf16[32,32,128]{2,1,0:T(8,128)(2,1)S(1)}, u32[]{:S(2)}, u32[]{:S(2)}) async-start(bf16[32,32,128]{2,1,0:T(8,128)(2,1)} %get-tuple-element.60), calls=%async_computation | async-start | bytes 524288 | tf_op jit(solution)/shard_map/all_to_all | solution.py:592
  32.2 1.8 collective-permute-start.9
  34.3 1.8 collective-permute-start.6
  36.0 6.7 %all-to-all-done.r_0_ = bf16[32,32,128]{2,1,0:T(8,128)(2,1)S(1)} async-done(((bf16[32,32,128]{2,1,0:T(8,128)(2,1)}), bf16[32,32,128]{2,1,0:T(8,128)(2,1)S(1)}, u32[]{:S(2)}, u32[]{:S(2)}) %all-to-all-start) | async-done | bytes 262176 | tf_op jit(solution)/shard_map/all_to_all | solution.py:592
  43.4 5.7 %shard_map.157 = (bf16[32,32,128]{2,1,0:T(8,128)(2,1)}, bf16[216,576]{1,0:T(8,128)(2,1)}, bf16[216,576]{1,0:T(8,128)(2,1)}, bf16[288,432]{1,0:T(8,128)(2,1)}, bf16[288,432]{1,0:T(8,128)(2,1)}) custom-call(bf16[32,32,128]{2,1,0:T(8,128)(2,1)} %copy-done.25, f32[216,8]{1,0:T(8,128)} %constant.13.clone.r_1_, f32[8,288]{1,0:T(8,128)} %constant.14.clone.r_2_, ...), custom_call_target="tpu_custom_call" | custom-call | flops 1000000000 | bytes 1048576 | tf_op jit(solution)/shard_map/pallas_call | solution.py:555
  49.2 7.6 %collective-permute-done.7.r_8_ = bf16[192,768]{1,0:T(8,128)(2,1)S(1)} collective-permute-done((bf16[192,768]{1,0:T(8,128)(2,1)}, bf16[192,768]{1,0:T(8,128)(2,1)S(1)}, u32[]{:S(2)}, u32[]{:S(2)}) %collective-permute-start.7) | collective-permute-done | bytes 294944 | tf_op jit(solution)/shard_map/ppermute | solution.py:586
  56.8 1.6 collective-permute-start.8
  59.6 6.6 %collective-permute-done.8.r_9_ = bf16[192,768]{1,0:T(8,128)(2,1)S(1)} collective-permute-done((bf16[192,768]{1,0:T(8,128)(2,1)S(1)}, bf16[192,768]{1,0:T(8,128)(2,1)S(1)}, u32[]{:S(2)}, u32[]{:S(2)}) %collective-permute-start.8) | collective-permute-done | bytes 294944 | tf_op jit(solution)/shard_map/ppermute | solution.py:589
  66.9 4.7 %all-to-all-start.1 = ((bf16[32,32,128]{2,1,0:T(8,128)(2,1)}), bf16[32,32,128]{2,1,0:T(8,128)(2,1)S(1)}, u32[]{:S(2)}, u32[]{:S(2)}) async-start(bf16[32,32,128]{2,1,0:T(8,128)(2,1)} %get-tuple-element.67), calls=%async_computation.1 | async-start | bytes 524288 | tf_op jit(solution)/shard_map/all_to_all | solution.py:592
  71.9 10.2 %all-to-all-done.1.r_0_ = bf16[32,32,128]{2,1,0:T(8,128)(2,1)S(1)} async-done(((bf16[32,32,128]{2,1,0:T(8,128)(2,1)}), bf16[32,32,128]{2,1,0:T(8,128)(2,1)S(1)}, u32[]{:S(2)}, u32[]{:S(2)}) %all-to-all-start.1) | async-done | bytes 262176 | tf_op jit(solution)/shard_map/all_to_all | solution.py:592
  85.4 5.5 %shard_map.159 = (f32[144,768]{1,0:T(8,128)S(1)}, bf16[32,32,128]{2,1,0:T(8,128)(2,1)S(1)}, f32[16,768]{1,0:T(8,128)S(1)}, bf16[768,3072]{1,0:T(8,128)(2,1)S(1)}, bf16[3072,768]{1,0:T(8,128)(2,1)S(1)}) custom-call(bf16[32,32,128]{2,1,0:T(8,128)(2,1)S(1)} %all-to-all-done.1.r_0_, f32[304,768]{1,0:T(8,128)S(1)} %copy-done.23, bf16[768,768]{1,0:T(8,128)(2,1)S(1)} %copy-done, ...), custom_call_target="tpu_custom_call" | custom-call | flops 10000000000 | bytes 1048576 | tf_op jit(solution)/shard_map/pallas_call | solution.py:555
  90.9 12.8 %all_to_all.40.r_0_ = bf16[32,32,128]{2,1,0:T(8,128)(2,1)S(1)} all-to-all(bf16[32,32,128]{2,1,0:T(8,128)(2,1)S(1)} %get-tuple-element.76), channel_id=1, replica_groups=mesh['lat'=8,'ch'=4] {'lat','ch'}, dimensions={0} | all-to-all | bytes 524288 | tf_op jit(solution)/shard_map/all_to_all | solution.py:592
  103.8 1.7 shard_map.160
  105.5 12.8 %all_to_all.41.r_0_ = bf16[32,32,128]{2,1,0:T(8,128)(2,1)S(1)} all-to-all(bf16[32,32,128]{2,1,0:T(8,128)(2,1)S(1)} %shard_map.160), channel_id=1, replica_groups=mesh['lat'=8,'ch'=4] {'lat','ch'}, dimensions={0} | all-to-all | bytes 524288 | tf_op jit(solution)/shard_map/all_to_all | solution.py:592
  118.3 3.9 %shard_map.161 = (f32[144,768]{1,0:T(8,128)S(1)}, bf16[32,32,128]{2,1,0:T(8,128)(2,1)S(1)}) custom-call(bf16[32,32,128]{2,1,0:T(8,128)(2,1)S(1)} %all_to_all.41.r_0_, f32[144,768]{1,0:T(8,128)S(1)} %get-tuple-element.81.r_1_, bf16[4,144,144]{2,1,0:T(8,128)(2,1)S(1)} %copy-done.16, f32[16,768]{1,0:T(8,128)S(1)} %get-tuple-element.82.r_3_, ...), custom_call_target="tpu_custom_call" | custom-call | flops 10000000000 | bytes 1048576 | tf_op jit(solution)/shard_map/pallas_call | solution.py:555
  122.2 12.8 %all_to_all.42.r_0_ = bf16[32,32,128]{2,1,0:T(8,128)(2,1)S(1)} all-to-all(bf16[32,32,128]{2,1,0:T(8,128)(2,1)S(1)} %get-tuple-element.85), channel_id=1, replica_groups=mesh['lat'=8,'ch'=4] {'lat','ch'}, dimensions={0} | all-to-all | bytes 524288 | tf_op jit(solution)/shard_map/all_to_all | solution.py:592
  135.0 1.7 shard_map.162
  136.7 12.8 %all_to_all.43.r_0_ = bf16[32,32,128]{2,1,0:T(8,128)(2,1)S(1)} all-to-all(bf16[32,32,128]{2,1,0:T(8,128)(2,1)S(1)} %shard_map.162), channel_id=1, replica_groups=mesh['lat'=8,'ch'=4] {'lat','ch'}, dimensions={0} | all-to-all | bytes 524288 | tf_op jit(solution)/shard_map/all_to_all | solution.py:592
  149.5 3.9 %shard_map.163 = (f32[144,768]{1,0:T(8,128)S(1)}, bf16[32,32,128]{2,1,0:T(8,128)(2,1)S(1)}) custom-call(bf16[32,32,128]{2,1,0:T(8,128)(2,1)S(1)} %all_to_all.43.r_0_, f32[144,768]{1,0:T(8,128)S(1)} %get-tuple-element.86.r_1_, bf16[4,144,144]{2,1,0:T(8,128)(2,1)S(1)} %copy-done.16, f32[16,768]{1,0:T(8,128)S(1)} %get-tuple-element.82.r_3_, ...), custom_call_target="tpu_custom_call" | custom-call | flops 10000000000 | bytes 1048576 | tf_op jit(solution)/shard_map/pallas_call | solution.py:555
  153.4 12.8 %all_to_all.44.r_0_ = bf16[32,32,128]{2,1,0:T(8,128)(2,1)S(1)} all-to-all(bf16[32,32,128]{2,1,0:T(8,128)(2,1)S(1)} %get-tuple-element.87), channel_id=1, replica_groups=mesh['lat'=8,'ch'=4] {'lat','ch'}, dimensions={0} | all-to-all | bytes 524288 | tf_op jit(solution)/shard_map/all_to_all | solution.py:592
  166.2 1.7 shard_map.164
  167.9 12.8 %all_to_all.45.r_0_ = bf16[32,32,128]{2,1,0:T(8,128)(2,1)S(1)} all-to-all(bf16[32,32,128]{2,1,0:T(8,128)(2,1)S(1)} %shard_map.164), channel_id=1, replica_groups=mesh['lat'=8,'ch'=4] {'lat','ch'}, dimensions={0} | all-to-all | bytes 524288 | tf_op jit(solution)/shard_map/all_to_all | solution.py:592
  180.7 3.5 %shard_map.165 = (f32[216,128]{1,0:T(8,128)S(1)}, f32[216,128]{1,0:T(8,128)S(1)}, f32[216,128]{1,0:T(8,128)S(1)}, f32[216,128]{1,0:T(8,128)S(1)}) custom-call(bf16[32,32,128]{2,1,0:T(8,128)(2,1)S(1)} %all_to_all.45.r_0_, f32[144,768]{1,0:T(8,128)S(1)} %get-tuple-element.88.r_1_, bf16[4,144,144]{2,1,0:T(8,128)(2,1)S(1)} %copy-done.16, ...), custom_call_target="tpu_custom_call" | custom-call | flops 10000000000 | bytes 1048576 | tf_op jit(solution)/shard_map/pallas_call | solution.py:555
  186.2 4.1 %collective-permute-done.16.r_2_ = f32[216,128]{1,0:T(8,128)S(1)} collective-permute-done((f32[216,128]{1,0:T(8,128)S(1)}, f32[216,128]{1,0:T(8,128)S(1)}, u32[]{:S(2)}, u32[]{:S(2)}) %collective-permute-start.16) | collective-permute-done | bytes 110624 | tf_op jit(solution)/shard_map/ppermute | solution.py:586
  190.3 1.3 collective-permute-done.17.r_3_
  191.8 1.4 copy.17
  (81 shorter events, 10.8 us)
Async XLA Ops:
  2.3 20.6 %copy-start.15 = (bf16[4,144,144]{2,1,0:T(8,128)(2,1)S(1)}, bf16[4,144,144]{2,1,0:T(8,128)(2,1)}, u32[]{:S(2)}) copy-start(bf16[4,144,144]{2,1,0:T(8,128)(2,1)} %constant.12.clone.r_4_.r_2_) | copy-start | bytes 497668
  2.4 31.9 %collective-permute-start.5 = (bf16[768,384]{1,0:T(8,128)(2,1)}, bf16[768,384]{1,0:T(8,128)(2,1)S(1)}, u32[]{:S(2)}, u32[]{:S(2)}) collective-permute-start(bf16[768,384]{1,0:T(8,128)(2,1)} %get-tuple-element.69), channel_id=1, source_target_pairs={{0,2},{1,3},{2,0},{3,1},{4,6},{5,7},{6,4},{7,5},{8,10},{9,11},{10,... | collective-permute-start | bytes 1769480 | tf_op jit(solution)/shard_map/ppermute | solution.py:586
  5.8 4.3 %collective-permute-start = (f32[216,128]{1,0:T(8,128)S(1)}, f32[216,128]{1,0:T(8,128)S(1)}, u32[]{:S(2)}, u32[]{:S(2)}) collective-permute-start(f32[216,128]{1,0:T(8,128)S(1)} %get-tuple-element.50), channel_id=1, source_target_pairs={{0,1},{1,0},{2,3},{3,2},{4,5},{5,4},{6,7},{7,6},{8,9},{9,8},{10,11... | collective-permute-start | bytes 331784 | tf_op jit(solution)/shard_map/ppermute | solution.py:586
  5.9 16.3 %collective-permute-start.1 = (f32[216,128]{1,0:T(8,128)S(1)}, f32[216,128]{1,0:T(8,128)S(1)}, u32[]{:S(2)}, u32[]{:S(2)}) collective-permute-start(f32[216,128]{1,0:T(8,128)S(1)} %get-tuple-element.58), channel_id=1, source_target_pairs={{0,2},{1,3},{2,0},{3,1},{4,6},{5,7},{6,4},{7,5},{8,10},{9,11},{10,... | collective-permute-start | bytes 331784 | tf_op jit(solution)/shard_map/ppermute | solution.py:586
  5.9 17.0 %collective-permute-start.2 = (f32[216,128]{1,0:T(8,128)S(1)}, f32[216,128]{1,0:T(8,128)S(1)}, u32[]{:S(2)}, u32[]{:S(2)}) collective-permute-start(f32[216,128]{1,0:T(8,128)S(1)} %get-tuple-element.59), channel_id=1, source_target_pairs={{0,3},{1,2},{2,1},{3,0},{4,7},{5,6},{6,5},{7,4},{8,11},{9,10},{10,... | collective-permute-start | bytes 331784 | tf_op jit(solution)/shard_map/ppermute | solution.py:586
  25.9 16.9 %all-to-all-start = ((bf16[32,32,128]{2,1,0:T(8,128)(2,1)}), bf16[32,32,128]{2,1,0:T(8,128)(2,1)S(1)}, u32[]{:S(2)}, u32[]{:S(2)}) async-start(bf16[32,32,128]{2,1,0:T(8,128)(2,1)} %get-tuple-element.60), calls=%async_computation | async-start | bytes 524288 | tf_op jit(solution)/shard_map/all_to_all | solution.py:592
  32.2 24.6 %collective-permute-start.9 = (bf16[384,768]{1,0:T(8,128)(2,1)}, bf16[384,768]{1,0:T(8,128)(2,1)}, u32[]{:S(2)}, u32[]{:S(2)}) collective-permute-start(bf16[384,768]{1,0:T(8,128)(2,1)} %get-tuple-element.72), channel_id=1, source_target_pairs={{0,2},{1,3},{2,0},{3,1},{4,6},{5,7},{6,4},{7,5},{8,10},{9,11},{10,... | collective-permute-start | bytes 1769480 | tf_op jit(solution)/shard_map/ppermute | solution.py:586
  34.0 37.6 %collective-permute-start.3 = (bf16[768,768]{1,0:T(8,128)(2,1)S(1)}, bf16[768,768]{1,0:T(8,128)(2,1)}, u32[]{:S(2)}, u32[]{:S(2)}) collective-permute-start(bf16[768,768]{1,0:T(8,128)(2,1)S(1)} %copy-done), channel_id=1, source_target_pairs={{0,1},{1,0},{2,3},{3,2},{4,5},{5,4},{6,7},{7,6},{8,9},{9,8},{10,11... | collective-permute-start | bytes 3538952 | tf_op jit(solution)/shard_map/ppermute | solution.py:586
  34.0 22.8 %collective-permute-start.7 = (bf16[192,768]{1,0:T(8,128)(2,1)}, bf16[192,768]{1,0:T(8,128)(2,1)S(1)}, u32[]{:S(2)}, u32[]{:S(2)}) collective-permute-start(bf16[192,768]{1,0:T(8,128)(2,1)} %get-tuple-element.70), channel_id=1, source_target_pairs={{0,2},{1,3},{2,0},{3,1},{4,6},{5,7},{6,4},{7,5},{8,10},{9,11},{10,... | collective-permute-start | bytes 884744 | tf_op jit(solution)/shard_map/ppermute | solution.py:586
  34.3 24.1 %collective-permute-start.6 = (bf16[768,384]{1,0:T(8,128)(2,1)S(1)}, bf16[768,384]{1,0:T(8,128)(2,1)}, u32[]{:S(2)}, u32[]{:S(2)}) collective-permute-start(bf16[768,384]{1,0:T(8,128)(2,1)S(1)} %collective-permute-done.5.r_6_), channel_id=1, source_target_pairs={{0,4},{4,0},{8,12},{12,8},{16,20},{20,16},{24,28},{28,24},{1,5},{5... | collective-permute-start | bytes 1769480 | tf_op jit(solution)/shard_map/ppermute | solution.py:589
  36.0 46.2 %collective-permute-start.4 = (bf16[768,768]{1,0:T(8,128)(2,1)S(1)}, bf16[768,768]{1,0:T(8,128)(2,1)}, u32[]{:S(2)}, u32[]{:S(2)}) collective-permute-start(bf16[768,768]{1,0:T(8,128)(2,1)S(1)} %copy-done.1), channel_id=1, source_target_pairs={{0,1},{1,0},{2,3},{3,2},{4,5},{5,4},{6,7},{7,6},{8,9},{9,8},{10,11... | collective-permute-start | bytes 3538952 | tf_op jit(solution)/shard_map/ppermute | solution.py:586
  56.7 1.8 collective-permute-start.12
  56.8 9.4 %collective-permute-start.8 = (bf16[192,768]{1,0:T(8,128)(2,1)S(1)}, bf16[192,768]{1,0:T(8,128)(2,1)S(1)}, u32[]{:S(2)}, u32[]{:S(2)}) collective-permute-start(bf16[192,768]{1,0:T(8,128)(2,1)S(1)} %collective-permute-done.7.r_8_), channel_id=1, source_target_pairs={{0,4},{4,0},{8,12},{12,8},{16,20},{20,16},{24,28},{28,24},{1,5},{5... | collective-permute-start | bytes 884744 | tf_op jit(solution)/shard_map/ppermute | solution.py:589
  58.3 23.9 %collective-permute-start.10 = (bf16[768,384]{1,0:T(8,128)(2,1)S(1)}, bf16[768,384]{1,0:T(8,128)(2,1)}, u32[]{:S(2)}, u32[]{:S(2)}) collective-permute-start(bf16[768,384]{1,0:T(8,128)(2,1)S(1)} %collective-permute-done.5.r_6_), channel_id=1, source_target_pairs={{0,1},{1,0},{2,3},{3,2},{4,5},{5,4},{6,7},{7,6},{8,9},{9,8},{10,11... | collective-permute-start | bytes 1769480 | tf_op jit(solution)/shard_map/ppermute | solution.py:586
  59.3 22.9 %collective-permute-start.14 = (bf16[384,768]{1,0:T(8,128)(2,1)}, bf16[384,768]{1,0:T(8,128)(2,1)}, u32[]{:S(2)}, u32[]{:S(2)}) collective-permute-start(bf16[384,768]{1,0:T(8,128)(2,1)} %collective-permute-done.9.r_10_), channel_id=1, source_target_pairs={{0,1},{1,0},{2,3},{3,2},{4,5},{5,4},{6,7},{7,6},{8,9},{9,8},{10,11... | collective-permute-start | bytes 1769480 | tf_op jit(solution)/shard_map/ppermute | solution.py:586
  66.9 15.3 %collective-permute-start.11 = (bf16[768,384]{1,0:T(8,128)(2,1)}, bf16[768,384]{1,0:T(8,128)(2,1)}, u32[]{:S(2)}, u32[]{:S(2)}) collective-permute-start(bf16[768,384]{1,0:T(8,128)(2,1)} %collective-permute-done.6.r_7_), channel_id=1, source_target_pairs={{0,1},{1,0},{2,3},{3,2},{4,5},{5,4},{6,7},{7,6},{8,9},{9,8},{10,11... | collective-permute-start | bytes 1769480 | tf_op jit(solution)/shard_map/ppermute | solution.py:586
  66.9 15.3 %all-to-all-start.1 = ((bf16[32,32,128]{2,1,0:T(8,128)(2,1)}), bf16[32,32,128]{2,1,0:T(8,128)(2,1)S(1)}, u32[]{:S(2)}, u32[]{:S(2)}) async-start(bf16[32,32,128]{2,1,0:T(8,128)(2,1)} %get-tuple-element.67), calls=%async_computation.1 | async-start | bytes 524288 | tf_op jit(solution)/shard_map/all_to_all | solution.py:592
  71.6 10.6 %collective-permute-start.13 = (bf16[192,768]{1,0:T(8,128)(2,1)}, bf16[192,768]{1,0:T(8,128)(2,1)}, u32[]{:S(2)}, u32[]{:S(2)}) collective-permute-start(bf16[192,768]{1,0:T(8,128)(2,1)} %copy-done.7), channel_id=1, source_target_pairs={{0,1},{1,0},{2,3},{3,2},{4,5},{5,4},{6,7},{7,6},{8,9},{9,8},{10,11... | collective-permute-start | bytes 884744 | tf_op jit(solution)/shard_map/ppermute | solution.py:586
  85.3 18.4 %copy-start.9 = (bf16[2,256,256]{2,1,0:T(8,128)(2,1)S(1)}, bf16[2,256,256]{2,1,0:T(8,128)(2,1)}, u32[]{:S(2)}) copy-start(bf16[2,256,256]{2,1,0:T(8,128)(2,1)} %get-tuple-element.61.r_6_.r_5_) | copy-start | bytes 786436
  85.3 18.4 %copy-start.10 = (bf16[2,256,256]{2,1,0:T(8,128)(2,1)S(1)}, bf16[2,256,256]{2,1,0:T(8,128)(2,1)}, u32[]{:S(2)}) copy-start(bf16[2,256,256]{2,1,0:T(8,128)(2,1)} %get-tuple-element.62.r_7_.r_6_) | copy-start | bytes 786436
  85.3 18.4 %copy-start.11 = (bf16[2,256,256]{2,1,0:T(8,128)(2,1)S(1)}, bf16[2,256,256]{2,1,0:T(8,128)(2,1)}, u32[]{:S(2)}) copy-start(bf16[2,256,256]{2,1,0:T(8,128)(2,1)} %get-tuple-element.63.r_8_.r_7_) | copy-start | bytes 786436
  85.3 18.4 %copy-start.12 = (bf16[2,256,256]{2,1,0:T(8,128)(2,1)S(1)}, bf16[2,256,256]{2,1,0:T(8,128)(2,1)}, u32[]{:S(2)}) copy-start(bf16[2,256,256]{2,1,0:T(8,128)(2,1)} %get-tuple-element.64.r_9_.r_8_) | copy-start | bytes 786436
  85.3 18.4 %copy-start.13 = (f32[1,384]{1,0:T(1,128)S(1)}, f32[1,384]{1,0:T(1,128)}, u32[]{:S(2)}) copy-start(f32[1,384]{1,0:T(1,128)} %get-tuple-element.65.r_10_.r_9_) | copy-start | bytes 4612
  85.3 18.4 %copy-start.14 = (f32[1,384]{1,0:T(1,128)S(1)}, f32[1,384]{1,0:T(1,128)}, u32[]{:S(2)}) copy-start(f32[1,384]{1,0:T(1,128)} %get-tuple-element.66.r_11_.r_10_) | copy-start | bytes 4612
  85.4 18.4 %copy-start.17 = (f32[216,128]{1,0:T(8,128)S(1)}, f32[216,128]{1,0:T(8,128)}, u32[]{:S(2)}) copy-start(f32[216,128]{1,0:T(8,128)} %constant.17.clone.r_5_.r_11_) | copy-start | bytes 331780
  85.4 18.4 %copy-start.18 = (bf16[288,432]{1,0:T(8,128)(2,1)S(1)}, bf16[288,432]{1,0:T(8,128)(2,1)}, u32[]{:S(2)}) copy-start(bf16[288,432]{1,0:T(8,128)(2,1)} %get-tuple-element.79.r_3_) | copy-start | bytes 746500
  85.4 18.4 %copy-start.19 = (bf16[288,432]{1,0:T(8,128)(2,1)S(1)}, bf16[288,432]{1,0:T(8,128)(2,1)}, u32[]{:S(2)}) copy-start(bf16[288,432]{1,0:T(8,128)(2,1)} %get-tuple-element.80.r_4_) | copy-start | bytes 746500
  85.4 18.4 %copy-start.20 = (bf16[216,576]{1,0:T(8,128)(2,1)S(1)}, bf16[216,576]{1,0:T(8,128)(2,1)}, u32[]{:S(2)}) copy-start(bf16[216,576]{1,0:T(8,128)(2,1)} %get-tuple-element.77.r_1_) | copy-start | bytes 746500
  85.4 18.4 %copy-start.21 = (bf16[216,576]{1,0:T(8,128)(2,1)S(1)}, bf16[216,576]{1,0:T(8,128)(2,1)}, u32[]{:S(2)}) copy-start(bf16[216,576]{1,0:T(8,128)(2,1)} %get-tuple-element.78.r_2_) | copy-start | bytes 746500
  184.2 1.9 collective-permute-start.15
  184.3 6.0 %collective-permute-start.16 = (f32[216,128]{1,0:T(8,128)S(1)}, f32[216,128]{1,0:T(8,128)S(1)}, u32[]{:S(2)}, u32[]{:S(2)}) collective-permute-start(f32[216,128]{1,0:T(8,128)S(1)} %get-tuple-element.91), channel_id=1, source_target_pairs={{0,2},{1,3},{2,0},{3,1},{4,6},{5,7},{6,4},{7,5},{8,10},{9,11},{10,... | collective-permute-start | bytes 331784 | tf_op jit(solution)/shard_map/ppermute | solution.py:586
  185.1 6.5 %collective-permute-start.17 = (f32[216,128]{1,0:T(8,128)S(1)}, f32[216,128]{1,0:T(8,128)S(1)}, u32[]{:S(2)}, u32[]{:S(2)}) collective-permute-start(f32[216,128]{1,0:T(8,128)S(1)} %get-tuple-element.92), channel_id=1, source_target_pairs={{0,3},{1,2},{2,1},{3,0},{4,7},{5,6},{6,5},{7,4},{8,11},{9,10},{10,... | collective-permute-start | bytes 331784 | tf_op jit(solution)/shard_map/ppermute | solution.py:586
  (14 other events, 66.6 us)
